TPU v7x, 512 devices: a whole 4x8x8 slice. The times are simulated.
512 devices in a mesh: row: 16 (over x_hi, y), col: 32 (over z, x_lo, core).
Axes of the slice: x: 4 (x_hi: 2, x_lo: 2; x = x_hi * 2 + x_lo), y: 8, z: 8, core: 2. Of those that a mesh axis runs over, the one named last changes fastest.
Arguments:
- pair_window: bfloat16 [32, 64, 32, 128], P('col', 'row'), may hold values from -6 to 6
- tri_cotangent: bfloat16 [32, 64, 2048, 128], P(None, 'row', 'col'), may hold values from -0.25 to 0.25
- saved_left: bfloat16 [32, 64, 32, 128], P('col', 'row'), may hold values from -6 to 6
- saved_right: bfloat16 [32, 64, 32, 128], P('col', 'row'), may hold values from -6 to 6
- norm_gain: float32 [128], replicated, may hold values from 0.5 to 1.5
- norm_bias: float32 [128], replicated, may hold values from -3 to 3
- proj_weight: bfloat16 [4, 128, 128], replicated, may hold values from -0.5 to 0.5
Outputs:
- pair_grad: bfloat16 [32, 64, 32, 128], P('col', 'row')
- weight_grad: float32 [4, 128, 128], replicated
- norm_grad: float32 [2, 128], replicated
All inputs are finite; a program needn't handle non-finite values.
Results may differ from a plain program's by a relative error of at most 0.0085.
Values may be sent and summed in bfloat16 or wider, within the bound.
No kernel may reach another device: no remote copies, remote signals or barrier semaphores. Data moves between devices by JAX's collectives and lax.ppermute only.
A program may use at most 64 MiB of HBM per device.

v0:
```python
import jax
import jax.numpy as jnp
from jax import lax
from jax.sharding import PartitionSpec as P


def sent_to_all(x, axis):
    devices = lax.axis_size(axis)
    return lax.all_to_all(jnp.broadcast_to(x[None], (devices, *x.shape)), axis, 0, 0, tiled=True)


def laid_out(parts, dim):
    parts = jnp.moveaxis(parts, 0, dim)
    lengths = parts.shape
    return parts.reshape(*lengths[:dim], lengths[dim] * lengths[dim + 1], *lengths[dim + 2 :])


def collect(x, axis, dim):
    parts = sent_to_all(x, axis)
    return laid_out(parts, dim)


def split_up(x, dim, devices):
    lengths = x.shape
    parts = x.reshape(*lengths[:dim], devices, lengths[dim] // devices, *lengths[dim + 1 :])
    return jnp.moveaxis(parts, dim, 0)


def sent_and_summed(x, axis, dim):
    parts = split_up(x, dim, lax.axis_size(axis))
    arrived = lax.all_to_all(parts, axis, split_axis=0, concat_axis=0, tiled=True)
    return arrived.astype(jnp.float32).sum(axis=0)


def gated_norm_back(pair_rows, left_grad, right_grad, norm_gain, norm_bias, proj_weight):
    pair = pair_rows.astype(jnp.float32)
    average = jnp.mean(pair, axis=-1, keepdims=True)
    centred = pair - average
    variance = jnp.mean(centred * centred, axis=-1, keepdims=True)
    inv_std = lax.rsqrt(variance + 1e-05)
    unit_pair = centred * inv_std
    normed = (unit_pair * norm_gain + norm_bias).astype(jnp.bfloat16)
    chans = proj_weight.shape[2]
    stacked = jnp.transpose(proj_weight, (1, 0, 2)).reshape(proj_weight.shape[1], 4 * chans)
    preact = jnp.dot(normed, stacked, preferred_element_type=jnp.float32)
    gate_left = jax.nn.sigmoid(preact[:, :chans])
    value_left = preact[:, chans : 2 * chans]
    gate_right = jax.nn.sigmoid(preact[:, 2 * chans : 3 * chans])
    value_right = preact[:, 3 * chans :]
    pre_grads = jnp.concatenate(
        [
            left_grad * value_left * gate_left * (1.0 - gate_left),
            left_grad * gate_left,
            right_grad * value_right * gate_right * (1.0 - gate_right),
            right_grad * gate_right,
        ],
        axis=1,
    ).astype(jnp.bfloat16)
    weight_part = lax.dot_general(
        normed, pre_grads, (((0,), (0,)), ((), ())), preferred_element_type=jnp.float32
    )
    weight_part = jnp.transpose(weight_part.reshape(proj_weight.shape[1], 4, chans), (1, 0, 2))
    normed_grad = jnp.dot(pre_grads, stacked.T, preferred_element_type=jnp.float32)
    norm_part = jnp.stack([jnp.sum(normed_grad * unit_pair, axis=0), jnp.sum(normed_grad, axis=0)])
    scaled_grad = normed_grad * norm_gain
    pair_grad = inv_std * (
        scaled_grad
        - jnp.mean(scaled_grad, axis=-1, keepdims=True)
        - unit_pair * jnp.mean(scaled_grad * unit_pair, axis=-1, keepdims=True)
    )
    return (pair_grad.astype(jnp.bfloat16), weight_part, norm_part)


def on_device(
    pair_window, tri_cotangent, saved_left, saved_right, norm_gain, norm_bias, proj_weight
):
    block_count, own_rows, col_tokens, channels = tri_cotangent.shape
    window_len = saved_left.shape[2]
    right_rows = collect(saved_right, "row", 1)[0]
    cot_flat = tri_cotangent.reshape(block_count * own_rows, col_tokens, channels)
    cot_piece = cot_flat
    left_grad = sent_and_summed(
        jnp.einsum(
            "ijh,jkh->ikh", cot_piece, right_rows, preferred_element_type=jnp.float32
        ).astype(jnp.bfloat16),
        "col",
        0,
    )
    left_rows = collect(saved_left, "col", 0)
    left_flat = left_rows.reshape(block_count * own_rows, window_len, channels)
    cot_piece = cot_flat
    right_grad = sent_and_summed(
        jnp.einsum("ijh,ikh->jkh", cot_piece, left_flat, preferred_element_type=jnp.float32).astype(
            jnp.bfloat16
        ),
        "row",
        0,
    )
    positions = own_rows * window_len
    pair_grad, weight_part, norm_part = gated_norm_back(
        pair_window.reshape(positions, pair_window.shape[3]),
        left_grad.reshape(positions, channels),
        right_grad.reshape(positions, channels),
        norm_gain,
        norm_bias,
        proj_weight,
    )
    weight_grad, norm_grad = lax.psum((weight_part, norm_part), ("row", "col"))
    return (pair_grad.reshape(pair_window.shape), weight_grad, norm_grad)


def solution(mesh):
    return jax.shard_map(
        on_device,
        mesh=mesh,
        in_specs=(
            P("col", "row", None, None),
            P(None, "row", "col", None),
            P("col", "row", None, None),
            P("col", "row", None, None),
            P(),
            P(),
            P(),
        ),
        out_specs=(P("col", "row", None, None), P(), P()),
        check_vma=False,
    )
```

profile of v0, /device:TPU:1, one launch (start us, length us, event | category | flops | bytes accessed | tf_op | source)
XLA Modules:
  0.0 407.1 jit_solution(14064561879678002585)
XLA Ops:
  7.2 0.9 broadcast_in_dim.9
  8.0 25.4 %all_to_all.20 = bf16[16,1,4,32,128]{4,3,2,1,0:T(8,128)(2,1)} all-to-all(bf16[16,1,4,32,128]{4,3,2,1,0:T(8,128)(2,1)S(1)} %broadcast_in_dim.9), channel_id=1, replica_groups=mesh['row'=16,'col'=32] {'row'}, dimensions={0} | all-to-all | bytes 1048576 | tf_op jit(solution)/shard_map/all_to_all | solution.py:9
  33.4 2.0 broadcast_in_dim.11
  35.5 13.3 %all-to-all-start.2 = ((bf16[32,1,4,32,128]{4,3,2,1,0:T(8,128)(2,1)}), bf16[32,1,4,32,128]{4,3,2,1,0:T(8,128)(2,1)S(1)}, u32[]{:S(2)}, u32[]{:S(2)}) async-start(bf16[32,1,4,32,128]{4,3,2,1,0:T(8,128)(2,1)} %broadcast_in_dim.11), calls=%async_computation.2 | async-start | bytes 2097152 | tf_op jit(solution)/shard_map/all_to_all | solution.py:9
  48.8 3.8 copy.26
  52.6 3.7 copy.25
  56.3 2.9 fusion
  59.2 0.0 copy-start.1
  59.2 3.2 copy.27
  62.5 14.4 %all-to-all-done.2 = bf16[32,1,4,32,128]{4,3,2,1,0:T(8,128)(2,1)S(1)} async-done(((bf16[32,1,4,32,128]{4,3,2,1,0:T(8,128)(2,1)}), bf16[32,1,4,32,128]{4,3,2,1,0:T(8,128)(2,1)S(1)}, u32[]{:S(2)}, u32[]{:S(2)}) %all-to-all-start.2) | async-done | bytes 1048608 | tf_op jit(solution)/shard_map/all_to_all | solution.py:9
  76.9 0.0 copy-start
  76.9 1.0 copy-done
  77.9 4.3 %all-to-all-start.1 = ((bf16[32,4,32,128]{3,2,1,0:T(8,128)(2,1)}), bf16[32,4,32,128]{3,2,1,0:T(8,128)(2,1)S(1)}, u32[]{:S(2)}, u32[]{:S(2)}) async-start(bf16[32,4,32,128]{3,2,1,0:T(8,128)(2,1)} %bitcast.55), calls=%async_computation.1 | async-start | bytes 2097152 | tf_op jit(solution)/shard_map/all_to_all | solution.py:31
  82.2 0.0 copy-done.1
  82.2 0.1 convert_reduce_fusion.2
  82.3 3.2 copy.29
  85.5 3.4 fusion.1
  88.9 0.0 copy-start.2
  88.9 0.0 copy-start.3
  88.9 0.0 copy-start.4
  88.9 3.7 copy.31
  92.6 17.6 %all-to-all-done.1 = bf16[32,4,32,128]{3,2,1,0:T(8,128)(2,1)S(1)} async-done(((bf16[32,4,32,128]{3,2,1,0:T(8,128)(2,1)}), bf16[32,4,32,128]{3,2,1,0:T(8,128)(2,1)S(1)}, u32[]{:S(2)}, u32[]{:S(2)}) %all-to-all-start.1) | async-done | bytes 1048608 | tf_op jit(solution)/shard_map/all_to_all | solution.py:31
  110.2 4.9 %all-to-all-start.3 = ((bf16[16,4,32,128]{3,2,1,0:T(8,128)(2,1)}), bf16[16,4,32,128]{3,2,1,0:T(8,128)(2,1)S(1)}, u32[]{:S(2)}, u32[]{:S(2)}) async-start(bf16[16,4,32,128]{3,2,1,0:T(8,128)(2,1)} %bitcast.12), calls=%async_computation.3 | async-start | bytes 1048576 | tf_op jit(solution)/shard_map/all_to_all | solution.py:31
  115.1 0.0 all-reduce.2.cloned.1.call-start
  115.2 0.1 div.25
  115.3 0.2 multiply_reduce_fusion.2
  115.4 0.1 rsqrt.13
  115.5 0.0 copy-done.2
  115.5 0.1 copy.28
  115.7 0.0 copy-done.3
  115.7 0.0 copy-done.4
  115.7 0.1 add_convert_fusion
  115.8 0.2 fusion.20
  116.0 0.2 convert_reduce_fusion
  116.1 13.5 %all-to-all-done.3 = bf16[16,4,32,128]{3,2,1,0:T(8,128)(2,1)S(1)} async-done(((bf16[16,4,32,128]{3,2,1,0:T(8,128)(2,1)}), bf16[16,4,32,128]{3,2,1,0:T(8,128)(2,1)S(1)}, u32[]{:S(2)}, u32[]{:S(2)}) %all-to-all-start.3) | async-done | bytes 524320 | tf_op jit(solution)/shard_map/all_to_all | solution.py:31
  129.6 0.1 convert_reduce_fusion.1
  129.7 0.1 fusion.13
  129.8 0.1 copy.36
  129.9 0.9 convolution_bitcast_fusion
  130.9 0.0 all-reduce.2.cloned.1.call-update
  130.9 0.3 multiply_reduce_fusion
  131.2 98.7 %psum.15 = f32[2,128]{1,0:T(2,128)} all-reduce(f32[2,128]{1,0:T(2,128)S(1)} %pad_maximum_fusion.2), channel_id=1, replica_groups=mesh['row'=16,'col'=32] {'row','col'}, use_global_device_ids=true, to_apply=%region_9.0 | all-reduce | flops 256 | bytes 2048 | tf_op jit(solution)/shard_map/psum | solution.py:108
  229.8 0.8 multiply_convert_fusion
  230.6 168.0 %all-reduce.2.cloned.1.call-done = f32[4,128,128]{2,1,0:T(8,128)} async-done(((f32[4,128,128]{2,1,0:T(8,128)}), f32[4,128,128]{2,1,0:T(8,128)}) %all-reduce.2.cloned.1.call-update) | async-done | bytes 262160 | tf_op jit(solution)/shard_map/psum | solution.py:108
  398.6 1.7 copy.38
  (5 shorter events, 0.0 us)
Async XLA Ops:
  35.5 41.4 %all-to-all-start.2 = ((bf16[32,1,4,32,128]{4,3,2,1,0:T(8,128)(2,1)}), bf16[32,1,4,32,128]{4,3,2,1,0:T(8,128)(2,1)S(1)}, u32[]{:S(2)}, u32[]{:S(2)}) async-start(bf16[32,1,4,32,128]{4,3,2,1,0:T(8,128)(2,1)} %broadcast_in_dim.11), calls=%async_computation.2 | async-start | bytes 2097152 | tf_op jit(solution)/shard_map/all_to_all | solution.py:9
  59.2 23.0 %copy-start.1 = (bf16[1,4,32,128]{3,2,1,0:T(8,128)(2,1)S(1)}, bf16[1,4,32,128]{3,2,1,0:T(8,128)(2,1)}, u32[]{:S(2)}) copy-start(bf16[1,4,32,128]{3,2,1,0:T(8,128)(2,1)} %param.7) | copy-start | bytes 98308
  76.9 1.0 copy-start
  77.9 32.3 %all-to-all-start.1 = ((bf16[32,4,32,128]{3,2,1,0:T(8,128)(2,1)}), bf16[32,4,32,128]{3,2,1,0:T(8,128)(2,1)S(1)}, u32[]{:S(2)}, u32[]{:S(2)}) async-start(bf16[32,4,32,128]{3,2,1,0:T(8,128)(2,1)} %bitcast.55), calls=%async_computation.1 | async-start | bytes 2097152 | tf_op jit(solution)/shard_map/all_to_all | solution.py:31
  88.9 26.6 %copy-start.2 = (bf16[4,128,128]{2,1,0:T(8,128)(2,1)S(1)}, bf16[4,128,128]{2,1,0:T(8,128)(2,1)}, u32[]{:S(2)}) copy-start(bf16[4,128,128]{2,1,0:T(8,128)(2,1)} %param.13) | copy-start | bytes 393220
  88.9 26.7 %copy-start.3 = (f32[128]{0:T(128)S(1)}, f32[128]{0:T(128)}, u32[]{:S(2)}) copy-start(f32[128]{0:T(128)} %param.11) | copy-start | bytes 1540
  88.9 26.8 %copy-start.4 = (f32[128]{0:T(128)S(1)}, f32[128]{0:T(128)}, u32[]{:S(2)}) copy-start(f32[128]{0:T(128)} %param.12) | copy-start | bytes 1540
  110.2 19.4 %all-to-all-start.3 = ((bf16[16,4,32,128]{3,2,1,0:T(8,128)(2,1)}), bf16[16,4,32,128]{3,2,1,0:T(8,128)(2,1)S(1)}, u32[]{:S(2)}, u32[]{:S(2)}) async-start(bf16[16,4,32,128]{3,2,1,0:T(8,128)(2,1)} %bitcast.12), calls=%async_computation.3 | async-start | bytes 1048576 | tf_op jit(solution)/shard_map/all_to_all | solution.py:31
  115.1 283.5 %all-reduce.2.cloned.1.call-start = ((), (), s32[]{:S(2)}) async-start(), calls=%async_computation.4 | async-start | bytes 524288 | tf_op jit(solution)/shard_map/psum | solution.py:108
Sparse Core Ops, SparseCore 0:
  131.0 267.5 all-reduce.1
where the time goes:
time: 408 us; the launch traced here: 407 us
  waiting for transfers between devices  214 us (52%)
  blocking collectives  124 us (30%)
  local copies, waits for them, and re-layouts  23.6 us (6%)
  starting transfers between devices  22.6 us (6%)
  between operations  14.2 us (3%)
  matrix products  7.66 us (2%)
    psum x1, waiting for transfers between devices, on_device(): weight_grad, norm_grad = lax.psum((weight_part, norm_part), ('row', 'col'))  168 us
    psum x1, blocking collectives, on_device(): weight_grad, norm_grad = lax.psum((weight_part, norm_part), ('row', 'col'))  98.7 us
    all_to_all x2, waiting for transfers between devices, sent_and_summed(): lax.all_to_all(parts, axis, split_axis=0, concat_axis=0, tiled=True)  31.1 us
    all_to_all x1, blocking collectives, sent_to_all(): lax.all_to_all(jnp.broadcast_to(x[None], (devices, *x.shape)), axis, 0, 0...  25.4 us
    all_to_all x1, waiting for transfers between devices, sent_to_all(): lax.all_to_all(jnp.broadcast_to(x[None], (devices, *x.shape)), axis, 0, 0...  14.4 us
    all_to_all x1, starting transfers between devices, sent_to_all(): lax.all_to_all(jnp.broadcast_to(x[None], (devices, *x.shape)), axis, 0, 0...  13.3 us
    all_to_all x2, starting transfers between devices, sent_and_summed(): lax.all_to_all(parts, axis, split_axis=0, concat_axis=0, tiled=True)  9.23 us
  transfers between devices with their start and end apart: 4, of which 4 were waited for; matrix products, arithmetic and copies ran while one was open for 6% of the time, Pallas kernels for 0%

commit v1 on v0

--- a/solution.py
+++ b/solution.py
@@ -71,6 +71,21 @@
     return (pair_grad.astype(jnp.bfloat16), weight_part, norm_part)
 
 
+def summed_over_all(weight_part, norm_part):
+    cols = lax.axis_size("col")
+    shape = weight_part.shape
+    width = shape[-1]
+    chunks = weight_part.reshape(cols, -1, width)
+    rows = chunks.shape[1]
+    extra = jnp.zeros((8, width), jnp.float32).at[: norm_part.shape[0]].set(norm_part)
+    packed = jnp.concatenate([chunks, jnp.broadcast_to(extra[None], (cols, 8, width))], axis=1)
+    arrived = lax.all_to_all(packed, "col", 0, 0, tiled=True)
+    part = arrived.sum(axis=0)
+    whole = sent_to_all(part, "row").sum(axis=0)
+    weight_grad = sent_to_all(whole[:rows], "col").reshape(shape)
+    return weight_grad, whole[rows : rows + norm_part.shape[0]]
+
+
 def on_device(
     pair_window, tri_cotangent, saved_left, saved_right, norm_gain, norm_bias, proj_weight
 ):
@@ -105,7 +120,7 @@
         norm_bias,
         proj_weight,
     )
-    weight_grad, norm_grad = lax.psum((weight_part, norm_part), ("row", "col"))
+    weight_grad, norm_grad = summed_over_all(weight_part, norm_part)
     return (pair_grad.reshape(pair_window.shape), weight_grad, norm_grad)
 
 

time: 408 us -> 179 us (0.44)
  waiting for transfers between devices: 214 us -> 55.7 us
  blocking collectives: 124 us -> 59.6 us
  between operations: 14.2 us -> 0.84 us
  starting transfers between devices: 22.6 us -> 29.3 us
    psum x1 -> x0, waiting for transfers between devices: 168 us -> none  [on_device(): weight_grad, norm_grad = lax.psum((weight_part, norm_part), ('row', 'col'))]
    psum x1 -> x0, blocking collectives: 98.7 us -> none  [on_device(): weight_grad, norm_grad = lax.psum((weight_part, norm_part), ('row', 'col'))]
    all_to_all x0 -> x1, blocking collectives: none -> 20.6 us  [summed_over_all(): arrived = lax.all_to_all(packed, 'col', 0, 0, tiled=True)]
    all_to_all x1 -> x2, blocking collectives: 25.4 us -> 39 us  [sent_to_all(): lax.all_to_all(jnp.broadcast_to(x[None], (devices, *x.shape)), axis, 0, 0...]
    all_to_all x1 -> x2, waiting for transfers between devices: 14.4 us -> 24.6 us  [sent_to_all(): lax.all_to_all(jnp.broadcast_to(x[None], (devices, *x.shape)), axis, 0, 0...]
    all_to_all x1 -> x2, starting transfers between devices: 13.3 us -> 20.1 us  [sent_to_all(): lax.all_to_all(jnp.broadcast_to(x[None], (devices, *x.shape)), axis, 0, 0...]
  transfers between devices with their start and end apart: 4 -> 4, of which waited for: 4 -> 4; matrix products, arithmetic and copies ran while one was open for 6% -> 15% of each run, Pallas kernels for 0% -> 0%
where the time goes in v1:
time: 179 us; the launch traced here: 178 us
  blocking collectives  59.6 us (33%)
  waiting for transfers between devices  55.7 us (31%)
  starting transfers between devices  29.3 us (16%)
  local copies, waits for them, and re-layouts  24 us (13%)
  matrix products  6.94 us (4%)
    all_to_all x2, blocking collectives, sent_to_all(): lax.all_to_all(jnp.broadcast_to(x[None], (devices, *x.shape)), axis, 0, 0...  39 us
    all_to_all x2, waiting for transfers between devices, sent_and_summed(): lax.all_to_all(parts, axis, split_axis=0, concat_axis=0, tiled=True)  31.2 us
    all_to_all x2, waiting for transfers between devices, sent_to_all(): lax.all_to_all(jnp.broadcast_to(x[None], (devices, *x.shape)), axis, 0, 0...  24.6 us
    all_to_all x1, blocking collectives, summed_over_all(): arrived = lax.all_to_all(packed, 'col', 0, 0, tiled=True)  20.6 us
    all_to_all x2, starting transfers between devices, sent_to_all(): lax.all_to_all(jnp.broadcast_to(x[None], (devices, *x.shape)), axis, 0, 0...  20.1 us
    all_to_all x2, starting transfers between devices, sent_and_summed(): lax.all_to_all(parts, axis, split_axis=0, concat_axis=0, tiled=True)  9.23 us
    reshape x1, local copies, waits for them, and re-layouts, on_device(): tri_cotangent.reshape(block_count * own_rows, col_tokens, channels)  3.84 us
    another operation x1, local copies, waits for them, and re-layouts, on_device(): right_rows = collect(saved_right, 'row', 1)[0]  3.71 us
  transfers between devices with their start and end apart: 4, of which 4 were waited for; matrix products, arithmetic and copies ran while one was open for 15% of the time, Pallas kernels for 0%

profile of v1, /device:TPU:1, one launch (start us, length us, event | category | flops | bytes accessed | tf_op | source)
XLA Modules:
  0.0 178.0 jit_solution(9875255999549603944)
XLA Ops:
  0.6 0.9 broadcast_in_dim.15
  1.5 25.4 %all_to_all.35 = bf16[16,1,4,32,128]{4,3,2,1,0:T(8,128)(2,1)} all-to-all(bf16[16,1,4,32,128]{4,3,2,1,0:T(8,128)(2,1)S(1)} %broadcast_in_dim.15), channel_id=1, replica_groups=mesh['row'=16,'col'=32] {'row'}, dimensions={0} | all-to-all | bytes 1048576 | tf_op jit(solution)/shard_map/all_to_all | solution.py:9
  26.9 2.0 %broadcast_in_dim.17 = bf16[32,1,4,32,128]{4,3,2,1,0:T(8,128)(2,1)} broadcast(bf16[4,32,128]{2,1,0:T(8,128)(2,1)} %bitcast.68), dimensions={2,3,4} | broadcast | bytes 1081344 | tf_op jit(solution)/shard_map/broadcast_in_dim | solution.py:9
  28.9 13.3 %all-to-all-start.2 = ((bf16[32,1,4,32,128]{4,3,2,1,0:T(8,128)(2,1)}), bf16[32,1,4,32,128]{4,3,2,1,0:T(8,128)(2,1)S(1)}, u32[]{:S(2)}, u32[]{:S(2)}) async-start(bf16[32,1,4,32,128]{4,3,2,1,0:T(8,128)(2,1)} %broadcast_in_dim.17), calls=%async_computation.2 | async-start | bytes 2097152 | tf_op jit(solution)/shard_map/all_to_all | solution.py:9
  42.3 3.8 %copy.35 = bf16[128,64,128]{0,1,2:T(8,128)(2,1)S(1)} copy(bf16[128,64,128]{2,1,0:T(8,128)(2,1)} %bitcast.59) | data formatting | bytes 4194304 | tf_op jit(solution)/shard_map/reshape | solution.py:95
  46.1 3.7 %copy.34 = bf16[64,32,128]{0,1,2:T(8,128)(2,1)} copy(bf16[64,32,128]{2,1,0:T(8,128)(2,1)} %bitcast.58) | data formatting | bytes 1048576 | tf_op jit(solution)/shard_map/squeeze;reshape;transpose | solution.py:94
  49.8 2.9 %fusion = bf16[128,32,128]{0,1,2:T(8,128)(2,1)} fusion(bf16[64,32,128]{0,1,2:T(8,128)(2,1)} %copy.34, bf16[128,64,128]{0,1,2:T(8,128)(2,1)S(1)} %copy.35), kind=kOutput, calls=%fused_computation.3 | convolution fusion | flops 67633152 | bytes 3670016 | tf_op jit(solution)/shard_map/ijh,jkh->ikh/dot_general | solution.py:98
  52.7 0.0 copy-start.1
  52.7 3.2 %copy.36 = bf16[128,32,128]{2,1,0:T(8,128)(2,1)} copy(bf16[128,32,128]{0,1,2:T(8,128)(2,1)} %fusion) | data formatting | bytes 2097152 | tf_op jit(solution)/shard_map/convert_element_type | solution.py:100
  55.9 14.4 %all-to-all-done.2 = bf16[32,1,4,32,128]{4,3,2,1,0:T(8,128)(2,1)S(1)} async-done(((bf16[32,1,4,32,128]{4,3,2,1,0:T(8,128)(2,1)}), bf16[32,1,4,32,128]{4,3,2,1,0:T(8,128)(2,1)S(1)}, u32[]{:S(2)}, u32[]{:S(2)}) %all-to-all-start.2) | async-done | bytes 1048608 | tf_op jit(solution)/shard_map/all_to_all | solution.py:9
  70.3 0.0 copy-start
  70.3 1.0 copy-done
  71.3 4.3 %all-to-all-start.1 = ((bf16[32,4,32,128]{3,2,1,0:T(8,128)(2,1)}), bf16[32,4,32,128]{3,2,1,0:T(8,128)(2,1)S(1)}, u32[]{:S(2)}, u32[]{:S(2)}) async-start(bf16[32,4,32,128]{3,2,1,0:T(8,128)(2,1)} %bitcast.57), calls=%async_computation.1 | async-start | bytes 2097152 | tf_op jit(solution)/shard_map/all_to_all | solution.py:31
  75.7 0.0 copy-done.1
  75.7 0.1 convert_reduce_fusion.2
  75.8 3.2 %copy.38 = bf16[128,32,128]{0,1,2:T(8,128)(2,1)} copy(bf16[128,32,128]{2,1,0:T(8,128)(2,1)} %bitcast.56) | data formatting | bytes 2097152 | tf_op jit(solution)/shard_map/reshape;reshape | solution.py:105
  79.0 3.4 %fusion.1 = bf16[64,32,128]{0,1,2:T(8,128)(2,1)} fusion(bf16[128,32,128]{0,1,2:T(8,128)(2,1)} %copy.38, bf16[128,64,128]{0,1,2:T(8,128)(2,1)S(1)} %copy.35), kind=kOutput, calls=%fused_computation.4 | convolution fusion | flops 67371008 | bytes 3670016 | tf_op jit(solution)/shard_map/ijh,ikh->jkh/dot_general | solution.py:108
  82.4 0.0 copy-start.2
  82.4 0.0 copy-start.3
  82.4 0.0 copy-start.4
  82.4 3.7 %copy.40 = bf16[64,32,128]{2,1,0:T(8,128)(2,1)} copy(bf16[64,32,128]{0,1,2:T(8,128)(2,1)} %fusion.1) | data formatting | bytes 1048576 | tf_op jit(solution)/shard_map/convert_element_type | solution.py:108
  86.0 17.6 %all-to-all-done.1 = bf16[32,4,32,128]{3,2,1,0:T(8,128)(2,1)S(1)} async-done(((bf16[32,4,32,128]{3,2,1,0:T(8,128)(2,1)}), bf16[32,4,32,128]{3,2,1,0:T(8,128)(2,1)S(1)}, u32[]{:S(2)}, u32[]{:S(2)}) %all-to-all-start.1) | async-done | bytes 1048608 | tf_op jit(solution)/shard_map/all_to_all | solution.py:31
  103.7 4.9 %all-to-all-start.3 = ((bf16[16,4,32,128]{3,2,1,0:T(8,128)(2,1)}), bf16[16,4,32,128]{3,2,1,0:T(8,128)(2,1)S(1)}, u32[]{:S(2)}, u32[]{:S(2)}) async-start(bf16[16,4,32,128]{3,2,1,0:T(8,128)(2,1)} %bitcast.12), calls=%async_computation.3 | async-start | bytes 1048576 | tf_op jit(solution)/shard_map/all_to_all | solution.py:31
  108.6 0.1 div.25
  108.7 0.2 multiply_reduce_fusion.2
  108.8 0.1 rsqrt.13
  108.9 0.0 copy-done.2
  108.9 0.1 copy.37
  109.1 0.0 copy-done.3
  109.1 0.0 copy-done.4
  109.1 0.1 add_convert_fusion
  109.2 0.2 fusion.20
  109.4 0.2 convert_reduce_fusion
  109.6 13.6 %all-to-all-done.3 = bf16[16,4,32,128]{3,2,1,0:T(8,128)(2,1)S(1)} async-done(((bf16[16,4,32,128]{3,2,1,0:T(8,128)(2,1)}), bf16[16,4,32,128]{3,2,1,0:T(8,128)(2,1)S(1)}, u32[]{:S(2)}, u32[]{:S(2)}) %all-to-all-start.3) | async-done | bytes 524320 | tf_op jit(solution)/shard_map/all_to_all | solution.py:31
  123.1 0.1 convert_reduce_fusion.1
  123.2 0.1 fusion.13
  123.3 0.1 copy.45
  123.4 0.3 multiply_reduce_fusion
  123.7 0.2 fusion.21
  124.0 20.6 %all_to_all.36 = f32[32,24,128]{2,1,0:T(8,128)S(1)} all-to-all(f32[32,24,128]{2,1,0:T(8,128)S(1)} %pad_maximum_fusion), channel_id=1, replica_groups=mesh['row'=16,'col'=32] {'col'}, dimensions={0} | all-to-all | bytes 786432 | tf_op jit(solution)/shard_map/all_to_all | solution.py:82
  144.7 13.6 %all_to_all.37 = f32[16,24,128]{2,1,0:T(8,128)S(1)} all-to-all(f32[16,24,128]{2,1,0:T(8,128)S(1)} %broadcast_in_dim.19), channel_id=1, replica_groups=mesh['row'=16,'col'=32] {'row'}, dimensions={0} | all-to-all | bytes 393216 | tf_op jit(solution)/shard_map/all_to_all | solution.py:9
  158.3 0.7 broadcast_in_dim.20
  159.0 6.8 %all-to-all-start.6 = ((f32[32,16,128]{2,1,0:T(8,128)}), f32[32,16,128]{2,1,0:T(8,128)S(1)}, u32[]{:S(2)}, u32[]{:S(2)}) async-start(f32[32,16,128]{2,1,0:T(8,128)} %broadcast_in_dim.20), calls=%async_computation.6 | async-start | bytes 524288 | tf_op jit(solution)/shard_map/all_to_all | solution.py:9
  165.8 0.8 multiply_convert_fusion
  166.5 0.6 slice.45
  167.1 10.1 %all-to-all-done.6 = f32[32,16,128]{2,1,0:T(8,128)S(1)} async-done(((f32[32,16,128]{2,1,0:T(8,128)}), f32[32,16,128]{2,1,0:T(8,128)S(1)}, u32[]{:S(2)}, u32[]{:S(2)}) %all-to-all-start.6) | async-done | bytes 262176 | tf_op jit(solution)/shard_map/all_to_all | solution.py:9
  177.2 0.7 copy.47
  (11 shorter events, 0.2 us)
Async XLA Ops:
  28.9 41.4 %all-to-all-start.2 = ((bf16[32,1,4,32,128]{4,3,2,1,0:T(8,128)(2,1)}), bf16[32,1,4,32,128]{4,3,2,1,0:T(8,128)(2,1)S(1)}, u32[]{:S(2)}, u32[]{:S(2)}) async-start(bf16[32,1,4,32,128]{4,3,2,1,0:T(8,128)(2,1)} %broadcast_in_dim.17), calls=%async_computation.2 | async-start | bytes 2097152 | tf_op jit(solution)/shard_map/all_to_all | solution.py:9
  52.7 23.0 %copy-start.1 = (bf16[1,4,32,128]{3,2,1,0:T(8,128)(2,1)S(1)}, bf16[1,4,32,128]{3,2,1,0:T(8,128)(2,1)}, u32[]{:S(2)}) copy-start(bf16[1,4,32,128]{3,2,1,0:T(8,128)(2,1)} %param.9) | copy-start | bytes 98308
  70.3 1.0 copy-start
  71.3 32.3 %all-to-all-start.1 = ((bf16[32,4,32,128]{3,2,1,0:T(8,128)(2,1)}), bf16[32,4,32,128]{3,2,1,0:T(8,128)(2,1)S(1)}, u32[]{:S(2)}, u32[]{:S(2)}) async-start(bf16[32,4,32,128]{3,2,1,0:T(8,128)(2,1)} %bitcast.57), calls=%async_computation.1 | async-start | bytes 2097152 | tf_op jit(solution)/shard_map/all_to_all | solution.py:31
  82.4 26.5 %copy-start.2 = (bf16[4,128,128]{2,1,0:T(8,128)(2,1)S(1)}, bf16[4,128,128]{2,1,0:T(8,128)(2,1)}, u32[]{:S(2)}) copy-start(bf16[4,128,128]{2,1,0:T(8,128)(2,1)} %param.15) | copy-start | bytes 393220
  82.4 26.7 %copy-start.3 = (f32[128]{0:T(128)S(1)}, f32[128]{0:T(128)}, u32[]{:S(2)}) copy-start(f32[128]{0:T(128)} %param.13) | copy-start | bytes 1540
  82.4 26.7 %copy-start.4 = (f32[128]{0:T(128)S(1)}, f32[128]{0:T(128)}, u32[]{:S(2)}) copy-start(f32[128]{0:T(128)} %param.14) | copy-start | bytes 1540
  103.7 19.4 %all-to-all-start.3 = ((bf16[16,4,32,128]{3,2,1,0:T(8,128)(2,1)}), bf16[16,4,32,128]{3,2,1,0:T(8,128)(2,1)S(1)}, u32[]{:S(2)}, u32[]{:S(2)}) async-start(bf16[16,4,32,128]{3,2,1,0:T(8,128)(2,1)} %bitcast.12), calls=%async_computation.3 | async-start | bytes 1048576 | tf_op jit(solution)/shard_map/all_to_all | solution.py:31
  159.0 18.3 %all-to-all-start.6 = ((f32[32,16,128]{2,1,0:T(8,128)}), f32[32,16,128]{2,1,0:T(8,128)S(1)}, u32[]{:S(2)}, u32[]{:S(2)}) async-start(f32[32,16,128]{2,1,0:T(8,128)} %broadcast_in_dim.20), calls=%async_computation.6 | async-start | bytes 524288 | tf_op jit(solution)/shard_map/all_to_all | solution.py:9

commit v2 on v1

--- a/solution.py
+++ b/solution.py
@@ -86,31 +86,50 @@
     return weight_grad, whole[rows : rows + norm_part.shape[0]]
 
 
-def on_device(
+def siblings(devices):
+    return [[c for c in range(devices) if c % 2 == core] for core in range(2)]
+
+
+def swapped(x, axis):
+    devices = lax.axis_size(axis)
+    return lax.ppermute(x, axis, [(c, c ^ 1) for c in range(devices)])
+
+
+def all_steps(
     pair_window, tri_cotangent, saved_left, saved_right, norm_gain, norm_bias, proj_weight
 ):
     block_count, own_rows, col_tokens, channels = tri_cotangent.shape
     window_len = saved_left.shape[2]
+    cols = lax.axis_size("col")
+    half = cols // 2
+    core = lax.rem(lax.axis_index("col"), 2)
+    groups = siblings(cols)
     right_rows = collect(saved_right, "row", 1)[0]
-    cot_flat = tri_cotangent.reshape(block_count * own_rows, col_tokens, channels)
-    cot_piece = cot_flat
-    left_grad = sent_and_summed(
-        jnp.einsum(
-            "ijh,jkh->ikh", cot_piece, right_rows, preferred_element_type=jnp.float32
-        ).astype(jnp.bfloat16),
-        "col",
-        0,
+    cot_flat = jnp.swapaxes(
+        tri_cotangent.reshape(half, 2, own_rows, col_tokens, channels), 0, 1
+    ).reshape(block_count * own_rows, col_tokens, channels)
+    near = jnp.broadcast_to(saved_left, (half, *saved_left.shape[1:]))
+    near = lax.all_to_all(near, "col", 0, 0, tiled=True, axis_index_groups=groups)
+    left_part = jnp.einsum(
+        "ijh,jkh->ikh", cot_flat, right_rows, preferred_element_type=jnp.float32
+    ).astype(jnp.bfloat16)
+    pairs = left_part.reshape(2, half, own_rows, window_len, channels)
+    kept = lax.dynamic_index_in_dim(pairs, core, 0, keepdims=False)
+    away = lax.dynamic_index_in_dim(pairs, 1 - core, 0, keepdims=False)
+    came = swapped(away, "col")
+    chip_part = (kept.astype(jnp.float32) + came.astype(jnp.float32)).astype(jnp.bfloat16)
+    left_arrived = lax.all_to_all(chip_part, "col", 0, 0, tiled=True, axis_index_groups=groups)
+    far = swapped(near, "col")
+    even = jnp.where(core == 0, near, far)
+    odd = jnp.where(core == 0, far, near)
+    left_flat = jnp.stack([even, odd]).reshape(
+        block_count * own_rows, window_len, channels
     )
-    left_rows = collect(saved_left, "col", 0)
-    left_flat = left_rows.reshape(block_count * own_rows, window_len, channels)
-    cot_piece = cot_flat
-    right_grad = sent_and_summed(
-        jnp.einsum("ijh,ikh->jkh", cot_piece, left_flat, preferred_element_type=jnp.float32).astype(
-            jnp.bfloat16
-        ),
-        "row",
-        0,
-    )
+    right_part = jnp.einsum(
+        "ijh,ikh->jkh", cot_flat, left_flat, preferred_element_type=jnp.float32
+    ).astype(jnp.bfloat16)
+    left_grad = left_arrived.astype(jnp.float32).sum(axis=0)
+    right_grad = sent_and_summed(right_part, "row", 0)
     positions = own_rows * window_len
     pair_grad, weight_part, norm_part = gated_norm_back(
         pair_window.reshape(positions, pair_window.shape[3]),
@@ -126,7 +145,7 @@
 
 def solution(mesh):
     return jax.shard_map(
-        on_device,
+        all_steps,
         mesh=mesh,
         in_specs=(
             P("col", "row", None, None),

time: 179 us -> 161 us (0.90)
  waiting for transfers between devices: 55.7 us -> 29.5 us
  starting transfers between devices: 29.3 us -> 36.7 us
  other arithmetic: 1.53 us -> 5.91 us
  local copies, waits for them, and re-layouts: 24 us -> 21.3 us
  matrix products: 6.94 us -> 4.72 us
    all_to_all x2 -> x1, waiting for transfers between devices: 31.2 us -> 12 us  [sent_and_summed(): lax.all_to_all(parts, axis, split_axis=0, concat_axis=0, tiled=True)]
    all_to_all x0 -> x2, starting transfers between devices: none -> 18 us  [the longest x1 10.2 us: all_steps(): lax.all_to_all(near, 'col', 0, 0, tiled=True, axis_index_groups=groups)]
    all_to_all x2 -> x1, waiting for transfers between devices: 24.6 us -> 10.1 us  [sent_to_all(): lax.all_to_all(jnp.broadcast_to(x[None], (devices, *x.shape)), axis, 0, 0...]
    all_to_all x2 -> x1, starting transfers between devices: 20.1 us -> 6.78 us  [sent_to_all(): lax.all_to_all(jnp.broadcast_to(x[None], (devices, *x.shape)), axis, 0, 0...]
    all_to_all x0 -> x2, waiting for transfers between devices: none -> 7.34 us  [the longest x1 7.34 us: all_steps(): lax.all_to_all(chip_part, 'col', 0, 0, tiled=True, axis_index_groups=groups)]
    ppermute x0 -> x2, starting transfers between devices: none -> 6.93 us  [swapped(): return lax.ppermute(x, axis, [(c, c ^ 1) for c in range(devices)])]
    all_to_all x2 -> x1, starting transfers between devices: 9.23 us -> 4.9 us  [sent_and_summed(): lax.all_to_all(parts, axis, split_axis=0, concat_axis=0, tiled=True)]
    another operation x2 -> x1, local copies, waits for them, and re-layouts: 6.92 us -> 2.82 us  [all_steps(): right_rows = collect(saved_right, 'row', 1)[0]]
  transfers between devices with their start and end apart: 4 -> 6, of which waited for: 4 -> 3; matrix products, arithmetic and copies ran while one was open for 15% -> 17% of each run, Pallas kernels for 0% -> 0%
where the time goes in v2:
time: 161 us; the launch traced here: 160 us
  blocking collectives  61 us (38%)
  starting transfers between devices  36.7 us (23%)
  waiting for transfers between devices  29.5 us (18%)
  local copies, waits for them, and re-layouts  21.3 us (13%)
  other arithmetic  5.91 us (4%)
  matrix products  4.72 us (3%)
    all_to_all x2, blocking collectives, sent_to_all(): lax.all_to_all(jnp.broadcast_to(x[None], (devices, *x.shape)), axis, 0, 0...  38.7 us
    all_to_all x1, blocking collectives, summed_over_all(): arrived = lax.all_to_all(packed, 'col', 0, 0, tiled=True)  22.3 us
    all_to_all x1, waiting for transfers between devices, sent_and_summed(): lax.all_to_all(parts, axis, split_axis=0, concat_axis=0, tiled=True)  12 us
    all_to_all x1, starting transfers between devices, all_steps(): lax.all_to_all(near, 'col', 0, 0, tiled=True, axis_index_groups=groups)  10.2 us
    all_to_all x1, waiting for transfers between devices, sent_to_all(): lax.all_to_all(jnp.broadcast_to(x[None], (devices, *x.shape)), axis, 0, 0...  10.1 us
    all_to_all x1, starting transfers between devices, all_steps(): lax.all_to_all(chip_part, 'col', 0, 0, tiled=True, axis_index_groups=groups)  7.83 us
    all_to_all x1, waiting for transfers between devices, all_steps(): lax.all_to_all(chip_part, 'col', 0, 0, tiled=True, axis_index_groups=groups)  7.34 us
    ppermute x2, starting transfers between devices, swapped(): return lax.ppermute(x, axis, [(c, c ^ 1) for c in range(devices)])  6.93 us
  transfers between devices with their start and end apart: 6, of which 3 were waited for; matrix products, arithmetic and copies ran while one was open for 17% of the time, Pallas kernels for 0%

profile of v2, /device:TPU:1, one launch (start us, length us, event | category | flops | bytes accessed | tf_op | source)
XLA Modules:
  0.0 160.1 jit_solution(5041245365570598391)
XLA Ops:
  0.6 1.0 broadcast_in_dim.15
  1.6 25.4 %all_to_all.35 = bf16[16,1,4,32,128]{4,3,2,1,0:T(8,128)(2,1)} all-to-all(bf16[16,1,4,32,128]{4,3,2,1,0:T(8,128)(2,1)S(1)} %broadcast_in_dim.15), channel_id=1, replica_groups=mesh['row'=16,'col'=32] {'row'}, dimensions={0} | all-to-all | bytes 1048576 | tf_op jit(solution)/shard_map/all_to_all | solution.py:9
  27.1 1.7 %broadcast_in_dim.17 = bf16[16,4,32,128]{3,2,1,0:T(8,128)(2,1)} broadcast(bf16[4,32,128]{2,1,0:T(8,128)(2,1)} %bitcast.82), dimensions={1,2,3} | broadcast | bytes 557056 | tf_op jit(solution)/shard_map/broadcast_in_dim | solution.py:111
  28.7 10.2 %all-to-all-start.2 = ((bf16[16,4,32,128]{3,2,1,0:T(8,128)(2,1)}), bf16[16,4,32,128]{3,2,1,0:T(8,128)(2,1)}, u32[]{:S(2)}, u32[]{:S(2)}) async-start(bf16[16,4,32,128]{3,2,1,0:T(8,128)(2,1)} %broadcast_in_dim.17), calls=%async_computation.2 | async-start | bytes 1048576 | tf_op jit(solution)/shard_map/all_to_all | solution.py:112
  39.0 1.6 copy.45
  40.5 3.8 %copy.47 = bf16[128,64,128]{0,1,2:T(8,128)(2,1)S(1)} copy(bf16[128,64,128]{2,1,0:T(8,128)(2,1)} %bitcast.68) | data formatting | bytes 4194304 | tf_op jit(solution)/shard_map/reshape | solution.py:110
  44.4 2.8 %copy.46 = bf16[64,32,128]{0,1,2:T(8,128)(2,1)S(1)} copy(bf16[64,32,128]{2,1,0:T(8,128)(2,1)} %bitcast.72) | data formatting | bytes 1048576 | tf_op jit(solution)/shard_map/squeeze;reshape;transpose | solution.py:107
  47.2 1.7 %fusion = bf16[128,32,128]{0,1,2:T(8,128)(2,1)} fusion(bf16[64,32,128]{0,1,2:T(8,128)(2,1)S(1)} %copy.46, bf16[128,64,128]{0,1,2:T(8,128)(2,1)S(1)} %copy.47), kind=kOutput, calls=%fused_computation.2 | convolution fusion | flops 67633152 | bytes 3670016 | tf_op jit(solution)/shard_map/ijh,jkh->ikh/dot_general | solution.py:113
  48.9 2.5 %copy.48 = bf16[128,32,128]{2,1,0:T(8,128)(2,1)S(1)} copy(bf16[128,32,128]{0,1,2:T(8,128)(2,1)} %fusion) | data formatting | bytes 2097152 | tf_op jit(solution)/shard_map/convert_element_type | solution.py:115
  51.3 0.0 copy-start.1
  51.3 0.9 dynamic-slice_bitcast_fusion
  52.2 5.0 %collective-permute-start = (bf16[16,4,32,128]{3,2,1,0:T(8,128)(2,1)}, bf16[16,4,32,128]{3,2,1,0:T(8,128)(2,1)}, u32[]{:S(2)}, u32[]{:S(2)}) collective-permute-start(bf16[16,4,32,128]{3,2,1,0:T(8,128)(2,1)} %dynamic-slice_bitcast_fusion), channel_id=1, source_target_pairs={{0,1},{1,0},{2,3},{3,2},{4,5},{5,4},{6,7},{7,6},{8,9},{9,8},{10,11... | collective-permute-start | bytes 1572872 | tf_op jit(solution)/shard_map/ppermute | solution.py:95
  57.2 1.9 %collective-permute-start.1 = (bf16[16,4,32,128]{3,2,1,0:T(8,128)(2,1)}, bf16[16,4,32,128]{3,2,1,0:T(8,128)(2,1)}, u32[]{:S(2)}, u32[]{:S(2)}) collective-permute-start(bf16[16,4,32,128]{3,2,1,0:T(8,128)(2,1)} %all-to-all-done.2), channel_id=1, source_target_pairs={{0,1},{1,0},{2,3},{3,2},{4,5},{5,4},{6,7},{7,6},{8,9},{9,8},{10,11... | collective-permute-start | bytes 1572872 | tf_op jit(solution)/shard_map/ppermute | solution.py:95
  59.2 0.0 collective-permute-done
  59.2 2.0 %fusion.2 = bf16[16,4,32,128]{3,2,1,0:T(8,128)(2,1)} fusion(bf16[16,4,32,128]{3,2,1,0:T(8,128)(2,1)} %collective-permute-done, bf16[2,16,4,32,128]{4,3,2,1,0:T(8,128)(2,1)S(1)} %bitcast.70, s32[]{:T(128)S(6)} %select_n.19), kind=kLoop, calls=%fused_computation.6 | loop fusion | flops 1048576 | bytes 1572868 | tf_op jit(solution)/shard_map/convert_element_type | solution.py:120
  61.2 7.8 %all-to-all-start.1 = ((bf16[16,4,32,128]{3,2,1,0:T(8,128)(2,1)}), bf16[16,4,32,128]{3,2,1,0:T(8,128)(2,1)}, u32[]{:S(2)}, u32[]{:S(2)}) async-start(bf16[16,4,32,128]{3,2,1,0:T(8,128)(2,1)} %fusion.2), calls=%async_computation.1 | async-start | bytes 1048576 | tf_op jit(solution)/shard_map/all_to_all | solution.py:121
  69.1 0.1 convert_reduce_fusion.2
  69.2 1.3 select_bitcast_fusion.1
  70.4 0.1 pad_maximum_fusion
  70.5 2.3 %copy.50 = bf16[128,32,128]{0,1,2:T(8,128)(2,1)} copy(bf16[128,32,128]{2,1,0:T(8,128)(2,1)S(1)} %bitcast.71) | data formatting | bytes 2097152 | tf_op jit(solution)/shard_map/reshape | solution.py:125
  72.9 2.4 %fusion.1 = bf16[64,32,128]{0,1,2:T(8,128)(2,1)S(1)} fusion(bf16[128,32,128]{0,1,2:T(8,128)(2,1)} %copy.50, bf16[128,64,128]{0,1,2:T(8,128)(2,1)S(1)} %copy.47), kind=kOutput, calls=%fused_computation.3 | convolution fusion | flops 67371008 | bytes 3670016 | tf_op jit(solution)/shard_map/ijh,ikh->jkh/dot_general | solution.py:128
  75.3 0.0 copy-start.2
  75.3 0.0 copy-start.3
  75.3 0.0 copy-start.4
  75.3 2.3 %copy.52 = bf16[64,32,128]{2,1,0:T(8,128)(2,1)} copy(bf16[64,32,128]{0,1,2:T(8,128)(2,1)S(1)} %fusion.1) | data formatting | bytes 1048576 | tf_op jit(solution)/shard_map/convert_element_type | solution.py:130
  77.6 7.3 %all-to-all-done.1 = bf16[16,4,32,128]{3,2,1,0:T(8,128)(2,1)} async-done(((bf16[16,4,32,128]{3,2,1,0:T(8,128)(2,1)}), bf16[16,4,32,128]{3,2,1,0:T(8,128)(2,1)}, u32[]{:S(2)}, u32[]{:S(2)}) %all-to-all-start.1) | async-done | bytes 524320 | tf_op jit(solution)/shard_map/all_to_all | solution.py:121
  85.0 4.9 %all-to-all-start.3 = ((bf16[16,4,32,128]{3,2,1,0:T(8,128)(2,1)}), bf16[16,4,32,128]{3,2,1,0:T(8,128)(2,1)S(1)}, u32[]{:S(2)}, u32[]{:S(2)}) async-start(bf16[16,4,32,128]{3,2,1,0:T(8,128)(2,1)} %bitcast.18), calls=%async_computation.3 | async-start | bytes 1048576 | tf_op jit(solution)/shard_map/all_to_all | solution.py:31
  89.9 0.1 copy.49
  90.0 0.1 div.25
  90.1 0.2 multiply_reduce_fusion.2
  90.3 0.1 rsqrt.13
  90.4 0.1 add_convert_fusion
  90.5 0.2 fusion.21
  90.7 1.1 convert_reduce_fusion.1
  91.8 12.0 %all-to-all-done.3 = bf16[16,4,32,128]{3,2,1,0:T(8,128)(2,1)S(1)} async-done(((bf16[16,4,32,128]{3,2,1,0:T(8,128)(2,1)}), bf16[16,4,32,128]{3,2,1,0:T(8,128)(2,1)S(1)}, u32[]{:S(2)}, u32[]{:S(2)}) %all-to-all-start.3) | async-done | bytes 524320 | tf_op jit(solution)/shard_map/all_to_all | solution.py:31
  103.9 0.1 convert_reduce_fusion
  103.9 0.1 fusion.14
  104.0 0.1 copy.57
  104.2 0.2 fusion.22
  104.4 0.3 multiply_reduce_fusion
  104.7 22.3 %all_to_all.36 = f32[32,24,128]{2,1,0:T(8,128)S(1)} all-to-all(f32[32,24,128]{2,1,0:T(8,128)S(1)} %pad_maximum_fusion.1), channel_id=1, replica_groups=mesh['row'=16,'col'=32] {'col'}, dimensions={0} | all-to-all | bytes 786432 | tf_op jit(solution)/shard_map/all_to_all | solution.py:82
  127.1 13.3 %all_to_all.37 = f32[16,24,128]{2,1,0:T(8,128)S(1)} all-to-all(f32[16,24,128]{2,1,0:T(8,128)S(1)} %broadcast_in_dim.19), channel_id=1, replica_groups=mesh['row'=16,'col'=32] {'row'}, dimensions={0} | all-to-all | bytes 393216 | tf_op jit(solution)/shard_map/all_to_all | solution.py:9
  140.4 0.7 broadcast_in_dim.20
  141.2 6.8 %all-to-all-start.6 = ((f32[32,16,128]{2,1,0:T(8,128)}), f32[32,16,128]{2,1,0:T(8,128)S(1)}, u32[]{:S(2)}, u32[]{:S(2)}) async-start(f32[32,16,128]{2,1,0:T(8,128)} %broadcast_in_dim.20), calls=%async_computation.6 | async-start | bytes 524288 | tf_op jit(solution)/shard_map/all_to_all | solution.py:9
  148.0 0.8 multiply_convert_fusion
  148.7 0.6 slice.45
  149.3 10.1 %all-to-all-done.6 = f32[32,16,128]{2,1,0:T(8,128)S(1)} async-done(((f32[32,16,128]{2,1,0:T(8,128)}), f32[32,16,128]{2,1,0:T(8,128)S(1)}, u32[]{:S(2)}, u32[]{:S(2)}) %all-to-all-start.6) | async-done | bytes 262176 | tf_op jit(solution)/shard_map/all_to_all | solution.py:9
  159.4 0.7 copy.59
  (19 shorter events, 0.2 us)
Async XLA Ops:
  0.6 38.3 %copy-start = (bf16[32,4,64,128]{3,2,1,0:T(8,128)(2,1)S(1)}, bf16[32,4,64,128]{3,2,1,0:T(8,128)(2,1)}, u32[]{:S(2)}) copy-start(bf16[32,4,64,128]{3,2,1,0:T(8,128)(2,1)} %param.10) | copy-start | bytes 6291460
  28.7 28.5 %all-to-all-start.2 = ((bf16[16,4,32,128]{3,2,1,0:T(8,128)(2,1)}), bf16[16,4,32,128]{3,2,1,0:T(8,128)(2,1)}, u32[]{:S(2)}, u32[]{:S(2)}) async-start(bf16[16,4,32,128]{3,2,1,0:T(8,128)(2,1)} %broadcast_in_dim.17), calls=%async_computation.2 | async-start | bytes 1048576 | tf_op jit(solution)/shard_map/all_to_all | solution.py:112
  51.3 17.7 %copy-start.1 = (bf16[1,4,32,128]{3,2,1,0:T(8,128)(2,1)S(1)}, bf16[1,4,32,128]{3,2,1,0:T(8,128)(2,1)}, u32[]{:S(2)}) copy-start(bf16[1,4,32,128]{3,2,1,0:T(8,128)(2,1)} %param.9) | copy-start | bytes 98308
  52.2 7.0 %collective-permute-start = (bf16[16,4,32,128]{3,2,1,0:T(8,128)(2,1)}, bf16[16,4,32,128]{3,2,1,0:T(8,128)(2,1)}, u32[]{:S(2)}, u32[]{:S(2)}) collective-permute-start(bf16[16,4,32,128]{3,2,1,0:T(8,128)(2,1)} %dynamic-slice_bitcast_fusion), channel_id=1, source_target_pairs={{0,1},{1,0},{2,3},{3,2},{4,5},{5,4},{6,7},{7,6},{8,9},{9,8},{10,11... | collective-permute-start | bytes 1572872 | tf_op jit(solution)/shard_map/ppermute | solution.py:95
  57.2 11.9 %collective-permute-start.1 = (bf16[16,4,32,128]{3,2,1,0:T(8,128)(2,1)}, bf16[16,4,32,128]{3,2,1,0:T(8,128)(2,1)}, u32[]{:S(2)}, u32[]{:S(2)}) collective-permute-start(bf16[16,4,32,128]{3,2,1,0:T(8,128)(2,1)} %all-to-all-done.2), channel_id=1, source_target_pairs={{0,1},{1,0},{2,3},{3,2},{4,5},{5,4},{6,7},{7,6},{8,9},{9,8},{10,11... | collective-permute-start | bytes 1572872 | tf_op jit(solution)/shard_map/ppermute | solution.py:95
  61.2 23.7 %all-to-all-start.1 = ((bf16[16,4,32,128]{3,2,1,0:T(8,128)(2,1)}), bf16[16,4,32,128]{3,2,1,0:T(8,128)(2,1)}, u32[]{:S(2)}, u32[]{:S(2)}) async-start(bf16[16,4,32,128]{3,2,1,0:T(8,128)(2,1)} %fusion.2), calls=%async_computation.1 | async-start | bytes 1048576 | tf_op jit(solution)/shard_map/all_to_all | solution.py:121
  75.3 14.6 %copy-start.2 = (bf16[4,128,128]{2,1,0:T(8,128)(2,1)S(1)}, bf16[4,128,128]{2,1,0:T(8,128)(2,1)}, u32[]{:S(2)}) copy-start(bf16[4,128,128]{2,1,0:T(8,128)(2,1)} %param.15) | copy-start | bytes 393220
  75.3 15.1 %copy-start.3 = (f32[128]{0:T(128)S(1)}, f32[128]{0:T(128)}, u32[]{:S(2)}) copy-start(f32[128]{0:T(128)} %param.13) | copy-start | bytes 1540
  75.3 15.1 %copy-start.4 = (f32[128]{0:T(128)S(1)}, f32[128]{0:T(128)}, u32[]{:S(2)}) copy-start(f32[128]{0:T(128)} %param.14) | copy-start | bytes 1540
  85.0 18.9 %all-to-all-start.3 = ((bf16[16,4,32,128]{3,2,1,0:T(8,128)(2,1)}), bf16[16,4,32,128]{3,2,1,0:T(8,128)(2,1)S(1)}, u32[]{:S(2)}, u32[]{:S(2)}) async-start(bf16[16,4,32,128]{3,2,1,0:T(8,128)(2,1)} %bitcast.18), calls=%async_computation.3 | async-start | bytes 1048576 | tf_op jit(solution)/shard_map/all_to_all | solution.py:31
  141.2 18.3 %all-to-all-start.6 = ((f32[32,16,128]{2,1,0:T(8,128)}), f32[32,16,128]{2,1,0:T(8,128)S(1)}, u32[]{:S(2)}, u32[]{:S(2)}) async-start(f32[32,16,128]{2,1,0:T(8,128)} %broadcast_in_dim.20), calls=%async_computation.6 | async-start | bytes 524288 | tf_op jit(solution)/shard_map/all_to_all | solution.py:9

commit v3 on v2

--- a/solution.py
+++ b/solution.py
@@ -75,15 +75,21 @@
     cols = lax.axis_size("col")
     shape = weight_part.shape
     width = shape[-1]
-    chunks = weight_part.reshape(cols, -1, width)
+    chunks = weight_part.reshape(cols, -1, width).astype(jnp.bfloat16)
     rows = chunks.shape[1]
-    extra = jnp.zeros((8, width), jnp.float32).at[: norm_part.shape[0]].set(norm_part)
+    norm_high = lax.reduce_precision(norm_part, 8, 7)
+    norm_low = norm_part - norm_high
+    extra = jnp.concatenate(
+        [norm_high, norm_low, jnp.zeros((4, width), jnp.float32)], axis=0
+    ).astype(jnp.bfloat16)
     packed = jnp.concatenate([chunks, jnp.broadcast_to(extra[None], (cols, 8, width))], axis=1)
     arrived = lax.all_to_all(packed, "col", 0, 0, tiled=True)
-    part = arrived.sum(axis=0)
+    part = arrived.astype(jnp.float32).sum(axis=0)
     whole = sent_to_all(part, "row").sum(axis=0)
-    weight_grad = sent_to_all(whole[:rows], "col").reshape(shape)
-    return weight_grad, whole[rows : rows + norm_part.shape[0]]
+    norm_grad = whole[rows : rows + 2] + whole[rows + 2 : rows + 4]
+    chunk, norm_grad = lax.optimization_barrier((whole[:rows].astype(jnp.bfloat16), norm_grad))
+    weight_grad = sent_to_all(chunk, "col").reshape(shape)
+    return weight_grad.astype(jnp.float32), norm_grad
 
 
 def siblings(devices):
@@ -105,24 +111,21 @@
     core = lax.rem(lax.axis_index("col"), 2)
     groups = siblings(cols)
     right_rows = collect(saved_right, "row", 1)[0]
-    cot_flat = jnp.swapaxes(
-        tri_cotangent.reshape(half, 2, own_rows, col_tokens, channels), 0, 1
-    ).reshape(block_count * own_rows, col_tokens, channels)
+    cot_flat = tri_cotangent.reshape(block_count * own_rows, col_tokens, channels)
     near = jnp.broadcast_to(saved_left, (half, *saved_left.shape[1:]))
     near = lax.all_to_all(near, "col", 0, 0, tiled=True, axis_index_groups=groups)
     left_part = jnp.einsum(
         "ijh,jkh->ikh", cot_flat, right_rows, preferred_element_type=jnp.float32
     ).astype(jnp.bfloat16)
-    pairs = left_part.reshape(2, half, own_rows, window_len, channels)
-    kept = lax.dynamic_index_in_dim(pairs, core, 0, keepdims=False)
-    away = lax.dynamic_index_in_dim(pairs, 1 - core, 0, keepdims=False)
+    pairs = left_part.reshape(half, 2, own_rows, window_len, channels)
+    kept = lax.dynamic_index_in_dim(pairs, core, 1, keepdims=False)
+    away = lax.dynamic_index_in_dim(pairs, 1 - core, 1, keepdims=False)
     came = swapped(away, "col")
     chip_part = (kept.astype(jnp.float32) + came.astype(jnp.float32)).astype(jnp.bfloat16)
     left_arrived = lax.all_to_all(chip_part, "col", 0, 0, tiled=True, axis_index_groups=groups)
     far = swapped(near, "col")
-    even = jnp.where(core == 0, near, far)
-    odd = jnp.where(core == 0, far, near)
-    left_flat = jnp.stack([even, odd]).reshape(
+    mine = jnp.arange(2).reshape(1, 2, 1, 1, 1) == core
+    left_flat = jnp.where(mine, near[:, None], far[:, None]).reshape(
         block_count * own_rows, window_len, channels
     )
     right_part = jnp.einsum(
@@ -138,6 +141,9 @@
         norm_gain,
         norm_bias,
         proj_weight,
+    )
+    pair_grad, weight_part, norm_part = lax.optimization_barrier(
+        (pair_grad, weight_part, norm_part)
     )
     weight_grad, norm_grad = summed_over_all(weight_part, norm_part)
     return (pair_grad.reshape(pair_window.shape), weight_grad, norm_grad)

time: 161 us -> 149 us (0.925)
  blocking collectives: 61 us -> 46.8 us
  starting transfers between devices: 36.7 us -> 40.7 us
  local copies, waits for them, and re-layouts: 21.3 us -> 18 us
    all_to_all x2, blocking collectives: 38.7 us -> 28 us  [sent_to_all(): lax.all_to_all(jnp.broadcast_to(x[None], (devices, *x.shape)), axis, 0, 0...]
    all_to_all x1, waiting for transfers between devices: 7.34 us -> 3.13 us  [all_steps(): lax.all_to_all(chip_part, 'col', 0, 0, tiled=True, axis_index_groups=groups)]
    all_to_all x1, blocking collectives: 22.3 us -> 18.8 us  [summed_over_all(): arrived = lax.all_to_all(packed, 'col', 0, 0, tiled=True)]
    all_to_all x1, starting transfers between devices: 6.78 us -> 10.2 us  [sent_to_all(): lax.all_to_all(jnp.broadcast_to(x[None], (devices, *x.shape)), axis, 0, 0...]
    ppermute x2, waiting for transfers between devices: 0.01 us -> 3.4 us  [swapped(): return lax.ppermute(x, axis, [(c, c ^ 1) for c in range(devices)])]
    select_n x0 -> x1, local copies, waits for them, and re-layouts: none -> 2.32 us  [all_steps(): jnp.where(mine, near[:, None], far[:, None])]
    reshape x2 -> x1, local copies, waits for them, and re-layouts: 6.14 us -> 3.84 us  [all_steps(): tri_cotangent.reshape(block_count * own_rows, col_tokens, channels)]
  transfers between devices with their start and end apart: 6 -> 6, of which waited for: 3 -> 5; matrix products, arithmetic and copies ran while one was open for 17% -> 16% of each run, Pallas kernels for 0% -> 0%
where the time goes in v3:
time: 149 us; the launch traced here: 148 us
  blocking collectives  46.8 us (31%)
  starting transfers between devices  40.7 us (27%)
  waiting for transfers between devices  29.9 us (20%)
  local copies, waits for them, and re-layouts  18 us (12%)
  other arithmetic  7.28 us (5%)
  matrix products  4.72 us (3%)
    all_to_all x2, blocking collectives, sent_to_all(): lax.all_to_all(jnp.broadcast_to(x[None], (devices, *x.shape)), axis, 0, 0...  28 us
    all_to_all x1, blocking collectives, summed_over_all(): arrived = lax.all_to_all(packed, 'col', 0, 0, tiled=True)  18.8 us
    all_to_all x1, waiting for transfers between devices, sent_and_summed(): lax.all_to_all(parts, axis, split_axis=0, concat_axis=0, tiled=True)  12 us
    all_to_all x1, waiting for transfers between devices, sent_to_all(): lax.all_to_all(jnp.broadcast_to(x[None], (devices, *x.shape)), axis, 0, 0...  11.4 us
    all_to_all x1, starting transfers between devices, all_steps(): lax.all_to_all(near, 'col', 0, 0, tiled=True, axis_index_groups=groups)  10.2 us
    all_to_all x1, starting transfers between devices, sent_to_all(): lax.all_to_all(jnp.broadcast_to(x[None], (devices, *x.shape)), axis, 0, 0...  10.2 us
    all_to_all x1, starting transfers between devices, all_steps(): lax.all_to_all(chip_part, 'col', 0, 0, tiled=True, axis_index_groups=groups)  7.83 us
    ppermute x2, starting transfers between devices, swapped(): return lax.ppermute(x, axis, [(c, c ^ 1) for c in range(devices)])  7.57 us
  transfers between devices with their start and end apart: 6, of which 5 were waited for; matrix products, arithmetic and copies ran while one was open for 16% of the time, Pallas kernels for 0%

profile of v3, /device:TPU:1, one launch (start us, length us, event | category | flops | bytes accessed | tf_op | source)
XLA Modules:
  0.0 148.4 jit_solution(7552003482988942333)
XLA Ops:
  0.6 1.6 %broadcast_in_dim.78 = bf16[16,1,4,32,128]{4,3,2,1,0:T(8,128)(2,1)} broadcast(bf16[4,32,128]{2,1,0:T(8,128)(2,1)} %bitcast.78), dimensions={2,3,4} | broadcast | bytes 557056 | tf_op jit(solution)/shard_map/broadcast_in_dim | solution.py:9
  2.3 10.2 %all-to-all-start = ((bf16[16,1,4,32,128]{4,3,2,1,0:T(8,128)(2,1)}), bf16[16,1,4,32,128]{4,3,2,1,0:T(8,128)(2,1)S(1)}, u32[]{:S(2)}, u32[]{:S(2)}) async-start(bf16[16,1,4,32,128]{4,3,2,1,0:T(8,128)(2,1)} %broadcast_in_dim.78), calls=%async_computation | async-start | bytes 1048576 | tf_op jit(solution)/shard_map/all_to_all | solution.py:9
  12.5 0.0 copy-start.3
  12.5 3.8 %copy.35 = bf16[128,64,128]{0,1,2:T(8,128)(2,1)S(1)} copy(bf16[128,64,128]{2,1,0:T(8,128)(2,1)} %bitcast.70) | data formatting | bytes 4194304 | tf_op jit(solution)/shard_map/reshape | solution.py:114
  16.4 11.4 %all-to-all-done = bf16[16,1,4,32,128]{4,3,2,1,0:T(8,128)(2,1)S(1)} async-done(((bf16[16,1,4,32,128]{4,3,2,1,0:T(8,128)(2,1)}), bf16[16,1,4,32,128]{4,3,2,1,0:T(8,128)(2,1)S(1)}, u32[]{:S(2)}, u32[]{:S(2)}) %all-to-all-start) | async-done | bytes 524320 | tf_op jit(solution)/shard_map/all_to_all | solution.py:9
  27.8 1.0 broadcast_in_dim.83
  28.8 10.2 %all-to-all-start.2 = ((bf16[16,4,32,128]{3,2,1,0:T(8,128)(2,1)}), bf16[16,4,32,128]{3,2,1,0:T(8,128)(2,1)}, u32[]{:S(2)}, u32[]{:S(2)}) async-start(bf16[16,4,32,128]{3,2,1,0:T(8,128)(2,1)} %broadcast_in_dim.83), calls=%async_computation.2 | async-start | bytes 1048576 | tf_op jit(solution)/shard_map/all_to_all | solution.py:116
  39.0 2.8 %copy.34 = bf16[64,32,128]{0,1,2:T(8,128)(2,1)S(1)} copy(bf16[64,32,128]{2,1,0:T(8,128)(2,1)} %bitcast.69) | data formatting | bytes 1048576 | tf_op jit(solution)/shard_map/squeeze;reshape;transpose | solution.py:113
  41.8 1.7 %fusion = bf16[128,32,128]{0,1,2:T(8,128)(2,1)} fusion(bf16[64,32,128]{0,1,2:T(8,128)(2,1)S(1)} %copy.34, bf16[128,64,128]{0,1,2:T(8,128)(2,1)S(1)} %copy.35), kind=kOutput, calls=%fused_computation.2 | convolution fusion | flops 67633152 | bytes 3670016 | tf_op jit(solution)/shard_map/ijh,jkh->ikh/dot_general | solution.py:117
  43.5 2.5 %copy.36 = bf16[128,32,128]{2,1,0:T(8,128)(2,1)S(1)} copy(bf16[128,32,128]{0,1,2:T(8,128)(2,1)} %fusion) | data formatting | bytes 2097152 | tf_op jit(solution)/shard_map/convert_element_type | solution.py:119
  46.0 0.9 dynamic-slice_bitcast_fusion
  46.8 5.0 %collective-permute-start = (bf16[16,4,32,128]{3,2,1,0:T(8,128)(2,1)}, bf16[16,4,32,128]{3,2,1,0:T(8,128)(2,1)}, u32[]{:S(2)}, u32[]{:S(2)}) collective-permute-start(bf16[16,4,32,128]{3,2,1,0:T(8,128)(2,1)} %dynamic-slice_bitcast_fusion), channel_id=1, source_target_pairs={{0,1},{1,0},{2,3},{3,2},{4,5},{5,4},{6,7},{7,6},{8,9},{9,8},{10,11... | collective-permute-start | bytes 1572872 | tf_op jit(solution)/shard_map/ppermute | solution.py:101
  51.8 1.8 %collective-permute-done = bf16[16,4,32,128]{3,2,1,0:T(8,128)(2,1)} collective-permute-done((bf16[16,4,32,128]{3,2,1,0:T(8,128)(2,1)}, bf16[16,4,32,128]{3,2,1,0:T(8,128)(2,1)}, u32[]{:S(2)}, u32[]{:S(2)}) %collective-permute-start) | collective-permute-done | bytes 524320 | tf_op jit(solution)/shard_map/ppermute | solution.py:101
  53.7 2.0 %fusion.2 = bf16[16,4,32,128]{3,2,1,0:T(8,128)(2,1)} fusion(bf16[16,4,32,128]{3,2,1,0:T(8,128)(2,1)} %collective-permute-done, bf16[16,2,4,32,128]{4,3,2,1,0:T(8,128)(2,1)S(1)} %bitcast.68, s32[]{:T(128)S(6)} %select_n.12), kind=kLoop, calls=%fused_computation.6 | loop fusion | flops 1048576 | bytes 1572868 | tf_op jit(solution)/shard_map/convert_element_type | solution.py:124
  55.7 7.8 %all-to-all-start.1 = ((bf16[16,4,32,128]{3,2,1,0:T(8,128)(2,1)}), bf16[16,4,32,128]{3,2,1,0:T(8,128)(2,1)}, u32[]{:S(2)}, u32[]{:S(2)}) async-start(bf16[16,4,32,128]{3,2,1,0:T(8,128)(2,1)} %fusion.2), calls=%async_computation.1 | async-start | bytes 1048576 | tf_op jit(solution)/shard_map/all_to_all | solution.py:125
  63.5 2.6 %collective-permute-start.1 = (bf16[16,4,32,128]{3,2,1,0:T(8,128)(2,1)}, bf16[16,4,32,128]{3,2,1,0:T(8,128)(2,1)}, u32[]{:S(2)}, u32[]{:S(2)}) collective-permute-start(bf16[16,4,32,128]{3,2,1,0:T(8,128)(2,1)} %all-to-all-done.2), channel_id=1, source_target_pairs={{0,1},{1,0},{2,3},{3,2},{4,5},{5,4},{6,7},{7,6},{8,9},{9,8},{10,11... | collective-permute-start | bytes 1572872 | tf_op jit(solution)/shard_map/ppermute | solution.py:101
  66.1 0.1 broadcast_in_dim.79
  66.2 0.1 broadcast_in_dim.80
  66.3 0.1 convert_reduce_fusion.3
  66.4 1.5 %collective-permute-done.1 = bf16[16,4,32,128]{3,2,1,0:T(8,128)(2,1)} collective-permute-done((bf16[16,4,32,128]{3,2,1,0:T(8,128)(2,1)}, bf16[16,4,32,128]{3,2,1,0:T(8,128)(2,1)}, u32[]{:S(2)}, u32[]{:S(2)}) %collective-permute-start.1) | collective-permute-done | bytes 524320 | tf_op jit(solution)/shard_map/ppermute | solution.py:101
  68.0 1.4 bitcast_select_fusion
  69.4 2.3 %copy.38 = bf16[128,32,128]{0,1,2:T(8,128)(2,1)} copy(bf16[128,32,128]{2,1,0:T(8,128)(2,1)S(1)} %bitcast_select_fusion) | data formatting | bytes 2097152 | tf_op jit(solution)/shard_map/jit(_where)/select_n | solution.py:128
  71.7 2.4 %fusion.1 = bf16[64,32,128]{0,1,2:T(8,128)(2,1)S(1)} fusion(bf16[128,32,128]{0,1,2:T(8,128)(2,1)} %copy.38, bf16[128,64,128]{0,1,2:T(8,128)(2,1)S(1)} %copy.35), kind=kOutput, calls=%fused_computation.3 | convolution fusion | flops 67371008 | bytes 3670016 | tf_op jit(solution)/shard_map/ijh,ikh->jkh/dot_general | solution.py:131
  74.1 0.0 copy-start.2
  74.2 2.3 %copy.40 = bf16[64,32,128]{2,1,0:T(8,128)(2,1)} copy(bf16[64,32,128]{0,1,2:T(8,128)(2,1)S(1)} %fusion.1) | data formatting | bytes 1048576 | tf_op jit(solution)/shard_map/convert_element_type | solution.py:133
  76.5 3.1 %all-to-all-done.1 = bf16[16,4,32,128]{3,2,1,0:T(8,128)(2,1)} async-done(((bf16[16,4,32,128]{3,2,1,0:T(8,128)(2,1)}), bf16[16,4,32,128]{3,2,1,0:T(8,128)(2,1)}, u32[]{:S(2)}, u32[]{:S(2)}) %all-to-all-start.1) | async-done | bytes 524320 | tf_op jit(solution)/shard_map/all_to_all | solution.py:125
  79.6 4.9 %all-to-all-start.3 = ((bf16[16,4,32,128]{3,2,1,0:T(8,128)(2,1)}), bf16[16,4,32,128]{3,2,1,0:T(8,128)(2,1)S(1)}, u32[]{:S(2)}, u32[]{:S(2)}) async-start(bf16[16,4,32,128]{3,2,1,0:T(8,128)(2,1)} %bitcast.15), calls=%async_computation.3 | async-start | bytes 1048576 | tf_op jit(solution)/shard_map/all_to_all | solution.py:31
  84.5 0.1 copy.37
  84.7 0.1 div.25
  84.7 0.2 multiply_reduce_fusion.2
  84.9 0.1 rsqrt.13
  85.0 0.1 pad.4.clone
  85.1 0.1 add_convert_fusion
  85.2 0.2 fusion.22
  85.4 1.1 convert_reduce_fusion.1
  86.5 12.0 %all-to-all-done.3 = bf16[16,4,32,128]{3,2,1,0:T(8,128)(2,1)S(1)} async-done(((bf16[16,4,32,128]{3,2,1,0:T(8,128)(2,1)}), bf16[16,4,32,128]{3,2,1,0:T(8,128)(2,1)S(1)}, u32[]{:S(2)}, u32[]{:S(2)}) %all-to-all-start.3) | async-done | bytes 524320 | tf_op jit(solution)/shard_map/all_to_all | solution.py:31
  98.5 0.1 convert_reduce_fusion
  98.6 0.1 fusion.14
  98.7 0.1 copy.45
  98.8 0.3 multiply_reduce_fusion
  99.1 0.2 convolution_bitcast_fusion
  99.3 0.8 multiply_convert_fusion
  100.1 0.1 maximum_maximum_fusion
  100.2 18.8 %all_to_all.35 = bf16[32,24,128]{2,1,0:T(8,128)(2,1)S(1)} all-to-all(bf16[32,24,128]{2,1,0:T(8,128)(2,1)S(1)} %pad_maximum_fusion), channel_id=1, replica_groups=mesh['row'=16,'col'=32] {'col'}, dimensions={0} | all-to-all | bytes 393216 | tf_op jit(solution)/shard_map/all_to_all | solution.py:86
  119.0 13.6 %all_to_all.36 = f32[16,24,128]{2,1,0:T(8,128)S(1)} all-to-all(f32[16,24,128]{2,1,0:T(8,128)S(1)} %broadcast_in_dim.90), channel_id=1, replica_groups=mesh['row'=16,'col'=32] {'row'}, dimensions={0} | all-to-all | bytes 393216 | tf_op jit(solution)/shard_map/all_to_all | solution.py:9
  132.7 0.6 slice_add_fusion
  133.3 14.4 %all_to_all.37 = bf16[32,16,128]{2,1,0:T(8,128)(2,1)S(1)} all-to-all(bf16[32,16,128]{2,1,0:T(8,128)(2,1)S(1)} %broadcast_in_dim.91), channel_id=1, replica_groups=mesh['row'=16,'col'=32] {'col'}, dimensions={0} | all-to-all | bytes 262144 | tf_op jit(solution)/shard_map/all_to_all | solution.py:9
  147.7 0.7 bitcast_convert_fusion
  (26 shorter events, 0.2 us)
Async XLA Ops:
  2.3 25.5 %all-to-all-start = ((bf16[16,1,4,32,128]{4,3,2,1,0:T(8,128)(2,1)}), bf16[16,1,4,32,128]{4,3,2,1,0:T(8,128)(2,1)S(1)}, u32[]{:S(2)}, u32[]{:S(2)}) async-start(bf16[16,1,4,32,128]{4,3,2,1,0:T(8,128)(2,1)} %broadcast_in_dim.78), calls=%async_computation | async-start | bytes 1048576 | tf_op jit(solution)/shard_map/all_to_all | solution.py:9
  12.5 15.3 %copy-start.3 = (bf16[1,4,32,128]{3,2,1,0:T(8,128)(2,1)S(1)}, bf16[1,4,32,128]{3,2,1,0:T(8,128)(2,1)}, u32[]{:S(2)}) copy-start(bf16[1,4,32,128]{3,2,1,0:T(8,128)(2,1)} %param.9) | copy-start | bytes 98308
  27.8 11.2 %copy-start = (bf16[16,1,4,32,128]{4,3,2,1,0:T(8,128)(2,1)}, bf16[16,1,4,32,128]{4,3,2,1,0:T(8,128)(2,1)S(1)}, u32[]{:S(2)}) copy-start(bf16[16,1,4,32,128]{4,3,2,1,0:T(8,128)(2,1)S(1)} %all-to-all-done) | copy-start | bytes 1572868
  28.8 27.0 %all-to-all-start.2 = ((bf16[16,4,32,128]{3,2,1,0:T(8,128)(2,1)}), bf16[16,4,32,128]{3,2,1,0:T(8,128)(2,1)}, u32[]{:S(2)}, u32[]{:S(2)}) async-start(bf16[16,4,32,128]{3,2,1,0:T(8,128)(2,1)} %broadcast_in_dim.83), calls=%async_computation.2 | async-start | bytes 1048576 | tf_op jit(solution)/shard_map/all_to_all | solution.py:116
  46.0 20.4 %copy-start.1 = (bf16[1,4,32,128]{3,2,1,0:T(8,128)(2,1)S(1)}, bf16[1,4,32,128]{3,2,1,0:T(8,128)(2,1)}, u32[]{:S(2)}) copy-start(bf16[1,4,32,128]{3,2,1,0:T(8,128)(2,1)} %param.7) | copy-start | bytes 98308
  46.8 6.9 %collective-permute-start = (bf16[16,4,32,128]{3,2,1,0:T(8,128)(2,1)}, bf16[16,4,32,128]{3,2,1,0:T(8,128)(2,1)}, u32[]{:S(2)}, u32[]{:S(2)}) collective-permute-start(bf16[16,4,32,128]{3,2,1,0:T(8,128)(2,1)} %dynamic-slice_bitcast_fusion), channel_id=1, source_target_pairs={{0,1},{1,0},{2,3},{3,2},{4,5},{5,4},{6,7},{7,6},{8,9},{9,8},{10,11... | collective-permute-start | bytes 1572872 | tf_op jit(solution)/shard_map/ppermute | solution.py:101
  55.7 23.9 %all-to-all-start.1 = ((bf16[16,4,32,128]{3,2,1,0:T(8,128)(2,1)}), bf16[16,4,32,128]{3,2,1,0:T(8,128)(2,1)}, u32[]{:S(2)}, u32[]{:S(2)}) async-start(bf16[16,4,32,128]{3,2,1,0:T(8,128)(2,1)} %fusion.2), calls=%async_computation.1 | async-start | bytes 1048576 | tf_op jit(solution)/shard_map/all_to_all | solution.py:125
  63.5 4.4 %collective-permute-start.1 = (bf16[16,4,32,128]{3,2,1,0:T(8,128)(2,1)}, bf16[16,4,32,128]{3,2,1,0:T(8,128)(2,1)}, u32[]{:S(2)}, u32[]{:S(2)}) collective-permute-start(bf16[16,4,32,128]{3,2,1,0:T(8,128)(2,1)} %all-to-all-done.2), channel_id=1, source_target_pairs={{0,1},{1,0},{2,3},{3,2},{4,5},{5,4},{6,7},{7,6},{8,9},{9,8},{10,11... | collective-permute-start | bytes 1572872 | tf_op jit(solution)/shard_map/ppermute | solution.py:101
  74.1 10.4 %copy-start.2 = (bf16[4,128,128]{2,1,0:T(8,128)(2,1)S(1)}, bf16[4,128,128]{2,1,0:T(8,128)(2,1)}, u32[]{:S(2)}) copy-start(bf16[4,128,128]{2,1,0:T(8,128)(2,1)} %param.13) | copy-start | bytes 393220
  74.1 11.0 %copy-start.4 = (f32[128]{0:T(128)S(1)}, f32[128]{0:T(128)}, u32[]{:S(2)}) copy-start(f32[128]{0:T(128)} %param.11) | copy-start | bytes 1540
  74.1 11.0 %copy-start.5 = (f32[128]{0:T(128)S(1)}, f32[128]{0:T(128)}, u32[]{:S(2)}) copy-start(f32[128]{0:T(128)} %param.12) | copy-start | bytes 1540
  79.6 18.9 %all-to-all-start.3 = ((bf16[16,4,32,128]{3,2,1,0:T(8,128)(2,1)}), bf16[16,4,32,128]{3,2,1,0:T(8,128)(2,1)S(1)}, u32[]{:S(2)}, u32[]{:S(2)}) async-start(bf16[16,4,32,128]{3,2,1,0:T(8,128)(2,1)} %bitcast.15), calls=%async_computation.3 | async-start | bytes 1048576 | tf_op jit(solution)/shard_map/all_to_all | solution.py:31

commit v4 on v3

--- a/solution.py
+++ b/solution.py
@@ -7,17 +7,6 @@
 def sent_to_all(x, axis):
     devices = lax.axis_size(axis)
     return lax.all_to_all(jnp.broadcast_to(x[None], (devices, *x.shape)), axis, 0, 0, tiled=True)
-
-
-def laid_out(parts, dim):
-    parts = jnp.moveaxis(parts, 0, dim)
-    lengths = parts.shape
-    return parts.reshape(*lengths[:dim], lengths[dim] * lengths[dim + 1], *lengths[dim + 2 :])
-
-
-def collect(x, axis, dim):
-    parts = sent_to_all(x, axis)
-    return laid_out(parts, dim)
 
 
 def split_up(x, dim, devices):
@@ -92,13 +81,14 @@
     return weight_grad.astype(jnp.float32), norm_grad
 
 
-def siblings(devices):
-    return [[c for c in range(devices) if c % 2 == core] for core in range(2)]
+def exchanged(x, axis, step):
+    devices = lax.axis_size(axis)
+    return lax.ppermute(x, axis, [(d, d ^ step) for d in range(devices)])
 
 
-def swapped(x, axis):
-    devices = lax.axis_size(axis)
-    return lax.ppermute(x, axis, [(c, c ^ 1) for c in range(devices)])
+def with_other(near, far, mine, dim):
+    which = jnp.arange(2).reshape([2 if d == dim else 1 for d in range(near.ndim + 1)])
+    return jnp.where(which == mine, jnp.expand_dims(near, dim), jnp.expand_dims(far, dim))
 
 
 def all_steps(
@@ -108,26 +98,37 @@
     window_len = saved_left.shape[2]
     cols = lax.axis_size("col")
     half = cols // 2
-    core = lax.rem(lax.axis_index("col"), 2)
-    groups = siblings(cols)
-    right_rows = collect(saved_right, "row", 1)[0]
+    rows = lax.axis_size("row")
+    col, row = lax.axis_index("col"), lax.axis_index("row")
+    core, x_low = lax.rem(col, 2), lax.rem(lax.div(col, 2), 2)
+    x_high = lax.div(row, rows // 2)
+    lines_y = [[x * (rows // 2) + y for y in range(rows // 2)] for x in range(2)]
+    lines_z = [[z * 4 + k for z in range(cols // 4)] for k in range(4)]
+    one_core = [[c for c in range(cols) if c % 2 == k] for k in range(2)]
+    right_near = jnp.broadcast_to(saved_right, (rows // 2, *saved_right.shape[1:]))
+    right_near = lax.all_to_all(
+        right_near, "row", 0, 0, tiled=True, axis_index_groups=lines_y
+    )
+    right_far = exchanged(right_near, "row", rows // 2)
+    right_rows = with_other(right_near, right_far, x_high, 0).reshape(
+        col_tokens, window_len, channels
+    )
     cot_flat = tri_cotangent.reshape(block_count * own_rows, col_tokens, channels)
-    near = jnp.broadcast_to(saved_left, (half, *saved_left.shape[1:]))
-    near = lax.all_to_all(near, "col", 0, 0, tiled=True, axis_index_groups=groups)
+    left_pair = with_other(saved_left[0], exchanged(saved_left[0], "col", 2), x_low, 0)
+    near = jnp.broadcast_to(left_pair[None], (cols // 4, *left_pair.shape))
+    near = lax.all_to_all(near, "col", 0, 0, tiled=True, axis_index_groups=lines_z)
+    near = near.reshape(half, own_rows, window_len, channels)
     left_part = jnp.einsum(
         "ijh,jkh->ikh", cot_flat, right_rows, preferred_element_type=jnp.float32
     ).astype(jnp.bfloat16)
     pairs = left_part.reshape(half, 2, own_rows, window_len, channels)
     kept = lax.dynamic_index_in_dim(pairs, core, 1, keepdims=False)
     away = lax.dynamic_index_in_dim(pairs, 1 - core, 1, keepdims=False)
-    came = swapped(away, "col")
+    came = exchanged(away, "col", 1)
     chip_part = (kept.astype(jnp.float32) + came.astype(jnp.float32)).astype(jnp.bfloat16)
-    left_arrived = lax.all_to_all(chip_part, "col", 0, 0, tiled=True, axis_index_groups=groups)
-    far = swapped(near, "col")
-    mine = jnp.arange(2).reshape(1, 2, 1, 1, 1) == core
-    left_flat = jnp.where(mine, near[:, None], far[:, None]).reshape(
-        block_count * own_rows, window_len, channels
-    )
+    left_arrived = lax.all_to_all(chip_part, "col", 0, 0, tiled=True, axis_index_groups=one_core)
+    far = exchanged(near, "col", 1)
+    left_flat = with_other(near, far, core, 1).reshape(block_count * own_rows, window_len, channels)
     right_part = jnp.einsum(
         "ijh,ikh->jkh", cot_flat, left_flat, preferred_element_type=jnp.float32
     ).astype(jnp.bfloat16)

time: 149 us -> 150 us (level)
  waiting for transfers between devices: 29.9 us -> 24.5 us
  starting transfers between devices: 40.7 us -> 44.5 us
    ppermute x2 -> x4, starting transfers between devices: 7.57 us -> 16.2 us  [exchanged(): return lax.ppermute(x, axis, [(d, d ^ step) for d in range(devices)])]
    all_to_all x3, waiting for transfers between devices: 14.6 us -> 9.43 us  [the longest x1 6.29 us: all_steps(): lax.all_to_all(right_near, 'row', 0, 0, tiled=True, axis_index_groups=lin...]
    all_to_all x3, starting transfers between devices: 28.3 us -> 24.8 us  [the longest x1 10 us: all_steps(): lax.all_to_all(near, 'col', 0, 0, tiled=True, axis_index_groups=lines_z)]
    another operation x1 -> x0, local copies, waits for them, and re-layouts: 2.82 us -> none  [all_steps(): right_rows = collect(saved_right, 'row', 1)[0]]
    select_n x1 -> x2, local copies, waits for them, and re-layouts: 2.32 us -> 5.13 us  [with_other(): jnp.where(which == mine, jnp.expand_dims(near, dim), jnp.expand_dims(far,...]
    broadcast_in_dim x3 -> x2, local copies, waits for them, and re-layouts: 1.68 us -> 0.03 us  [sent_to_all(): jnp.broadcast_to(x[None], (devices, *x.shape))]
    broadcast_in_dim x3 -> x6, local copies, waits for them, and re-layouts: 1.15 us -> 2.78 us  [the longest x1 1.5 us: all_steps(): jnp.broadcast_to(saved_right, (rows // 2, *saved_right.shape[1:]))]
    ppermute x2 -> x4, waiting for transfers between devices: 3.4 us -> 3.4 us  [exchanged(): return lax.ppermute(x, axis, [(d, d ^ step) for d in range(devices)])]
  transfers between devices with their start and end apart: 6 -> 8, of which waited for: 5 -> 5; matrix products, arithmetic and copies ran while one was open for 16% -> 18% of each run, Pallas kernels for 0% -> 0%
where the time goes in v4:
time: 150 us; the launch traced here: 149 us
  blocking collectives  47.6 us (32%)
  starting transfers between devices  44.5 us (30%)
  waiting for transfers between devices  24.5 us (16%)
  local copies, waits for them, and re-layouts  18 us (12%)
  other arithmetic  8.3 us (6%)
  matrix products  4.72 us (3%)
    all_to_all x2, blocking collectives, sent_to_all(): lax.all_to_all(jnp.broadcast_to(x[None], (devices, *x.shape)), axis, 0, 0...  28.4 us
    all_to_all x1, blocking collectives, summed_over_all(): arrived = lax.all_to_all(packed, 'col', 0, 0, tiled=True)  19.2 us
    ppermute x4, starting transfers between devices, exchanged(): return lax.ppermute(x, axis, [(d, d ^ step) for d in range(devices)])  16.2 us
    all_to_all x1, waiting for transfers between devices, sent_and_summed(): lax.all_to_all(parts, axis, split_axis=0, concat_axis=0, tiled=True)  11.7 us
    all_to_all x1, starting transfers between devices, all_steps(): lax.all_to_all(near, 'col', 0, 0, tiled=True, axis_index_groups=lines_z)  10 us
    all_to_all x1, starting transfers between devices, all_steps(): lax.all_to_all(right_near, 'row', 0, 0, tiled=True, axis_index_groups=lin...  7.64 us
    all_to_all x1, starting transfers between devices, all_steps(): lax.all_to_all(chip_part, 'col', 0, 0, tiled=True, axis_index_groups=one_...  7.11 us
    all_to_all x1, waiting for transfers between devices, all_steps(): lax.all_to_all(right_near, 'row', 0, 0, tiled=True, axis_index_groups=lin...  6.29 us
  transfers between devices with their start and end apart: 8, of which 5 were waited for; matrix products, arithmetic and copies ran while one was open for 18% of the time, Pallas kernels for 0%

profile of v4, /device:TPU:1, one launch (start us, length us, event | category | flops | bytes accessed | tf_op | source)
XLA Modules:
  0.0 148.7 jit_solution(13032848267214429929)
XLA Ops:
  0.6 1.5 %broadcast_in_dim.141 = bf16[8,4,32,128]{3,2,1,0:T(8,128)(2,1)} broadcast(bf16[4,32,128]{2,1,0:T(8,128)(2,1)} %bitcast.81), dimensions={1,2,3} | broadcast | bytes 294912 | tf_op jit(solution)/shard_map/broadcast_in_dim | solution.py:108
  2.1 7.6 %all-to-all-start = ((bf16[8,4,32,128]{3,2,1,0:T(8,128)(2,1)}), bf16[8,4,32,128]{3,2,1,0:T(8,128)(2,1)S(1)}, u32[]{:S(2)}, u32[]{:S(2)}) async-start(bf16[8,4,32,128]{3,2,1,0:T(8,128)(2,1)} %broadcast_in_dim.141), calls=%async_computation | async-start | bytes 524288 | tf_op jit(solution)/shard_map/all_to_all | solution.py:109
  9.8 3.1 %collective-permute-start.2 = (bf16[4,32,128]{2,1,0:T(8,128)(2,1)}, bf16[4,32,128]{2,1,0:T(8,128)(2,1)S(1)}, u32[]{:S(2)}, u32[]{:S(2)}) collective-permute-start(bf16[4,32,128]{2,1,0:T(8,128)(2,1)} %bitcast.82), channel_id=1, source_target_pairs={{0,2},{1,3},{2,0},{3,1},{4,6},{5,7},{6,4},{7,5},{8,10},{9,11},{10,... | collective-permute-start | bytes 98312 | tf_op jit(solution)/shard_map/ppermute | solution.py:86
  12.9 6.3 %all-to-all-done = bf16[8,4,32,128]{3,2,1,0:T(8,128)(2,1)S(1)} async-done(((bf16[8,4,32,128]{3,2,1,0:T(8,128)(2,1)}), bf16[8,4,32,128]{3,2,1,0:T(8,128)(2,1)S(1)}, u32[]{:S(2)}, u32[]{:S(2)}) %all-to-all-start) | async-done | bytes 262176 | tf_op jit(solution)/shard_map/all_to_all | solution.py:109
  19.2 5.7 %collective-permute-start = (bf16[8,4,32,128]{3,2,1,0:T(8,128)(2,1)S(1)}, bf16[8,4,32,128]{3,2,1,0:T(8,128)(2,1)S(1)}, u32[]{:S(2)}, u32[]{:S(2)}) collective-permute-start(bf16[8,4,32,128]{3,2,1,0:T(8,128)(2,1)S(1)} %all-to-all-done), channel_id=1, source_target_pairs={{0,256},{32,288},{64,320},{96,352},{128,384},{160,416},{192,448},{... | collective-permute-start | bytes 786440 | tf_op jit(solution)/shard_map/ppermute | solution.py:86
  25.0 0.1 broadcast_in_dim.138
  25.1 3.8 %copy.27 = bf16[128,64,128]{0,1,2:T(8,128)(2,1)S(1)} copy(bf16[128,64,128]{2,1,0:T(8,128)(2,1)} %bitcast.73) | data formatting | bytes 4194304 | tf_op jit(solution)/shard_map/reshape | solution.py:116
  29.0 0.1 broadcast_select_fusion
  29.1 0.9 broadcast_in_dim.153
  30.0 10.0 %all-to-all-start.2 = ((bf16[8,2,4,32,128]{4,3,2,1,0:T(8,128)(2,1)}), bf16[8,2,4,32,128]{4,3,2,1,0:T(8,128)(2,1)}, u32[]{:S(2)}, u32[]{:S(2)}) async-start(bf16[8,2,4,32,128]{4,3,2,1,0:T(8,128)(2,1)} %broadcast_in_dim.153), calls=%async_computation.2 | async-start | bytes 1048576 | tf_op jit(solution)/shard_map/all_to_all | solution.py:119
  40.0 0.9 bitcast_select_fusion.1
  41.0 2.8 %copy.26 = bf16[64,32,128]{0,1,2:T(8,128)(2,1)S(1)} copy(bf16[64,32,128]{2,1,0:T(8,128)(2,1)} %bitcast_select_fusion.1) | data formatting | bytes 1048576 | tf_op jit(solution)/shard_map/jit(_where)/select_n | solution.py:91
  43.8 1.7 %fusion = bf16[128,32,128]{0,1,2:T(8,128)(2,1)} fusion(bf16[64,32,128]{0,1,2:T(8,128)(2,1)S(1)} %copy.26, bf16[128,64,128]{0,1,2:T(8,128)(2,1)S(1)} %copy.27), kind=kOutput, calls=%fused_computation.2 | convolution fusion | flops 67633152 | bytes 3670016 | tf_op jit(solution)/shard_map/ijh,jkh->ikh/dot_general | solution.py:121
  45.5 2.5 %copy.28 = bf16[128,32,128]{2,1,0:T(8,128)(2,1)S(1)} copy(bf16[128,32,128]{0,1,2:T(8,128)(2,1)} %fusion) | data formatting | bytes 2097152 | tf_op jit(solution)/shard_map/convert_element_type | solution.py:123
  47.9 0.9 dynamic-slice_bitcast_fusion
  48.8 4.8 %collective-permute-start.1 = (bf16[16,4,32,128]{3,2,1,0:T(8,128)(2,1)}, bf16[16,4,32,128]{3,2,1,0:T(8,128)(2,1)}, u32[]{:S(2)}, u32[]{:S(2)}) collective-permute-start(bf16[16,4,32,128]{3,2,1,0:T(8,128)(2,1)} %dynamic-slice_bitcast_fusion), channel_id=1, source_target_pairs={{0,1},{1,0},{2,3},{3,2},{4,5},{5,4},{6,7},{7,6},{8,9},{9,8},{10,11... | collective-permute-start | bytes 1572872 | tf_op jit(solution)/shard_map/ppermute | solution.py:86
  53.6 1.8 %collective-permute-done.1 = bf16[16,4,32,128]{3,2,1,0:T(8,128)(2,1)} collective-permute-done((bf16[16,4,32,128]{3,2,1,0:T(8,128)(2,1)}, bf16[16,4,32,128]{3,2,1,0:T(8,128)(2,1)}, u32[]{:S(2)}, u32[]{:S(2)}) %collective-permute-start.1) | collective-permute-done | bytes 524320 | tf_op jit(solution)/shard_map/ppermute | solution.py:86
  55.5 2.0 %fusion.2 = bf16[16,4,32,128]{3,2,1,0:T(8,128)(2,1)} fusion(bf16[16,4,32,128]{3,2,1,0:T(8,128)(2,1)} %collective-permute-done.1, bf16[16,2,4,32,128]{4,3,2,1,0:T(8,128)(2,1)S(1)} %bitcast.72, s32[]{:T(128)S(6)} %select_n.26), kind=kLoop, calls=%fused_computation.6 | loop fusion | flops 1048576 | bytes 1572868 | tf_op jit(solution)/shard_map/convert_element_type | solution.py:128
  57.5 7.1 %all-to-all-start.1 = ((bf16[16,4,32,128]{3,2,1,0:T(8,128)(2,1)}), bf16[16,4,32,128]{3,2,1,0:T(8,128)(2,1)}, u32[]{:S(2)}, u32[]{:S(2)}) async-start(bf16[16,4,32,128]{3,2,1,0:T(8,128)(2,1)} %fusion.2), calls=%async_computation.1 | async-start | bytes 1048576 | tf_op jit(solution)/shard_map/all_to_all | solution.py:129
  64.6 2.6 %collective-permute-start.3 = (bf16[16,4,32,128]{3,2,1,0:T(8,128)(2,1)}, bf16[16,4,32,128]{3,2,1,0:T(8,128)(2,1)}, u32[]{:S(2)}, u32[]{:S(2)}) collective-permute-start(bf16[16,4,32,128]{3,2,1,0:T(8,128)(2,1)} %bitcast.13), channel_id=1, source_target_pairs={{0,1},{1,0},{2,3},{3,2},{4,5},{5,4},{6,7},{7,6},{8,9},{9,8},{10,11... | collective-permute-start | bytes 1572872 | tf_op jit(solution)/shard_map/ppermute | solution.py:86
  67.2 0.1 broadcast_in_dim.146
  67.2 0.1 broadcast_in_dim.147
  67.4 0.1 convert_reduce_fusion.3
  67.5 1.5 %collective-permute-done.3 = bf16[16,4,32,128]{3,2,1,0:T(8,128)(2,1)} collective-permute-done((bf16[16,4,32,128]{3,2,1,0:T(8,128)(2,1)}, bf16[16,4,32,128]{3,2,1,0:T(8,128)(2,1)}, u32[]{:S(2)}, u32[]{:S(2)}) %collective-permute-start.3) | collective-permute-done | bytes 524320 | tf_op jit(solution)/shard_map/ppermute | solution.py:86
  69.0 1.4 bitcast_select_fusion
  70.4 2.3 %copy.30 = bf16[128,32,128]{0,1,2:T(8,128)(2,1)} copy(bf16[128,32,128]{2,1,0:T(8,128)(2,1)S(1)} %bitcast_select_fusion) | data formatting | bytes 2097152 | tf_op jit(solution)/shard_map/jit(_where)/select_n | solution.py:91
  72.7 2.4 %fusion.1 = bf16[64,32,128]{0,1,2:T(8,128)(2,1)S(1)} fusion(bf16[128,32,128]{0,1,2:T(8,128)(2,1)} %copy.30, bf16[128,64,128]{0,1,2:T(8,128)(2,1)S(1)} %copy.27), kind=kOutput, calls=%fused_computation.3 | convolution fusion | flops 67371008 | bytes 3670016 | tf_op jit(solution)/shard_map/ijh,ikh->jkh/dot_general | solution.py:132
  75.2 2.3 %copy.32 = bf16[64,32,128]{2,1,0:T(8,128)(2,1)} copy(bf16[64,32,128]{0,1,2:T(8,128)(2,1)S(1)} %fusion.1) | data formatting | bytes 1048576 | tf_op jit(solution)/shard_map/convert_element_type | solution.py:134
  77.5 3.1 %all-to-all-done.1 = bf16[16,4,32,128]{3,2,1,0:T(8,128)(2,1)} async-done(((bf16[16,4,32,128]{3,2,1,0:T(8,128)(2,1)}), bf16[16,4,32,128]{3,2,1,0:T(8,128)(2,1)}, u32[]{:S(2)}, u32[]{:S(2)}) %all-to-all-start.1) | async-done | bytes 524320 | tf_op jit(solution)/shard_map/all_to_all | solution.py:129
  80.6 3.6 %all-to-all-start.3 = ((bf16[16,4,32,128]{3,2,1,0:T(8,128)(2,1)}), bf16[16,4,32,128]{3,2,1,0:T(8,128)(2,1)S(1)}, u32[]{:S(2)}, u32[]{:S(2)}) async-start(bf16[16,4,32,128]{3,2,1,0:T(8,128)(2,1)} %bitcast.17), calls=%async_computation.3 | async-start | bytes 1048576 | tf_op jit(solution)/shard_map/all_to_all | solution.py:20
  84.2 0.1 copy.29
  84.3 0.1 div.54
  84.4 0.2 multiply_reduce_fusion.2
  84.6 0.1 rsqrt.13
  84.7 0.1 pad.4.clone
  84.8 0.1 add_convert_fusion
  84.9 0.2 fusion.22
  85.1 1.1 convert_reduce_fusion.1
  86.2 11.7 %all-to-all-done.3 = bf16[16,4,32,128]{3,2,1,0:T(8,128)(2,1)S(1)} async-done(((bf16[16,4,32,128]{3,2,1,0:T(8,128)(2,1)}), bf16[16,4,32,128]{3,2,1,0:T(8,128)(2,1)S(1)}, u32[]{:S(2)}, u32[]{:S(2)}) %all-to-all-start.3) | async-done | bytes 524320 | tf_op jit(solution)/shard_map/all_to_all | solution.py:20
  98.1 0.1 copy.37
  98.2 0.3 multiply_reduce_fusion
  98.5 0.2 convolution_bitcast_fusion
  98.7 0.8 multiply_convert_fusion
  99.6 19.2 %all_to_all.35 = bf16[32,24,128]{2,1,0:T(8,128)(2,1)S(1)} all-to-all(bf16[32,24,128]{2,1,0:T(8,128)(2,1)S(1)} %pad_maximum_fusion), channel_id=1, replica_groups=mesh['row'=16,'col'=32] {'col'}, dimensions={0} | all-to-all | bytes 393216 | tf_op jit(solution)/shard_map/all_to_all | solution.py:75
  118.9 14.0 %all_to_all.36 = f32[16,24,128]{2,1,0:T(8,128)S(1)} all-to-all(f32[16,24,128]{2,1,0:T(8,128)S(1)} %broadcast_in_dim.161), channel_id=1, replica_groups=mesh['row'=16,'col'=32] {'row'}, dimensions={0} | all-to-all | bytes 393216 | tf_op jit(solution)/shard_map/all_to_all | solution.py:9
  132.9 0.6 slice_add_fusion
  133.5 14.4 %all_to_all.37 = bf16[32,16,128]{2,1,0:T(8,128)(2,1)S(1)} all-to-all(bf16[32,16,128]{2,1,0:T(8,128)(2,1)S(1)} %broadcast_in_dim.162), channel_id=1, replica_groups=mesh['row'=16,'col'=32] {'col'}, dimensions={0} | all-to-all | bytes 262144 | tf_op jit(solution)/shard_map/all_to_all | solution.py:9
  147.9 0.7 bitcast_convert_fusion
  (34 shorter events, 0.5 us)
Async XLA Ops:
  2.1 17.1 %all-to-all-start = ((bf16[8,4,32,128]{3,2,1,0:T(8,128)(2,1)}), bf16[8,4,32,128]{3,2,1,0:T(8,128)(2,1)S(1)}, u32[]{:S(2)}, u32[]{:S(2)}) async-start(bf16[8,4,32,128]{3,2,1,0:T(8,128)(2,1)} %broadcast_in_dim.141), calls=%async_computation | async-start | bytes 524288 | tf_op jit(solution)/shard_map/all_to_all | solution.py:109
  9.8 19.2 %collective-permute-start.2 = (bf16[4,32,128]{2,1,0:T(8,128)(2,1)}, bf16[4,32,128]{2,1,0:T(8,128)(2,1)S(1)}, u32[]{:S(2)}, u32[]{:S(2)}) collective-permute-start(bf16[4,32,128]{2,1,0:T(8,128)(2,1)} %bitcast.82), channel_id=1, source_target_pairs={{0,2},{1,3},{2,0},{3,1},{4,6},{5,7},{6,4},{7,5},{8,10},{9,11},{10,... | collective-permute-start | bytes 98312 | tf_op jit(solution)/shard_map/ppermute | solution.py:86
  19.2 20.8 %collective-permute-start = (bf16[8,4,32,128]{3,2,1,0:T(8,128)(2,1)S(1)}, bf16[8,4,32,128]{3,2,1,0:T(8,128)(2,1)S(1)}, u32[]{:S(2)}, u32[]{:S(2)}) collective-permute-start(bf16[8,4,32,128]{3,2,1,0:T(8,128)(2,1)S(1)} %all-to-all-done), channel_id=1, source_target_pairs={{0,256},{32,288},{64,320},{96,352},{128,384},{160,416},{192,448},{... | collective-permute-start | bytes 786440 | tf_op jit(solution)/shard_map/ppermute | solution.py:86
  25.1 3.9 %copy-start.2 = (bf16[1,4,32,128]{3,2,1,0:T(8,128)(2,1)S(1)}, bf16[1,4,32,128]{3,2,1,0:T(8,128)(2,1)}, u32[]{:S(2)}) copy-start(bf16[1,4,32,128]{3,2,1,0:T(8,128)(2,1)} %param.9) | copy-start | bytes 98308
  30.0 27.5 %all-to-all-start.2 = ((bf16[8,2,4,32,128]{4,3,2,1,0:T(8,128)(2,1)}), bf16[8,2,4,32,128]{4,3,2,1,0:T(8,128)(2,1)}, u32[]{:S(2)}, u32[]{:S(2)}) async-start(bf16[8,2,4,32,128]{4,3,2,1,0:T(8,128)(2,1)} %broadcast_in_dim.153), calls=%async_computation.2 | async-start | bytes 1048576 | tf_op jit(solution)/shard_map/all_to_all | solution.py:119
  47.9 19.4 %copy-start = (bf16[1,4,32,128]{3,2,1,0:T(8,128)(2,1)S(1)}, bf16[1,4,32,128]{3,2,1,0:T(8,128)(2,1)}, u32[]{:S(2)}) copy-start(bf16[1,4,32,128]{3,2,1,0:T(8,128)(2,1)} %param.7) | copy-start | bytes 98308
  48.8 6.7 %collective-permute-start.1 = (bf16[16,4,32,128]{3,2,1,0:T(8,128)(2,1)}, bf16[16,4,32,128]{3,2,1,0:T(8,128)(2,1)}, u32[]{:S(2)}, u32[]{:S(2)}) collective-permute-start(bf16[16,4,32,128]{3,2,1,0:T(8,128)(2,1)} %dynamic-slice_bitcast_fusion), channel_id=1, source_target_pairs={{0,1},{1,0},{2,3},{3,2},{4,5},{5,4},{6,7},{7,6},{8,9},{9,8},{10,11... | collective-permute-start | bytes 1572872 | tf_op jit(solution)/shard_map/ppermute | solution.py:86
  57.5 23.2 %all-to-all-start.1 = ((bf16[16,4,32,128]{3,2,1,0:T(8,128)(2,1)}), bf16[16,4,32,128]{3,2,1,0:T(8,128)(2,1)}, u32[]{:S(2)}, u32[]{:S(2)}) async-start(bf16[16,4,32,128]{3,2,1,0:T(8,128)(2,1)} %fusion.2), calls=%async_computation.1 | async-start | bytes 1048576 | tf_op jit(solution)/shard_map/all_to_all | solution.py:129
  64.6 4.4 %collective-permute-start.3 = (bf16[16,4,32,128]{3,2,1,0:T(8,128)(2,1)}, bf16[16,4,32,128]{3,2,1,0:T(8,128)(2,1)}, u32[]{:S(2)}, u32[]{:S(2)}) collective-permute-start(bf16[16,4,32,128]{3,2,1,0:T(8,128)(2,1)} %bitcast.13), channel_id=1, source_target_pairs={{0,1},{1,0},{2,3},{3,2},{4,5},{5,4},{6,7},{7,6},{8,9},{9,8},{10,11... | collective-permute-start | bytes 1572872 | tf_op jit(solution)/shard_map/ppermute | solution.py:86
  75.1 9.1 %copy-start.1 = (bf16[4,128,128]{2,1,0:T(8,128)(2,1)S(1)}, bf16[4,128,128]{2,1,0:T(8,128)(2,1)}, u32[]{:S(2)}) copy-start(bf16[4,128,128]{2,1,0:T(8,128)(2,1)} %param.13) | copy-start | bytes 393220
  75.2 9.6 %copy-start.3 = (f32[128]{0:T(128)S(1)}, f32[128]{0:T(128)}, u32[]{:S(2)}) copy-start(f32[128]{0:T(128)} %param.11) | copy-start | bytes 1540
  75.2 9.6 %copy-start.4 = (f32[128]{0:T(128)S(1)}, f32[128]{0:T(128)}, u32[]{:S(2)}) copy-start(f32[128]{0:T(128)} %param.12) | copy-start | bytes 1540
  80.6 17.3 %all-to-all-start.3 = ((bf16[16,4,32,128]{3,2,1,0:T(8,128)(2,1)}), bf16[16,4,32,128]{3,2,1,0:T(8,128)(2,1)S(1)}, u32[]{:S(2)}, u32[]{:S(2)}) async-start(bf16[16,4,32,128]{3,2,1,0:T(8,128)(2,1)} %bitcast.17), calls=%async_computation.3 | async-start | bytes 1048576 | tf_op jit(solution)/shard_map/all_to_all | solution.py:20

commit v5 on v4

--- a/solution.py
+++ b/solution.py
@@ -1,6 +1,10 @@
+import functools
+
 import jax
 import jax.numpy as jnp
 from jax import lax
+from jax.experimental import pallas as pl
+from jax.experimental.pallas import tpu as pltpu
 from jax.sharding import PartitionSpec as P
 
 
@@ -91,6 +95,126 @@
     return jnp.where(which == mine, jnp.expand_dims(near, dim), jnp.expand_dims(far, dim))
 
 
+PAD = 8
+ROWS_TURNED = (((1,), (1,)), ((), ()))
+
+
+def turned(x):
+    n = x.shape[1]
+    eye = lax.broadcasted_iota(jnp.int32, (n, n), 0) == lax.broadcasted_iota(jnp.int32, (n, n), 1)
+    return lax.dot_general(
+        eye.astype(jnp.float32).astype(jnp.bfloat16),
+        x,
+        ROWS_TURNED,
+        preferred_element_type=jnp.float32,
+    )
+
+
+def left_kernel(window_len, place_ref, near_ref, far_ref, cot_ref, kept_ref, away_ref, *scratch):
+    wide, by_key, product, rows_out = scratch
+    hidden, cols, rows = cot_ref.shape
+    x_high, core = place_ref[0], place_ref[1]
+    group, step = window_len + PAD, hidden + PAD
+    for source, half in ((near_ref, x_high), (far_ref, 1 - x_high)):
+        for j in range(cols // 2):
+            at = pl.multiple_of((half * (cols // 2) + j) * group, 8)
+            wide[pl.ds(at, window_len), :] = source[pl.ds(j * window_len, window_len), :].astype(
+                jnp.float32
+            )
+    for k in range(window_len):
+        by_key[pl.ds(k * step, hidden), :] = turned(
+            wide[pl.ds(k, cols, stride=group), :].astype(jnp.bfloat16)
+        )
+    for h in range(hidden):
+        keys = by_key[pl.ds(h, window_len, stride=step), :].astype(jnp.bfloat16)
+        product[pl.ds(h, window_len, stride=step), :] = jnp.dot(
+            keys, cot_ref[h], preferred_element_type=jnp.float32
+        )
+    for k in range(window_len):
+        rows_out[pl.ds(k, rows, stride=group), :] = turned(
+            product[pl.ds(k * step, hidden), :].astype(jnp.bfloat16)
+        )
+    tokens = kept_ref.shape[1] // window_len
+    for target, side in ((kept_ref, core), (away_ref, 1 - core)):
+        for q in range(kept_ref.shape[0]):
+            for t in range(tokens):
+                at = pl.multiple_of(((2 * q + side) * tokens + t) * group, 8)
+                target[q, pl.ds(t * window_len, window_len), :] = rows_out[
+                    pl.ds(at, window_len), :
+                ].astype(jnp.bfloat16)
+
+
+def left_parts(place, near, far, cot_turned, blocks, window_len):
+    hidden, cols, rows = cot_turned.shape
+    group, step = window_len + PAD, hidden + PAD
+    out = jax.ShapeDtypeStruct((blocks // 2, rows * window_len // blocks, hidden), jnp.bfloat16)
+    here = pl.BlockSpec(memory_space=pltpu.VMEM)
+    return pl.pallas_call(
+        functools.partial(left_kernel, window_len),
+        out_shape=(out, out),
+        in_specs=[pl.BlockSpec(memory_space=pltpu.SMEM), here, here, here],
+        out_specs=(here, here),
+        scratch_shapes=[
+            pltpu.VMEM((cols * group, hidden), jnp.float32),
+            pltpu.VMEM((window_len * step, cols), jnp.float32),
+            pltpu.VMEM((window_len * step, rows), jnp.float32),
+            pltpu.VMEM((rows * group, hidden), jnp.float32),
+        ],
+        name="left_parts",
+    )(place, near, far, cot_turned)
+
+
+def right_kernel(window_len, place_ref, near_ref, far_ref, cot_ref, out_ref, *scratch):
+    wide, by_key, product, rows_out = scratch
+    hidden, cols, rows = cot_ref.shape
+    core = place_ref[1]
+    group, step = window_len + PAD, hidden + PAD
+    tokens = near_ref.shape[1] // window_len
+    for source, side in ((near_ref, core), (far_ref, 1 - core)):
+        for q in range(near_ref.shape[0]):
+            for t in range(tokens):
+                at = pl.multiple_of(((2 * q + side) * tokens + t) * group, 8)
+                wide[pl.ds(at, window_len), :] = source[
+                    q, pl.ds(t * window_len, window_len), :
+                ].astype(jnp.float32)
+    for k in range(window_len):
+        by_key[pl.ds(k * step, hidden), :] = turned(
+            wide[pl.ds(k, rows, stride=group), :].astype(jnp.bfloat16)
+        )
+    for h in range(hidden):
+        keys = by_key[pl.ds(h, window_len, stride=step), :].astype(jnp.bfloat16)
+        product[pl.ds(h, window_len, stride=step), :] = lax.dot_general(
+            keys, cot_ref[h], ROWS_TURNED, preferred_element_type=jnp.float32
+        )
+    for k in range(window_len):
+        rows_out[pl.ds(k, cols, stride=group), :] = turned(
+            product[pl.ds(k * step, hidden), :].astype(jnp.bfloat16)
+        )
+    for j in range(cols):
+        out_ref[pl.ds(j * window_len, window_len), :] = rows_out[
+            pl.ds(j * group, window_len), :
+        ].astype(jnp.bfloat16)
+
+
+def right_parts(place, near, far, cot_turned, window_len):
+    hidden, cols, rows = cot_turned.shape
+    group, step = window_len + PAD, hidden + PAD
+    here = pl.BlockSpec(memory_space=pltpu.VMEM)
+    return pl.pallas_call(
+        functools.partial(right_kernel, window_len),
+        out_shape=jax.ShapeDtypeStruct((cols * window_len, hidden), jnp.bfloat16),
+        in_specs=[pl.BlockSpec(memory_space=pltpu.SMEM), here, here, here],
+        out_specs=here,
+        scratch_shapes=[
+            pltpu.VMEM((rows * group, hidden), jnp.float32),
+            pltpu.VMEM((window_len * step, rows), jnp.float32),
+            pltpu.VMEM((window_len * step, cols), jnp.float32),
+            pltpu.VMEM((cols * group, hidden), jnp.float32),
+        ],
+        name="right_parts",
+    )(place, near, far, cot_turned)
+
+
 def all_steps(
     pair_window, tri_cotangent, saved_left, saved_right, norm_gain, norm_bias, proj_weight
 ):
@@ -110,28 +234,26 @@
         right_near, "row", 0, 0, tiled=True, axis_index_groups=lines_y
     )
     right_far = exchanged(right_near, "row", rows // 2)
-    right_rows = with_other(right_near, right_far, x_high, 0).reshape(
-        col_tokens, window_len, channels
-    )
-    cot_flat = tri_cotangent.reshape(block_count * own_rows, col_tokens, channels)
+    cot_turned = lax.optimization_barrier(
+        jnp.transpose(
+            tri_cotangent.reshape(block_count * own_rows, col_tokens, channels), (2, 1, 0)
+        )
+    )
+    place = jnp.stack([x_high, core])
     left_pair = with_other(saved_left[0], exchanged(saved_left[0], "col", 2), x_low, 0)
     near = jnp.broadcast_to(left_pair[None], (cols // 4, *left_pair.shape))
     near = lax.all_to_all(near, "col", 0, 0, tiled=True, axis_index_groups=lines_z)
-    near = near.reshape(half, own_rows, window_len, channels)
-    left_part = jnp.einsum(
-        "ijh,jkh->ikh", cot_flat, right_rows, preferred_element_type=jnp.float32
-    ).astype(jnp.bfloat16)
-    pairs = left_part.reshape(half, 2, own_rows, window_len, channels)
-    kept = lax.dynamic_index_in_dim(pairs, core, 1, keepdims=False)
-    away = lax.dynamic_index_in_dim(pairs, 1 - core, 1, keepdims=False)
+    near = near.reshape(half, own_rows * window_len, channels)
+    flat = (-1, channels)
+    kept, away = left_parts(
+        place, right_near.reshape(flat), right_far.reshape(flat), cot_turned, cols, window_len
+    )
     came = exchanged(away, "col", 1)
     chip_part = (kept.astype(jnp.float32) + came.astype(jnp.float32)).astype(jnp.bfloat16)
     left_arrived = lax.all_to_all(chip_part, "col", 0, 0, tiled=True, axis_index_groups=one_core)
     far = exchanged(near, "col", 1)
-    left_flat = with_other(near, far, core, 1).reshape(block_count * own_rows, window_len, channels)
-    right_part = jnp.einsum(
-        "ijh,ikh->jkh", cot_flat, left_flat, preferred_element_type=jnp.float32
-    ).astype(jnp.bfloat16)
+    right_part = right_parts(place, near, far, cot_turned, window_len)
+    right_part = right_part.reshape(col_tokens, window_len, channels)
     left_grad = left_arrived.astype(jnp.float32).sum(axis=0)
     right_grad = sent_and_summed(right_part, "row", 0)
     positions = own_rows * window_len

time: 150 us -> 147 us (0.980)
  Pallas kernels: 0 us -> 10.6 us
  local copies, waits for them, and re-layouts: 18 us -> 8.09 us
  matrix products: 4.72 us -> 0.65 us
  waiting for transfers between devices: 24.5 us -> 27.5 us
  other arithmetic: 8.3 us -> 6.25 us
    pallas_call x0 -> x2, Pallas kernels: none -> 10.6 us  [the longest x1 5.74 us: right_parts(): pl.pallas_call(functools.partial(right_kernel, window_len), out_shape=jax...]
    select_n x2 -> x0, local copies, waits for them, and re-layouts: 5.13 us -> none  [with_other(): jnp.where(which == mine, jnp.expand_dims(near, dim), jnp.expand_dims(far,...]
    convert_element_type x2 -> x0, local copies, waits for them, and re-layouts: 4.77 us -> none  [the longest x1 2.47 us: all_steps(): left_part = jnp.einsum('ijh,jkh->ikh', cot_flat, right_rows, preferred_el...]
    dot_general x2 -> x0, matrix products: 4.07 us -> none  [the longest x1 2.41 us: all_steps(): jnp.einsum('ijh,ikh->jkh', cot_flat, left_flat, preferred_element_type=jn...]
    all_to_all x1, waiting for transfers between devices: 3.13 us -> 5.34 us  [all_steps(): lax.all_to_all(chip_part, 'col', 0, 0, tiled=True, axis_index_groups=one_...]
    select_n x3 -> x1, other arithmetic: 2.42 us -> 0.84 us  [with_other(): jnp.where(which == mine, jnp.expand_dims(near, dim), jnp.expand_dims(far,...]
    unnamed x11 -> x19, local copies, waits for them, and re-layouts: 0.17 us -> 1.67 us
  transfers between devices with their start and end apart: 8 -> 8, of which waited for: 5 -> 5; matrix products, arithmetic and copies ran while one was open for 18% -> 6% of each run, Pallas kernels for 0% -> 7%
where the time goes in v5:
time: 147 us; the launch traced here: 146 us
  blocking collectives  47.4 us (32%)
  starting transfers between devices  44.4 us (30%)
  waiting for transfers between devices  27.5 us (19%)
  Pallas kernels  10.6 us (7%)
  local copies, waits for them, and re-layouts  8.09 us (6%)
  other arithmetic  6.25 us (4%)
    all_to_all x2, blocking collectives, sent_to_all(): lax.all_to_all(jnp.broadcast_to(x[None], (devices, *x.shape)), axis, 0, 0...  28.4 us
    all_to_all x1, blocking collectives, summed_over_all(): arrived = lax.all_to_all(packed, 'col', 0, 0, tiled=True)  19 us
    ppermute x4, starting transfers between devices, exchanged(): return lax.ppermute(x, axis, [(d, d ^ step) for d in range(devices)])  16.2 us
    all_to_all x1, waiting for transfers between devices, sent_and_summed(): lax.all_to_all(parts, axis, split_axis=0, concat_axis=0, tiled=True)  12.8 us
    all_to_all x1, starting transfers between devices, all_steps(): lax.all_to_all(near, 'col', 0, 0, tiled=True, axis_index_groups=lines_z)  10 us
    all_to_all x1, starting transfers between devices, all_steps(): lax.all_to_all(right_near, 'row', 0, 0, tiled=True, axis_index_groups=lin...  7.64 us
    all_to_all x1, starting transfers between devices, all_steps(): lax.all_to_all(chip_part, 'col', 0, 0, tiled=True, axis_index_groups=one_...  7.05 us
    all_to_all x1, waiting for transfers between devices, all_steps(): lax.all_to_all(right_near, 'row', 0, 0, tiled=True, axis_index_groups=lin...  6.3 us
  transfers between devices with their start and end apart: 8, of which 5 were waited for; matrix products, arithmetic and copies ran while one was open for 6% of the time, Pallas kernels for 7%

profile of v5, /device:TPU:1, one launch (start us, length us, event | category | flops | bytes accessed | tf_op | source)
XLA Modules:
  0.0 145.8 jit_solution(8403381492608727092)
XLA Ops:
  0.6 1.7 %broadcast_in_dim.41 = bf16[8,4,32,128]{3,2,1,0:T(8,128)(2,1)} broadcast(bf16[4,32,128]{2,1,0:T(8,128)(2,1)} %bitcast.64), dimensions={1,2,3} | broadcast | bytes 294912 | tf_op jit(solution)/shard_map/broadcast_in_dim | solution.py:232
  2.3 7.6 %all-to-all-start = ((bf16[8,4,32,128]{3,2,1,0:T(8,128)(2,1)}), bf16[8,4,32,128]{3,2,1,0:T(8,128)(2,1)S(1)}, u32[]{:S(2)}, u32[]{:S(2)}) async-start(bf16[8,4,32,128]{3,2,1,0:T(8,128)(2,1)} %broadcast_in_dim.41), calls=%async_computation | async-start | bytes 524288 | tf_op jit(solution)/shard_map/all_to_all | solution.py:233
  9.9 3.1 %collective-permute-start.2 = (bf16[4,32,128]{2,1,0:T(8,128)(2,1)}, bf16[4,32,128]{2,1,0:T(8,128)(2,1)S(1)}, u32[]{:S(2)}, u32[]{:S(2)}) collective-permute-start(bf16[4,32,128]{2,1,0:T(8,128)(2,1)} %bitcast.65), channel_id=1, source_target_pairs={{0,2},{1,3},{2,0},{3,1},{4,6},{5,7},{6,4},{7,5},{8,10},{9,11},{10,... | collective-permute-start | bytes 98312 | tf_op jit(solution)/shard_map/ppermute | solution.py:90
  13.1 6.3 %all-to-all-done = bf16[8,4,32,128]{3,2,1,0:T(8,128)(2,1)S(1)} async-done(((bf16[8,4,32,128]{3,2,1,0:T(8,128)(2,1)}), bf16[8,4,32,128]{3,2,1,0:T(8,128)(2,1)S(1)}, u32[]{:S(2)}, u32[]{:S(2)}) %all-to-all-start) | async-done | bytes 262176 | tf_op jit(solution)/shard_map/all_to_all | solution.py:233
  19.4 5.7 %collective-permute-start = (bf16[8,4,32,128]{3,2,1,0:T(8,128)(2,1)S(1)}, bf16[8,4,32,128]{3,2,1,0:T(8,128)(2,1)S(1)}, u32[]{:S(2)}, u32[]{:S(2)}) collective-permute-start(bf16[8,4,32,128]{3,2,1,0:T(8,128)(2,1)S(1)} %all-to-all-done), channel_id=1, source_target_pairs={{0,256},{32,288},{64,320},{96,352},{128,384},{160,416},{192,448},{... | collective-permute-start | bytes 786440 | tf_op jit(solution)/shard_map/ppermute | solution.py:90
  25.1 0.8 broadcast_select_fusion
  25.9 0.9 broadcast_in_dim.74
  26.8 10.0 %all-to-all-start.2 = ((bf16[8,2,4,32,128]{4,3,2,1,0:T(8,128)(2,1)}), bf16[8,2,4,32,128]{4,3,2,1,0:T(8,128)(2,1)S(1)}, u32[]{:S(2)}, u32[]{:S(2)}) async-start(bf16[8,2,4,32,128]{4,3,2,1,0:T(8,128)(2,1)} %broadcast_in_dim.74), calls=%async_computation.2 | async-start | bytes 1048576 | tf_op jit(solution)/shard_map/all_to_all | solution.py:245
  36.9 3.4 %copy.17 = bf16[128,64,128]{0,1,2:T(8,128)(2,1)} copy(bf16[128,64,128]{2,1,0:T(8,128)(2,1)S(1)} %bitcast.51) | data formatting | bytes 4194304 | tf_op jit(solution)/shard_map/reshape | solution.py:239
  40.3 0.6 pad_add_fusion.place_ref
  40.9 0.0 collective-permute-done
  40.9 0.7 copy-done.5
  41.6 4.8 %left_parts.1 = (bf16[16,128,128]{2,1,0:T(8,128)(2,1)}, bf16[16,128,128]{2,1,0:T(8,128)(2,1)}) custom-call(s32[2]{0:T(128)} %pad_add_fusion.place_ref, bf16[1024,128]{1,0:T(8,128)(2,1)} %bitcast.55, bf16[1024,128]{1,0:T(8,128)(2,1)} %bitcast.63, bf16[128,64,128]{2,1,0:T(8,128)(2,1)} %bitcast.49), custom_call_target="tpu_custom_call" | custom-call | tf_op jit(solution)/shard_map/left_parts/pallas_call | solution.py:152
  46.5 4.8 %collective-permute-start.1 = (bf16[16,128,128]{2,1,0:T(8,128)(2,1)}, bf16[16,128,128]{2,1,0:T(8,128)(2,1)S(1)}, u32[]{:S(2)}, u32[]{:S(2)}) collective-permute-start(bf16[16,128,128]{2,1,0:T(8,128)(2,1)} %get-tuple-element.11), channel_id=1, source_target_pairs={{0,1},{1,0},{2,3},{3,2},{4,5},{5,4},{6,7},{7,6},{8,9},{9,8},{10,11... | collective-permute-start | bytes 1572872 | tf_op jit(solution)/shard_map/ppermute | solution.py:90
  51.3 1.7 %collective-permute-done.1 = bf16[16,128,128]{2,1,0:T(8,128)(2,1)S(1)} collective-permute-done((bf16[16,128,128]{2,1,0:T(8,128)(2,1)}, bf16[16,128,128]{2,1,0:T(8,128)(2,1)S(1)}, u32[]{:S(2)}, u32[]{:S(2)}) %collective-permute-start.1) | collective-permute-done | bytes 524320 | tf_op jit(solution)/shard_map/ppermute | solution.py:90
  53.0 2.0 %add_convert_fusion = bf16[16,128,128]{2,1,0:T(8,128)(2,1)} fusion(bf16[16,128,128]{2,1,0:T(8,128)(2,1)S(1)} %collective-permute-done.1, bf16[16,128,128]{2,1,0:T(8,128)(2,1)} %get-tuple-element.10), kind=kLoop, calls=%fused_computation.3 | loop fusion | flops 1048576 | bytes 1572864 | tf_op jit(solution)/shard_map/convert_element_type | solution.py:252
  55.0 7.0 %all-to-all-start.1 = ((bf16[16,128,128]{2,1,0:T(8,128)(2,1)}), bf16[16,128,128]{2,1,0:T(8,128)(2,1)S(1)}, u32[]{:S(2)}, u32[]{:S(2)}) async-start(bf16[16,128,128]{2,1,0:T(8,128)(2,1)} %add_convert_fusion), calls=%async_computation.1 | async-start | bytes 1048576 | tf_op jit(solution)/shard_map/all_to_all | solution.py:253
  62.0 2.6 %collective-permute-start.3 = (bf16[16,128,128]{2,1,0:T(8,128)(2,1)S(1)}, bf16[16,128,128]{2,1,0:T(8,128)(2,1)S(1)}, u32[]{:S(2)}, u32[]{:S(2)}) collective-permute-start(bf16[16,128,128]{2,1,0:T(8,128)(2,1)S(1)} %bitcast.52), channel_id=1, source_target_pairs={{0,1},{1,0},{2,3},{3,2},{4,5},{5,4},{6,7},{7,6},{8,9},{9,8},{10,11... | collective-permute-start | bytes 1572872 | tf_op jit(solution)/shard_map/ppermute | solution.py:90
  64.6 0.1 convert_reduce_fusion.3
  64.7 0.0 copy-start.6
  64.7 0.0 copy-start.7
  64.7 0.0 copy-start.8
  64.7 1.4 collective-permute-done.3.far_ref
  66.1 0.8 copy-done.4
  66.9 5.7 %right_parts.1 = bf16[2048,128]{1,0:T(8,128)(2,1)} custom-call(s32[2]{0:T(128)} %pad_add_fusion.place_ref, bf16[16,128,128]{2,1,0:T(8,128)(2,1)} %bitcast.53, bf16[16,128,128]{2,1,0:T(8,128)(2,1)} %copy-done.4, bf16[128,64,128]{2,1,0:T(8,128)(2,1)} %bitcast.50), custom_call_target="tpu_custom_call" | custom-call | tf_op jit(solution)/shard_map/right_parts/pallas_call | solution.py:203
  72.7 5.3 %all-to-all-done.1 = bf16[16,128,128]{2,1,0:T(8,128)(2,1)S(1)} async-done(((bf16[16,128,128]{2,1,0:T(8,128)(2,1)}), bf16[16,128,128]{2,1,0:T(8,128)(2,1)S(1)}, u32[]{:S(2)}, u32[]{:S(2)}) %all-to-all-start.1) | async-done | bytes 524320 | tf_op jit(solution)/shard_map/all_to_all | solution.py:253
  78.0 3.6 %all-to-all-start.3 = ((bf16[16,4,32,128]{3,2,1,0:T(8,128)(2,1)}), bf16[16,4,32,128]{3,2,1,0:T(8,128)(2,1)S(1)}, u32[]{:S(2)}, u32[]{:S(2)}) async-start(bf16[16,4,32,128]{3,2,1,0:T(8,128)(2,1)} %bitcast.54), calls=%async_computation.3 | async-start | bytes 1048576 | tf_op jit(solution)/shard_map/all_to_all | solution.py:24
  81.6 0.1 copy.18
  81.7 0.1 div.54
  81.8 0.2 multiply_reduce_fusion.2
  82.0 0.1 rsqrt.13
  82.1 0.1 pad.4.clone
  82.2 0.1 add_convert_fusion.1
  82.3 0.2 fusion.18
  82.5 0.1 convert_reduce_fusion.1
  82.6 12.8 %all-to-all-done.3 = bf16[16,4,32,128]{3,2,1,0:T(8,128)(2,1)S(1)} async-done(((bf16[16,4,32,128]{3,2,1,0:T(8,128)(2,1)}), bf16[16,4,32,128]{3,2,1,0:T(8,128)(2,1)S(1)}, u32[]{:S(2)}, u32[]{:S(2)}) %all-to-all-start.3) | async-done | bytes 524320 | tf_op jit(solution)/shard_map/all_to_all | solution.py:24
  95.3 0.1 convert_reduce_fusion
  95.4 0.1 fusion.11
  95.5 0.1 copy.23
  95.6 0.3 multiply_reduce_fusion
  95.9 0.2 convolution_bitcast_fusion
  96.1 0.8 multiply_convert_fusion
  96.9 0.1 maximum_maximum_fusion
  97.0 19.0 %all_to_all.35 = bf16[32,24,128]{2,1,0:T(8,128)(2,1)S(1)} all-to-all(bf16[32,24,128]{2,1,0:T(8,128)(2,1)S(1)} %pad_maximum_fusion), channel_id=1, replica_groups=mesh['row'=16,'col'=32] {'col'}, dimensions={0} | all-to-all | bytes 393216 | tf_op jit(solution)/shard_map/all_to_all | solution.py:79
  116.1 14.0 %all_to_all.36 = f32[16,24,128]{2,1,0:T(8,128)S(1)} all-to-all(f32[16,24,128]{2,1,0:T(8,128)S(1)} %broadcast_in_dim.77), channel_id=1, replica_groups=mesh['row'=16,'col'=32] {'row'}, dimensions={0} | all-to-all | bytes 393216 | tf_op jit(solution)/shard_map/all_to_all | solution.py:13
  130.1 0.6 slice_add_fusion
  130.7 14.4 %all_to_all.37 = bf16[32,16,128]{2,1,0:T(8,128)(2,1)S(1)} all-to-all(bf16[32,16,128]{2,1,0:T(8,128)(2,1)S(1)} %broadcast_in_dim.78), channel_id=1, replica_groups=mesh['row'=16,'col'=32] {'col'}, dimensions={0} | all-to-all | bytes 262144 | tf_op jit(solution)/shard_map/all_to_all | solution.py:13
  145.1 0.7 bitcast_convert_fusion
  (30 shorter events, 0.2 us)
Async XLA Ops:
  0.6 36.3 %copy-start = (bf16[32,4,64,128]{3,2,1,0:T(8,128)(2,1)S(1)}, bf16[32,4,64,128]{3,2,1,0:T(8,128)(2,1)}, u32[]{:S(2)}) copy-start(bf16[32,4,64,128]{3,2,1,0:T(8,128)(2,1)} %param.8) | copy-start | bytes 6291460
  2.3 17.1 %all-to-all-start = ((bf16[8,4,32,128]{3,2,1,0:T(8,128)(2,1)}), bf16[8,4,32,128]{3,2,1,0:T(8,128)(2,1)S(1)}, u32[]{:S(2)}, u32[]{:S(2)}) async-start(bf16[8,4,32,128]{3,2,1,0:T(8,128)(2,1)} %broadcast_in_dim.41), calls=%async_computation | async-start | bytes 524288 | tf_op jit(solution)/shard_map/all_to_all | solution.py:233
  9.9 15.2 %collective-permute-start.2 = (bf16[4,32,128]{2,1,0:T(8,128)(2,1)}, bf16[4,32,128]{2,1,0:T(8,128)(2,1)S(1)}, u32[]{:S(2)}, u32[]{:S(2)}) collective-permute-start(bf16[4,32,128]{2,1,0:T(8,128)(2,1)} %bitcast.65), channel_id=1, source_target_pairs={{0,2},{1,3},{2,0},{3,1},{4,6},{5,7},{6,4},{7,5},{8,10},{9,11},{10,... | collective-permute-start | bytes 98312 | tf_op jit(solution)/shard_map/ppermute | solution.py:90
  19.4 20.9 %copy-start.2 = (bf16[8,4,32,128]{3,2,1,0:T(8,128)(2,1)}, bf16[8,4,32,128]{3,2,1,0:T(8,128)(2,1)S(1)}, u32[]{:S(2)}) copy-start(bf16[8,4,32,128]{3,2,1,0:T(8,128)(2,1)S(1)} %all-to-all-done) | copy-start | bytes 786436
  19.4 21.5 %collective-permute-start = (bf16[8,4,32,128]{3,2,1,0:T(8,128)(2,1)S(1)}, bf16[8,4,32,128]{3,2,1,0:T(8,128)(2,1)S(1)}, u32[]{:S(2)}, u32[]{:S(2)}) collective-permute-start(bf16[8,4,32,128]{3,2,1,0:T(8,128)(2,1)S(1)} %all-to-all-done), channel_id=1, source_target_pairs={{0,256},{32,288},{64,320},{96,352},{128,384},{160,416},{192,448},{... | collective-permute-start | bytes 786440 | tf_op jit(solution)/shard_map/ppermute | solution.py:90
  26.8 28.1 %all-to-all-start.2 = ((bf16[8,2,4,32,128]{4,3,2,1,0:T(8,128)(2,1)}), bf16[8,2,4,32,128]{4,3,2,1,0:T(8,128)(2,1)S(1)}, u32[]{:S(2)}, u32[]{:S(2)}) async-start(bf16[8,2,4,32,128]{4,3,2,1,0:T(8,128)(2,1)} %broadcast_in_dim.74), calls=%async_computation.2 | async-start | bytes 1048576 | tf_op jit(solution)/shard_map/all_to_all | solution.py:245
  40.9 0.7 copy-start.5
  41.6 23.0 %copy-start.3 = (bf16[1,4,32,128]{3,2,1,0:T(8,128)(2,1)S(1)}, bf16[1,4,32,128]{3,2,1,0:T(8,128)(2,1)}, u32[]{:S(2)}) copy-start(bf16[1,4,32,128]{3,2,1,0:T(8,128)(2,1)} %param.7) | copy-start | bytes 98308
  46.5 6.5 %collective-permute-start.1 = (bf16[16,128,128]{2,1,0:T(8,128)(2,1)}, bf16[16,128,128]{2,1,0:T(8,128)(2,1)S(1)}, u32[]{:S(2)}, u32[]{:S(2)}) collective-permute-start(bf16[16,128,128]{2,1,0:T(8,128)(2,1)} %get-tuple-element.11), channel_id=1, source_target_pairs={{0,1},{1,0},{2,3},{3,2},{4,5},{5,4},{6,7},{7,6},{8,9},{9,8},{10,11... | collective-permute-start | bytes 1572872 | tf_op jit(solution)/shard_map/ppermute | solution.py:90
  55.0 11.1 %copy-start.1 = (bf16[8,2,4,32,128]{4,3,2,1,0:T(8,128)(2,1)}, bf16[8,2,4,32,128]{4,3,2,1,0:T(8,128)(2,1)S(1)}, u32[]{:S(2)}) copy-start(bf16[8,2,4,32,128]{4,3,2,1,0:T(8,128)(2,1)S(1)} %all-to-all-done.2) | copy-start | bytes 1572868
  55.0 23.0 %all-to-all-start.1 = ((bf16[16,128,128]{2,1,0:T(8,128)(2,1)}), bf16[16,128,128]{2,1,0:T(8,128)(2,1)S(1)}, u32[]{:S(2)}, u32[]{:S(2)}) async-start(bf16[16,128,128]{2,1,0:T(8,128)(2,1)} %add_convert_fusion), calls=%async_computation.1 | async-start | bytes 1048576 | tf_op jit(solution)/shard_map/all_to_all | solution.py:253
  62.0 4.1 %collective-permute-start.3 = (bf16[16,128,128]{2,1,0:T(8,128)(2,1)S(1)}, bf16[16,128,128]{2,1,0:T(8,128)(2,1)S(1)}, u32[]{:S(2)}, u32[]{:S(2)}) collective-permute-start(bf16[16,128,128]{2,1,0:T(8,128)(2,1)S(1)} %bitcast.52), channel_id=1, source_target_pairs={{0,1},{1,0},{2,3},{3,2},{4,5},{5,4},{6,7},{7,6},{8,9},{9,8},{10,11... | collective-permute-start | bytes 1572872 | tf_op jit(solution)/shard_map/ppermute | solution.py:90
  64.7 16.9 %copy-start.6 = (bf16[4,128,128]{2,1,0:T(8,128)(2,1)S(1)}, bf16[4,128,128]{2,1,0:T(8,128)(2,1)}, u32[]{:S(2)}) copy-start(bf16[4,128,128]{2,1,0:T(8,128)(2,1)} %param.13) | copy-start | bytes 393220
  64.7 17.5 %copy-start.7 = (f32[128]{0:T(128)S(1)}, f32[128]{0:T(128)}, u32[]{:S(2)}) copy-start(f32[128]{0:T(128)} %param.11) | copy-start | bytes 1540
  64.7 17.5 %copy-start.8 = (f32[128]{0:T(128)S(1)}, f32[128]{0:T(128)}, u32[]{:S(2)}) copy-start(f32[128]{0:T(128)} %param.12) | copy-start | bytes 1540
  66.1 0.8 copy-start.4
  78.0 17.3 %all-to-all-start.3 = ((bf16[16,4,32,128]{3,2,1,0:T(8,128)(2,1)}), bf16[16,4,32,128]{3,2,1,0:T(8,128)(2,1)S(1)}, u32[]{:S(2)}, u32[]{:S(2)}) async-start(bf16[16,4,32,128]{3,2,1,0:T(8,128)(2,1)} %bitcast.54), calls=%async_computation.3 | async-start | bytes 1048576 | tf_op jit(solution)/shard_map/all_to_all | solution.py:24

commit v6 on v5

--- a/solution.py
+++ b/solution.py
@@ -90,11 +90,6 @@
     return lax.ppermute(x, axis, [(d, d ^ step) for d in range(devices)])
 
 
-def with_other(near, far, mine, dim):
-    which = jnp.arange(2).reshape([2 if d == dim else 1 for d in range(near.ndim + 1)])
-    return jnp.where(which == mine, jnp.expand_dims(near, dim), jnp.expand_dims(far, dim))
-
-
 PAD = 8
 ROWS_TURNED = (((1,), (1,)), ((), ()))
 
@@ -110,10 +105,18 @@
     )
 
 
-def left_kernel(window_len, place_ref, near_ref, far_ref, cot_ref, kept_ref, away_ref, *scratch):
-    wide, by_key, product, rows_out = scratch
+def place_of():
+    row, col = lax.axis_index("row"), lax.axis_index("col")
+    half = lax.axis_size("row") // 2
+    return lax.div(row, half), lax.rem(lax.div(col, 2), 2), lax.rem(col, 2)
+
+
+def left_kernel(window_len, near_ref, far_ref, cot_hbm, kept_ref, away_ref, *scratch):
+    wide, by_key, product, rows_out, cot_ref, arrived = scratch
+    fetch = pltpu.make_async_copy(cot_hbm, cot_ref, arrived)
+    fetch.start()
     hidden, cols, rows = cot_ref.shape
-    x_high, core = place_ref[0], place_ref[1]
+    x_high, _, core = place_of()
     group, step = window_len + PAD, hidden + PAD
     for source, half in ((near_ref, x_high), (far_ref, 1 - x_high)):
         for j in range(cols // 2):
@@ -125,6 +128,7 @@
         by_key[pl.ds(k * step, hidden), :] = turned(
             wide[pl.ds(k, cols, stride=group), :].astype(jnp.bfloat16)
         )
+    fetch.wait()
     for h in range(hidden):
         keys = by_key[pl.ds(h, window_len, stride=step), :].astype(jnp.bfloat16)
         product[pl.ds(h, window_len, stride=step), :] = jnp.dot(
@@ -144,7 +148,7 @@
                 ].astype(jnp.bfloat16)
 
 
-def left_parts(place, near, far, cot_turned, blocks, window_len):
+def left_parts(near, far, cot_turned, blocks, window_len):
     hidden, cols, rows = cot_turned.shape
     group, step = window_len + PAD, hidden + PAD
     out = jax.ShapeDtypeStruct((blocks // 2, rows * window_len // blocks, hidden), jnp.bfloat16)
@@ -152,35 +156,45 @@
     return pl.pallas_call(
         functools.partial(left_kernel, window_len),
         out_shape=(out, out),
-        in_specs=[pl.BlockSpec(memory_space=pltpu.SMEM), here, here, here],
+        in_specs=[here, here, pl.BlockSpec(memory_space=pl.ANY)],
         out_specs=(here, here),
         scratch_shapes=[
             pltpu.VMEM((cols * group, hidden), jnp.float32),
             pltpu.VMEM((window_len * step, cols), jnp.float32),
             pltpu.VMEM((window_len * step, rows), jnp.float32),
             pltpu.VMEM((rows * group, hidden), jnp.float32),
+            pltpu.VMEM(cot_turned.shape, cot_turned.dtype),
+            pltpu.SemaphoreType.DMA,
         ],
         name="left_parts",
-    )(place, near, far, cot_turned)
-
-
-def right_kernel(window_len, place_ref, near_ref, far_ref, cot_ref, out_ref, *scratch):
-    wide, by_key, product, rows_out = scratch
+    )(near, far, cot_turned)
+
+
+def right_kernel(window_len, own_ref, x_ref, core_ref, both_ref, cot_hbm, out_ref, *scratch):
+    wide, by_key, product, rows_out, cot_ref, arrived = scratch
+    fetch = pltpu.make_async_copy(cot_hbm, cot_ref, arrived)
+    fetch.start()
     hidden, cols, rows = cot_ref.shape
-    core = place_ref[1]
+    _, x_low, core = place_of()
     group, step = window_len + PAD, hidden + PAD
-    tokens = near_ref.shape[1] // window_len
-    for source, side in ((near_ref, core), (far_ref, 1 - core)):
-        for q in range(near_ref.shape[0]):
+    tokens = own_ref.shape[1] // window_len
+    for source, x, side in (
+        (own_ref, x_low, core),
+        (x_ref, 1 - x_low, core),
+        (core_ref, x_low, 1 - core),
+        (both_ref, 1 - x_low, 1 - core),
+    ):
+        for z in range(own_ref.shape[0]):
             for t in range(tokens):
-                at = pl.multiple_of(((2 * q + side) * tokens + t) * group, 8)
+                at = pl.multiple_of(((z * 4 + 2 * x + side) * tokens + t) * group, 8)
                 wide[pl.ds(at, window_len), :] = source[
-                    q, pl.ds(t * window_len, window_len), :
+                    z, pl.ds(t * window_len, window_len), :
                 ].astype(jnp.float32)
     for k in range(window_len):
         by_key[pl.ds(k * step, hidden), :] = turned(
             wide[pl.ds(k, rows, stride=group), :].astype(jnp.bfloat16)
         )
+    fetch.wait()
     for h in range(hidden):
         keys = by_key[pl.ds(h, window_len, stride=step), :].astype(jnp.bfloat16)
         product[pl.ds(h, window_len, stride=step), :] = lax.dot_general(
@@ -196,23 +210,25 @@
         ].astype(jnp.bfloat16)
 
 
-def right_parts(place, near, far, cot_turned, window_len):
+def right_parts(pieces, cot_turned, window_len):
     hidden, cols, rows = cot_turned.shape
     group, step = window_len + PAD, hidden + PAD
     here = pl.BlockSpec(memory_space=pltpu.VMEM)
     return pl.pallas_call(
         functools.partial(right_kernel, window_len),
         out_shape=jax.ShapeDtypeStruct((cols * window_len, hidden), jnp.bfloat16),
-        in_specs=[pl.BlockSpec(memory_space=pltpu.SMEM), here, here, here],
+        in_specs=[here, here, here, here, pl.BlockSpec(memory_space=pl.ANY)],
         out_specs=here,
         scratch_shapes=[
             pltpu.VMEM((rows * group, hidden), jnp.float32),
             pltpu.VMEM((window_len * step, rows), jnp.float32),
             pltpu.VMEM((window_len * step, cols), jnp.float32),
             pltpu.VMEM((cols * group, hidden), jnp.float32),
+            pltpu.VMEM(cot_turned.shape, cot_turned.dtype),
+            pltpu.SemaphoreType.DMA,
         ],
         name="right_parts",
-    )(place, near, far, cot_turned)
+    )(*pieces, cot_turned)
 
 
 def all_steps(
@@ -221,11 +237,7 @@
     block_count, own_rows, col_tokens, channels = tri_cotangent.shape
     window_len = saved_left.shape[2]
     cols = lax.axis_size("col")
-    half = cols // 2
     rows = lax.axis_size("row")
-    col, row = lax.axis_index("col"), lax.axis_index("row")
-    core, x_low = lax.rem(col, 2), lax.rem(lax.div(col, 2), 2)
-    x_high = lax.div(row, rows // 2)
     lines_y = [[x * (rows // 2) + y for y in range(rows // 2)] for x in range(2)]
     lines_z = [[z * 4 + k for z in range(cols // 4)] for k in range(4)]
     one_core = [[c for c in range(cols) if c % 2 == k] for k in range(2)]
@@ -239,20 +251,20 @@
             tri_cotangent.reshape(block_count * own_rows, col_tokens, channels), (2, 1, 0)
         )
     )
-    place = jnp.stack([x_high, core])
-    left_pair = with_other(saved_left[0], exchanged(saved_left[0], "col", 2), x_low, 0)
-    near = jnp.broadcast_to(left_pair[None], (cols // 4, *left_pair.shape))
-    near = lax.all_to_all(near, "col", 0, 0, tiled=True, axis_index_groups=lines_z)
-    near = near.reshape(half, own_rows * window_len, channels)
+    own = jnp.broadcast_to(saved_left, (cols // 4, *saved_left.shape[1:]))
+    own = lax.all_to_all(own, "col", 0, 0, tiled=True, axis_index_groups=lines_z)
+    own = own.reshape(cols // 4, own_rows * window_len, channels)
     flat = (-1, channels)
     kept, away = left_parts(
-        place, right_near.reshape(flat), right_far.reshape(flat), cot_turned, cols, window_len
+        right_near.reshape(flat), right_far.reshape(flat), cot_turned, cols, window_len
     )
     came = exchanged(away, "col", 1)
     chip_part = (kept.astype(jnp.float32) + came.astype(jnp.float32)).astype(jnp.bfloat16)
     left_arrived = lax.all_to_all(chip_part, "col", 0, 0, tiled=True, axis_index_groups=one_core)
-    far = exchanged(near, "col", 1)
-    right_part = right_parts(place, near, far, cot_turned, window_len)
+    across = exchanged(own, "col", 2)
+    own_pair = exchanged(own, "col", 1)
+    across_pair = exchanged(across, "col", 1)
+    right_part = right_parts((own, across, own_pair, across_pair), cot_turned, window_len)
     right_part = right_part.reshape(col_tokens, window_len, channels)
     left_grad = left_arrived.astype(jnp.float32).sum(axis=0)
     right_grad = sent_and_summed(right_part, "row", 0)

time: 147 us -> 152 us (1.034)
  blocking collectives: 47.4 us -> 69.4 us
  waiting for transfers between devices: 27.5 us -> 17.2 us
  starting transfers between devices: 44.4 us -> 37.3 us
    all_to_all x0 -> x1, blocking collectives: none -> 21.1 us  [all_steps(): lax.all_to_all(own, 'col', 0, 0, tiled=True, axis_index_groups=lines_z)]
    all_to_all x1 -> x0, starting transfers between devices: 10 us -> none  [all_steps(): lax.all_to_all(near, 'col', 0, 0, tiled=True, axis_index_groups=lines_z)]
    all_to_all x1, waiting for transfers between devices: 12.8 us -> 2.89 us  [sent_and_summed(): lax.all_to_all(parts, axis, split_axis=0, concat_axis=0, tiled=True)]
    all_to_all x1, waiting for transfers between devices: 5.34 us -> 12.7 us  [all_steps(): lax.all_to_all(chip_part, 'col', 0, 0, tiled=True, axis_index_groups=one_...]
    all_to_all x1, waiting for transfers between devices: 6.3 us -> 0.01 us  [all_steps(): lax.all_to_all(right_near, 'row', 0, 0, tiled=True, axis_index_groups=lin...]
    ppermute x4 -> x5, starting transfers between devices: 16.2 us -> 19.9 us  [exchanged(): return lax.ppermute(x, axis, [(d, d ^ step) for d in range(devices)])]
    all_to_all x1, starting transfers between devices: 7.05 us -> 3.57 us  [all_steps(): lax.all_to_all(chip_part, 'col', 0, 0, tiled=True, axis_index_groups=one_...]
    all_to_all x1, starting transfers between devices: 3.57 us -> 7.04 us  [sent_and_summed(): lax.all_to_all(parts, axis, split_axis=0, concat_axis=0, tiled=True)]
  transfers between devices with their start and end apart: 8 -> 8, of which waited for: 5 -> 3; matrix products, arithmetic and copies ran while one was open for 6% -> 5% of each run, Pallas kernels for 7% -> 7%
where the time goes in v6:
time: 152 us; the launch traced here: 151 us
  blocking collectives  69.4 us (46%)
  starting transfers between devices  37.3 us (25%)
  waiting for transfers between devices  17.2 us (11%)
  Pallas kernels  11 us (7%)
  local copies, waits for them, and re-layouts  9.57 us (6%)
  other arithmetic  4.8 us (3%)
    all_to_all x2, blocking collectives, sent_to_all(): lax.all_to_all(jnp.broadcast_to(x[None], (devices, *x.shape)), axis, 0, 0...  29.9 us
    all_to_all x1, blocking collectives, all_steps(): lax.all_to_all(own, 'col', 0, 0, tiled=True, axis_index_groups=lines_z)  21.1 us
    ppermute x5, starting transfers between devices, exchanged(): return lax.ppermute(x, axis, [(d, d ^ step) for d in range(devices)])  19.9 us
    all_to_all x1, blocking collectives, summed_over_all(): arrived = lax.all_to_all(packed, 'col', 0, 0, tiled=True)  18.3 us
    all_to_all x1, waiting for transfers between devices, all_steps(): lax.all_to_all(chip_part, 'col', 0, 0, tiled=True, axis_index_groups=one_...  12.7 us
    all_to_all x1, starting transfers between devices, sent_and_summed(): lax.all_to_all(parts, axis, split_axis=0, concat_axis=0, tiled=True)  7.04 us
    all_to_all x1, starting transfers between devices, all_steps(): lax.all_to_all(right_near, 'row', 0, 0, tiled=True, axis_index_groups=lin...  6.82 us
    pallas_call x1, Pallas kernels, right_parts(): pl.pallas_call(functools.partial(right_kernel, window_len), out_shape=jax...  5.63 us
  transfers between devices with their start and end apart: 8, of which 3 were waited for; matrix products, arithmetic and copies ran while one was open for 5% of the time, Pallas kernels for 7%

profile of v6, /device:TPU:1, one launch (start us, length us, event | category | flops | bytes accessed | tf_op | source)
XLA Modules:
  0.0 150.8 jit_solution(9472153764402956326)
XLA Ops:
  0.6 0.8 broadcast_in_dim.19
  1.4 21.1 %all_to_all.35 = bf16[8,4,32,128]{3,2,1,0:T(8,128)(2,1)S(1)} all-to-all(bf16[8,4,32,128]{3,2,1,0:T(8,128)(2,1)S(1)} %broadcast_in_dim.19), channel_id=1, replica_groups={{0,4,8,12,16,20,24,28},{1,5,9,13,17,21,25,29},{2,6,10,14,18,22,26,30},{..., dimensions={0} | all-to-all | bytes 524288 | tf_op jit(solution)/shard_map/all_to_all | solution.py:255
  22.6 1.5 broadcast_in_dim.17
  24.1 6.8 %all-to-all-start = ((bf16[8,4,32,128]{3,2,1,0:T(8,128)(2,1)}), bf16[8,4,32,128]{3,2,1,0:T(8,128)(2,1)S(1)}, u32[]{:S(2)}, u32[]{:S(2)}) async-start(bf16[8,4,32,128]{3,2,1,0:T(8,128)(2,1)} %broadcast_in_dim.17), calls=%async_computation | async-start | bytes 524288 | tf_op jit(solution)/shard_map/all_to_all | solution.py:245
  30.9 3.1 %collective-permute-start.2 = (bf16[8,128,128]{2,1,0:T(8,128)(2,1)S(1)}, bf16[8,128,128]{2,1,0:T(8,128)(2,1)S(1)}, u32[]{:S(2)}, u32[]{:S(2)}) collective-permute-start(bf16[8,128,128]{2,1,0:T(8,128)(2,1)S(1)} %bitcast.51), channel_id=1, source_target_pairs={{0,2},{1,3},{2,0},{3,1},{4,6},{5,7},{6,4},{7,5},{8,10},{9,11},{10,... | collective-permute-start | bytes 786440 | tf_op jit(solution)/shard_map/ppermute | solution.py:90
  34.0 4.8 %collective-permute-start.3 = (bf16[8,128,128]{2,1,0:T(8,128)(2,1)S(1)}, bf16[8,128,128]{2,1,0:T(8,128)(2,1)S(1)}, u32[]{:S(2)}, u32[]{:S(2)}) collective-permute-start(bf16[8,128,128]{2,1,0:T(8,128)(2,1)S(1)} %bitcast.52), channel_id=1, source_target_pairs={{0,1},{1,0},{2,3},{3,2},{4,5},{5,4},{6,7},{7,6},{8,9},{9,8},{10,11... | collective-permute-start | bytes 786440 | tf_op jit(solution)/shard_map/ppermute | solution.py:90
  38.8 0.0 collective-permute-done.2.x_ref
  38.9 4.8 %collective-permute-start.4 = (bf16[8,128,128]{2,1,0:T(8,128)(2,1)S(1)}, bf16[8,128,128]{2,1,0:T(8,128)(2,1)S(1)}, u32[]{:S(2)}, u32[]{:S(2)}) collective-permute-start(bf16[8,128,128]{2,1,0:T(8,128)(2,1)S(1)} %collective-permute-done.2.x_ref), channel_id=1, source_target_pairs={{0,1},{1,0},{2,3},{3,2},{4,5},{5,4},{6,7},{7,6},{8,9},{9,8},{10,11... | collective-permute-start | bytes 786440 | tf_op jit(solution)/shard_map/ppermute | solution.py:90
  43.7 0.0 all-to-all-done
  43.7 0.0 copy-start.1
  43.7 4.7 %collective-permute-start = (bf16[8,4,32,128]{3,2,1,0:T(8,128)(2,1)S(1)}, bf16[8,4,32,128]{3,2,1,0:T(8,128)(2,1)S(1)}, u32[]{:S(2)}, u32[]{:S(2)}) collective-permute-start(bf16[8,4,32,128]{3,2,1,0:T(8,128)(2,1)S(1)} %all-to-all-done), channel_id=1, source_target_pairs={{0,256},{32,288},{64,320},{96,352},{128,384},{160,416},{192,448},{... | collective-permute-start | bytes 786440 | tf_op jit(solution)/shard_map/ppermute | solution.py:90
  48.4 4.6 %copy.17 = bf16[128,64,128]{0,1,2:T(8,128)(2,1)} copy(bf16[128,64,128]{2,1,0:T(8,128)(2,1)} %bitcast.50) | data formatting | bytes 4194304 | tf_op jit(solution)/shard_map/reshape | solution.py:251
  53.0 0.7 copy-done.4
  53.7 0.7 copy-done.5
  54.4 5.6 %right_parts.1 = bf16[2048,128]{1,0:T(8,128)(2,1)} custom-call(bf16[8,128,128]{2,1,0:T(8,128)(2,1)} %bitcast.53, bf16[8,128,128]{2,1,0:T(8,128)(2,1)} %copy-done.3, bf16[8,128,128]{2,1,0:T(8,128)(2,1)} %copy-done.4, bf16[8,128,128]{2,1,0:T(8,128)(2,1)} %copy-done.5, bf16[128,64,128]{2,1,0:T(8,128)(2,1)} %bitcast.47), custom_call_target="tpu_custom_call" | custom-call | tf_op jit(solution)/shard_map/right_parts/pallas_call | solution.py:217
  60.0 0.0 copy-start.2
  60.1 7.0 %all-to-all-start.3 = ((bf16[16,4,32,128]{3,2,1,0:T(8,128)(2,1)}), bf16[16,4,32,128]{3,2,1,0:T(8,128)(2,1)S(1)}, u32[]{:S(2)}, u32[]{:S(2)}) async-start(bf16[16,4,32,128]{3,2,1,0:T(8,128)(2,1)} %bitcast.49), calls=%async_computation.3 | async-start | bytes 1048576 | tf_op jit(solution)/shard_map/all_to_all | solution.py:24
  67.1 0.7 copy-done.6
  67.8 5.3 %left_parts.1 = (bf16[16,128,128]{2,1,0:T(8,128)(2,1)}, bf16[16,128,128]{2,1,0:T(8,128)(2,1)}) custom-call(bf16[1024,128]{1,0:T(8,128)(2,1)} %bitcast.54, bf16[1024,128]{1,0:T(8,128)(2,1)} %bitcast.62, bf16[128,64,128]{2,1,0:T(8,128)(2,1)} %bitcast.48), custom_call_target="tpu_custom_call" | custom-call | tf_op jit(solution)/shard_map/left_parts/pallas_call | solution.py:156
  73.2 0.0 copy-start.8
  73.2 0.0 copy-start.9
  73.2 2.5 %collective-permute-start.1 = (bf16[16,128,128]{2,1,0:T(8,128)(2,1)}, bf16[16,128,128]{2,1,0:T(8,128)(2,1)S(1)}, u32[]{:S(2)}, u32[]{:S(2)}) collective-permute-start(bf16[16,128,128]{2,1,0:T(8,128)(2,1)} %get-tuple-element.11), channel_id=1, source_target_pairs={{0,1},{1,0},{2,3},{3,2},{4,5},{5,4},{6,7},{7,6},{8,9},{9,8},{10,11... | collective-permute-start | bytes 1572872 | tf_op jit(solution)/shard_map/ppermute | solution.py:90
  75.7 0.1 convert_reduce_fusion.3
  75.8 1.6 %collective-permute-done.1 = bf16[16,128,128]{2,1,0:T(8,128)(2,1)S(1)} collective-permute-done((bf16[16,128,128]{2,1,0:T(8,128)(2,1)}, bf16[16,128,128]{2,1,0:T(8,128)(2,1)S(1)}, u32[]{:S(2)}, u32[]{:S(2)}) %collective-permute-start.1) | collective-permute-done | bytes 524320 | tf_op jit(solution)/shard_map/ppermute | solution.py:90
  77.4 2.0 %add_convert_fusion = bf16[16,128,128]{2,1,0:T(8,128)(2,1)} fusion(bf16[16,128,128]{2,1,0:T(8,128)(2,1)S(1)} %collective-permute-done.1, bf16[16,128,128]{2,1,0:T(8,128)(2,1)} %get-tuple-element.10), kind=kLoop, calls=%fused_computation.3 | loop fusion | flops 1048576 | bytes 1572864 | tf_op jit(solution)/shard_map/convert_element_type | solution.py:262
  79.4 2.9 %all-to-all-done.3 = bf16[16,4,32,128]{3,2,1,0:T(8,128)(2,1)S(1)} async-done(((bf16[16,4,32,128]{3,2,1,0:T(8,128)(2,1)}), bf16[16,4,32,128]{3,2,1,0:T(8,128)(2,1)S(1)}, u32[]{:S(2)}, u32[]{:S(2)}) %all-to-all-start.3) | async-done | bytes 524320 | tf_op jit(solution)/shard_map/all_to_all | solution.py:24
  82.3 3.6 %all-to-all-start.1 = ((bf16[16,128,128]{2,1,0:T(8,128)(2,1)}), bf16[16,128,128]{2,1,0:T(8,128)(2,1)S(1)}, u32[]{:S(2)}, u32[]{:S(2)}) async-start(bf16[16,128,128]{2,1,0:T(8,128)(2,1)} %add_convert_fusion), calls=%async_computation.1 | async-start | bytes 1048576 | tf_op jit(solution)/shard_map/all_to_all | solution.py:263
  85.9 0.1 copy.18
  86.0 0.1 div.25
  86.1 0.2 multiply_reduce_fusion.2
  86.3 0.1 rsqrt.13
  86.4 0.1 pad.4.clone
  86.4 0.1 add_convert_fusion.1
  86.6 0.2 fusion.18
  86.7 0.1 convert_reduce_fusion
  86.8 12.7 %all-to-all-done.1 = bf16[16,128,128]{2,1,0:T(8,128)(2,1)S(1)} async-done(((bf16[16,128,128]{2,1,0:T(8,128)(2,1)}), bf16[16,128,128]{2,1,0:T(8,128)(2,1)S(1)}, u32[]{:S(2)}, u32[]{:S(2)}) %all-to-all-start.1) | async-done | bytes 524320 | tf_op jit(solution)/shard_map/all_to_all | solution.py:263
  99.5 0.1 convert_reduce_fusion.1
  99.6 0.1 fusion.11
  99.7 0.1 copy.23
  99.8 0.3 multiply_reduce_fusion
  100.1 0.2 convolution_bitcast_fusion
  100.3 0.8 multiply_convert_fusion
  101.1 0.1 maximum_maximum_fusion
  101.2 18.3 %all_to_all.36 = bf16[32,24,128]{2,1,0:T(8,128)(2,1)S(1)} all-to-all(bf16[32,24,128]{2,1,0:T(8,128)(2,1)S(1)} %pad_maximum_fusion), channel_id=1, replica_groups=mesh['row'=16,'col'=32] {'col'}, dimensions={0} | all-to-all | bytes 393216 | tf_op jit(solution)/shard_map/all_to_all | solution.py:79
  119.5 15.4 %all_to_all.37 = f32[16,24,128]{2,1,0:T(8,128)S(1)} all-to-all(f32[16,24,128]{2,1,0:T(8,128)S(1)} %broadcast_in_dim.22), channel_id=1, replica_groups=mesh['row'=16,'col'=32] {'row'}, dimensions={0} | all-to-all | bytes 393216 | tf_op jit(solution)/shard_map/all_to_all | solution.py:13
  134.9 0.6 slice_add_fusion
  135.5 14.5 %all_to_all.38 = bf16[32,16,128]{2,1,0:T(8,128)(2,1)S(1)} all-to-all(bf16[32,16,128]{2,1,0:T(8,128)(2,1)S(1)} %broadcast_in_dim.23), channel_id=1, replica_groups=mesh['row'=16,'col'=32] {'col'}, dimensions={0} | all-to-all | bytes 262144 | tf_op jit(solution)/shard_map/all_to_all | solution.py:13
  150.1 0.7 bitcast_convert_fusion
  (30 shorter events, 0.2 us)
Async XLA Ops:
  22.6 30.4 %copy-start = (bf16[8,4,32,128]{3,2,1,0:T(8,128)(2,1)}, bf16[8,4,32,128]{3,2,1,0:T(8,128)(2,1)S(1)}, u32[]{:S(2)}) copy-start(bf16[8,4,32,128]{3,2,1,0:T(8,128)(2,1)S(1)} %all_to_all.35) | copy-start | bytes 786436
  24.1 19.6 %all-to-all-start = ((bf16[8,4,32,128]{3,2,1,0:T(8,128)(2,1)}), bf16[8,4,32,128]{3,2,1,0:T(8,128)(2,1)S(1)}, u32[]{:S(2)}, u32[]{:S(2)}) async-start(bf16[8,4,32,128]{3,2,1,0:T(8,128)(2,1)} %broadcast_in_dim.17), calls=%async_computation | async-start | bytes 524288 | tf_op jit(solution)/shard_map/all_to_all | solution.py:245
  30.9 7.9 %collective-permute-start.2 = (bf16[8,128,128]{2,1,0:T(8,128)(2,1)S(1)}, bf16[8,128,128]{2,1,0:T(8,128)(2,1)S(1)}, u32[]{:S(2)}, u32[]{:S(2)}) collective-permute-start(bf16[8,128,128]{2,1,0:T(8,128)(2,1)S(1)} %bitcast.51), channel_id=1, source_target_pairs={{0,2},{1,3},{2,0},{3,1},{4,6},{5,7},{6,4},{7,5},{8,10},{9,11},{10,... | collective-permute-start | bytes 786440 | tf_op jit(solution)/shard_map/ppermute | solution.py:90
  34.0 18.9 %collective-permute-start.3 = (bf16[8,128,128]{2,1,0:T(8,128)(2,1)S(1)}, bf16[8,128,128]{2,1,0:T(8,128)(2,1)S(1)}, u32[]{:S(2)}, u32[]{:S(2)}) collective-permute-start(bf16[8,128,128]{2,1,0:T(8,128)(2,1)S(1)} %bitcast.52), channel_id=1, source_target_pairs={{0,1},{1,0},{2,3},{3,2},{4,5},{5,4},{6,7},{7,6},{8,9},{9,8},{10,11... | collective-permute-start | bytes 786440 | tf_op jit(solution)/shard_map/ppermute | solution.py:90
  38.8 14.1 %copy-start.3 = (bf16[8,128,128]{2,1,0:T(8,128)(2,1)}, bf16[8,128,128]{2,1,0:T(8,128)(2,1)S(1)}, u32[]{:S(2)}) copy-start(bf16[8,128,128]{2,1,0:T(8,128)(2,1)S(1)} %collective-permute-done.2.x_ref) | copy-start | bytes 786436
  38.9 14.1 %collective-permute-start.4 = (bf16[8,128,128]{2,1,0:T(8,128)(2,1)S(1)}, bf16[8,128,128]{2,1,0:T(8,128)(2,1)S(1)}, u32[]{:S(2)}, u32[]{:S(2)}) collective-permute-start(bf16[8,128,128]{2,1,0:T(8,128)(2,1)S(1)} %collective-permute-done.2.x_ref), channel_id=1, source_target_pairs={{0,1},{1,0},{2,3},{3,2},{4,5},{5,4},{6,7},{7,6},{8,9},{9,8},{10,11... | collective-permute-start | bytes 786440 | tf_op jit(solution)/shard_map/ppermute | solution.py:90
  43.7 9.3 %copy-start.1 = (bf16[8,4,32,128]{3,2,1,0:T(8,128)(2,1)}, bf16[8,4,32,128]{3,2,1,0:T(8,128)(2,1)S(1)}, u32[]{:S(2)}) copy-start(bf16[8,4,32,128]{3,2,1,0:T(8,128)(2,1)S(1)} %all-to-all-done) | copy-start | bytes 786436
  43.7 23.4 %collective-permute-start = (bf16[8,4,32,128]{3,2,1,0:T(8,128)(2,1)S(1)}, bf16[8,4,32,128]{3,2,1,0:T(8,128)(2,1)S(1)}, u32[]{:S(2)}, u32[]{:S(2)}) collective-permute-start(bf16[8,4,32,128]{3,2,1,0:T(8,128)(2,1)S(1)} %all-to-all-done), channel_id=1, source_target_pairs={{0,256},{32,288},{64,320},{96,352},{128,384},{160,416},{192,448},{... | collective-permute-start | bytes 786440 | tf_op jit(solution)/shard_map/ppermute | solution.py:90
  53.0 0.7 copy-start.4
  53.7 0.7 copy-start.5
  60.0 15.6 %copy-start.2 = (bf16[1,4,32,128]{3,2,1,0:T(8,128)(2,1)S(1)}, bf16[1,4,32,128]{3,2,1,0:T(8,128)(2,1)}, u32[]{:S(2)}) copy-start(bf16[1,4,32,128]{3,2,1,0:T(8,128)(2,1)} %param.7) | copy-start | bytes 98308
  60.1 22.2 %all-to-all-start.3 = ((bf16[16,4,32,128]{3,2,1,0:T(8,128)(2,1)}), bf16[16,4,32,128]{3,2,1,0:T(8,128)(2,1)S(1)}, u32[]{:S(2)}, u32[]{:S(2)}) async-start(bf16[16,4,32,128]{3,2,1,0:T(8,128)(2,1)} %bitcast.49), calls=%async_computation.3 | async-start | bytes 1048576 | tf_op jit(solution)/shard_map/all_to_all | solution.py:24
  67.1 0.7 copy-start.6
  67.8 18.0 %copy-start.7 = (bf16[4,128,128]{2,1,0:T(8,128)(2,1)S(1)}, bf16[4,128,128]{2,1,0:T(8,128)(2,1)}, u32[]{:S(2)}) copy-start(bf16[4,128,128]{2,1,0:T(8,128)(2,1)} %param.13) | copy-start | bytes 393220
  73.2 13.3 %copy-start.8 = (f32[128]{0:T(128)S(1)}, f32[128]{0:T(128)}, u32[]{:S(2)}) copy-start(f32[128]{0:T(128)} %param.11) | copy-start | bytes 1540
  73.2 13.2 %copy-start.9 = (f32[128]{0:T(128)S(1)}, f32[128]{0:T(128)}, u32[]{:S(2)}) copy-start(f32[128]{0:T(128)} %param.12) | copy-start | bytes 1540
  73.2 4.2 %collective-permute-start.1 = (bf16[16,128,128]{2,1,0:T(8,128)(2,1)}, bf16[16,128,128]{2,1,0:T(8,128)(2,1)S(1)}, u32[]{:S(2)}, u32[]{:S(2)}) collective-permute-start(bf16[16,128,128]{2,1,0:T(8,128)(2,1)} %get-tuple-element.11), channel_id=1, source_target_pairs={{0,1},{1,0},{2,3},{3,2},{4,5},{5,4},{6,7},{7,6},{8,9},{9,8},{10,11... | collective-permute-start | bytes 1572872 | tf_op jit(solution)/shard_map/ppermute | solution.py:90
  82.3 17.2 %all-to-all-start.1 = ((bf16[16,128,128]{2,1,0:T(8,128)(2,1)}), bf16[16,128,128]{2,1,0:T(8,128)(2,1)S(1)}, u32[]{:S(2)}, u32[]{:S(2)}) async-start(bf16[16,128,128]{2,1,0:T(8,128)(2,1)} %add_convert_fusion), calls=%async_computation.1 | async-start | bytes 1048576 | tf_op jit(solution)/shard_map/all_to_all | solution.py:263

commit v7 on v6

--- a/solution.py
+++ b/solution.py
@@ -91,6 +91,7 @@
 
 
 PAD = 8
+VMEM_LIMIT = 24 * 2**20
 ROWS_TURNED = (((1,), (1,)), ((), ()))
 
 
@@ -111,10 +112,8 @@
     return lax.div(row, half), lax.rem(lax.div(col, 2), 2), lax.rem(col, 2)
 
 
-def left_kernel(window_len, near_ref, far_ref, cot_hbm, kept_ref, away_ref, *scratch):
-    wide, by_key, product, rows_out, cot_ref, arrived = scratch
-    fetch = pltpu.make_async_copy(cot_hbm, cot_ref, arrived)
-    fetch.start()
+def left_kernel(window_len, near_ref, far_ref, cot_ref, kept_ref, away_ref, *scratch):
+    wide, by_key, product, rows_out = scratch
     hidden, cols, rows = cot_ref.shape
     x_high, _, core = place_of()
     group, step = window_len + PAD, hidden + PAD
@@ -128,7 +127,6 @@
         by_key[pl.ds(k * step, hidden), :] = turned(
             wide[pl.ds(k, cols, stride=group), :].astype(jnp.bfloat16)
         )
-    fetch.wait()
     for h in range(hidden):
         keys = by_key[pl.ds(h, window_len, stride=step), :].astype(jnp.bfloat16)
         product[pl.ds(h, window_len, stride=step), :] = jnp.dot(
@@ -156,24 +154,21 @@
     return pl.pallas_call(
         functools.partial(left_kernel, window_len),
         out_shape=(out, out),
-        in_specs=[here, here, pl.BlockSpec(memory_space=pl.ANY)],
+        in_specs=[here, here, here],
         out_specs=(here, here),
         scratch_shapes=[
             pltpu.VMEM((cols * group, hidden), jnp.float32),
             pltpu.VMEM((window_len * step, cols), jnp.float32),
             pltpu.VMEM((window_len * step, rows), jnp.float32),
             pltpu.VMEM((rows * group, hidden), jnp.float32),
-            pltpu.VMEM(cot_turned.shape, cot_turned.dtype),
-            pltpu.SemaphoreType.DMA,
         ],
+        compiler_params=pltpu.CompilerParams(vmem_limit_bytes=VMEM_LIMIT),
         name="left_parts",
     )(near, far, cot_turned)
 
 
-def right_kernel(window_len, own_ref, x_ref, core_ref, both_ref, cot_hbm, out_ref, *scratch):
-    wide, by_key, product, rows_out, cot_ref, arrived = scratch
-    fetch = pltpu.make_async_copy(cot_hbm, cot_ref, arrived)
-    fetch.start()
+def right_kernel(window_len, own_ref, x_ref, core_ref, both_ref, cot_ref, out_ref, *scratch):
+    wide, by_key, product, rows_out = scratch
     hidden, cols, rows = cot_ref.shape
     _, x_low, core = place_of()
     group, step = window_len + PAD, hidden + PAD
@@ -194,7 +189,6 @@
         by_key[pl.ds(k * step, hidden), :] = turned(
             wide[pl.ds(k, rows, stride=group), :].astype(jnp.bfloat16)
         )
-    fetch.wait()
     for h in range(hidden):
         keys = by_key[pl.ds(h, window_len, stride=step), :].astype(jnp.bfloat16)
         product[pl.ds(h, window_len, stride=step), :] = lax.dot_general(
@@ -217,16 +211,15 @@
     return pl.pallas_call(
         functools.partial(right_kernel, window_len),
         out_shape=jax.ShapeDtypeStruct((cols * window_len, hidden), jnp.bfloat16),
-        in_specs=[here, here, here, here, pl.BlockSpec(memory_space=pl.ANY)],
+        in_specs=[here, here, here, here, here],
         out_specs=here,
         scratch_shapes=[
             pltpu.VMEM((rows * group, hidden), jnp.float32),
             pltpu.VMEM((window_len * step, rows), jnp.float32),
             pltpu.VMEM((window_len * step, cols), jnp.float32),
             pltpu.VMEM((cols * group, hidden), jnp.float32),
-            pltpu.VMEM(cot_turned.shape, cot_turned.dtype),
-            pltpu.SemaphoreType.DMA,
         ],
+        compiler_params=pltpu.CompilerParams(vmem_limit_bytes=VMEM_LIMIT),
         name="right_parts",
     )(*pieces, cot_turned)
 

time: 152 us -> 148 us (0.974)
  Pallas kernels: 11 us -> 7.05 us
  waiting for transfers between devices: 17.2 us -> 21.1 us
  local copies, waits for them, and re-layouts: 9.57 us -> 6.71 us
    all_to_all x1, waiting for transfers between devices: 2.89 us -> 6.99 us  [sent_and_summed(): lax.all_to_all(parts, axis, split_axis=0, concat_axis=0, tiled=True)]
    pallas_call x1, Pallas kernels: 5.34 us -> 3.14 us  [left_parts(): pl.pallas_call(functools.partial(left_kernel, window_len), out_shape=(out...]
    unnamed x21 -> x9, local copies, waits for them, and re-layouts: 2.27 us -> 0.15 us
    pallas_call x1, Pallas kernels: 5.63 us -> 3.91 us  [right_parts(): pl.pallas_call(functools.partial(right_kernel, window_len), out_shape=jax...]
  transfers between devices with their start and end apart: 8 -> 8, of which waited for: 3 -> 3; matrix products, arithmetic and copies ran while one was open for 5% -> 4% of each run, Pallas kernels for 7% -> 5%
where the time goes in v7:
time: 148 us; the launch traced here: 147 us
  blocking collectives  69.4 us (47%)
  starting transfers between devices  37.4 us (25%)
  waiting for transfers between devices  21.1 us (14%)
  Pallas kernels  7.05 us (5%)
  local copies, waits for them, and re-layouts  6.71 us (5%)
  other arithmetic  3.78 us (3%)
    all_to_all x2, blocking collectives, sent_to_all(): lax.all_to_all(jnp.broadcast_to(x[None], (devices, *x.shape)), axis, 0, 0...  29.9 us
    all_to_all x1, blocking collectives, all_steps(): lax.all_to_all(own, 'col', 0, 0, tiled=True, axis_index_groups=lines_z)  21.1 us
    ppermute x5, starting transfers between devices, exchanged(): return lax.ppermute(x, axis, [(d, d ^ step) for d in range(devices)])  19.9 us
    all_to_all x1, blocking collectives, summed_over_all(): arrived = lax.all_to_all(packed, 'col', 0, 0, tiled=True)  18.3 us
    all_to_all x1, waiting for transfers between devices, all_steps(): lax.all_to_all(chip_part, 'col', 0, 0, tiled=True, axis_index_groups=one_...  12.6 us
    all_to_all x1, starting transfers between devices, sent_and_summed(): lax.all_to_all(parts, axis, split_axis=0, concat_axis=0, tiled=True)  7.16 us
    all_to_all x1, waiting for transfers between devices, sent_and_summed(): lax.all_to_all(parts, axis, split_axis=0, concat_axis=0, tiled=True)  6.99 us
    all_to_all x1, starting transfers between devices, all_steps(): lax.all_to_all(right_near, 'row', 0, 0, tiled=True, axis_index_groups=lin...  6.82 us
  transfers between devices with their start and end apart: 8, of which 3 were waited for; matrix products, arithmetic and copies ran while one was open for 4% of the time, Pallas kernels for 5%

profile of v7, /device:TPU:1, one launch (start us, length us, event | category | flops | bytes accessed | tf_op | source)
XLA Modules:
  0.0 147.0 jit_solution(13992796630411587486)
XLA Ops:
  0.6 0.8 broadcast_in_dim.19
  1.4 21.1 %all_to_all.35 = bf16[8,4,32,128]{3,2,1,0:T(8,128)(2,1)S(1)} all-to-all(bf16[8,4,32,128]{3,2,1,0:T(8,128)(2,1)S(1)} %broadcast_in_dim.19), channel_id=1, replica_groups={{0,4,8,12,16,20,24,28},{1,5,9,13,17,21,25,29},{2,6,10,14,18,22,26,30},{..., dimensions={0} | all-to-all | bytes 524288 | tf_op jit(solution)/shard_map/all_to_all | solution.py:248
  22.6 1.5 %broadcast_in_dim.17 = bf16[8,4,32,128]{3,2,1,0:T(8,128)(2,1)} broadcast(bf16[4,32,128]{2,1,0:T(8,128)(2,1)} %bitcast.62), dimensions={1,2,3} | broadcast | bytes 294912 | tf_op jit(solution)/shard_map/broadcast_in_dim | solution.py:237
  24.1 6.8 %all-to-all-start = ((bf16[8,4,32,128]{3,2,1,0:T(8,128)(2,1)}), bf16[8,4,32,128]{3,2,1,0:T(8,128)(2,1)S(1)}, u32[]{:S(2)}, u32[]{:S(2)}) async-start(bf16[8,4,32,128]{3,2,1,0:T(8,128)(2,1)} %broadcast_in_dim.17), calls=%async_computation | async-start | bytes 524288 | tf_op jit(solution)/shard_map/all_to_all | solution.py:238
  30.9 3.1 %collective-permute-start.2 = (bf16[8,128,128]{2,1,0:T(8,128)(2,1)S(1)}, bf16[8,128,128]{2,1,0:T(8,128)(2,1)S(1)}, u32[]{:S(2)}, u32[]{:S(2)}) collective-permute-start(bf16[8,128,128]{2,1,0:T(8,128)(2,1)S(1)} %bitcast.49), channel_id=1, source_target_pairs={{0,2},{1,3},{2,0},{3,1},{4,6},{5,7},{6,4},{7,5},{8,10},{9,11},{10,... | collective-permute-start | bytes 786440 | tf_op jit(solution)/shard_map/ppermute | solution.py:90
  34.0 4.8 %collective-permute-start.3 = (bf16[8,128,128]{2,1,0:T(8,128)(2,1)S(1)}, bf16[8,128,128]{2,1,0:T(8,128)(2,1)S(1)}, u32[]{:S(2)}, u32[]{:S(2)}) collective-permute-start(bf16[8,128,128]{2,1,0:T(8,128)(2,1)S(1)} %bitcast.50), channel_id=1, source_target_pairs={{0,1},{1,0},{2,3},{3,2},{4,5},{5,4},{6,7},{7,6},{8,9},{9,8},{10,11... | collective-permute-start | bytes 786440 | tf_op jit(solution)/shard_map/ppermute | solution.py:90
  38.8 0.0 collective-permute-done.2.x_ref
  38.8 4.8 %collective-permute-start.4 = (bf16[8,128,128]{2,1,0:T(8,128)(2,1)S(1)}, bf16[8,128,128]{2,1,0:T(8,128)(2,1)S(1)}, u32[]{:S(2)}, u32[]{:S(2)}) collective-permute-start(bf16[8,128,128]{2,1,0:T(8,128)(2,1)S(1)} %collective-permute-done.2.x_ref), channel_id=1, source_target_pairs={{0,1},{1,0},{2,3},{3,2},{4,5},{5,4},{6,7},{7,6},{8,9},{9,8},{10,11... | collective-permute-start | bytes 786440 | tf_op jit(solution)/shard_map/ppermute | solution.py:90
  43.7 0.0 all-to-all-done
  43.7 4.7 %collective-permute-start = (bf16[8,4,32,128]{3,2,1,0:T(8,128)(2,1)S(1)}, bf16[8,4,32,128]{3,2,1,0:T(8,128)(2,1)}, u32[]{:S(2)}, u32[]{:S(2)}) collective-permute-start(bf16[8,4,32,128]{3,2,1,0:T(8,128)(2,1)S(1)} %all-to-all-done), channel_id=1, source_target_pairs={{0,256},{32,288},{64,320},{96,352},{128,384},{160,416},{192,448},{... | collective-permute-start | bytes 786440 | tf_op jit(solution)/shard_map/ppermute | solution.py:90
  48.4 3.8 %copy.17 = bf16[128,64,128]{0,1,2:T(8,128)(2,1)S(1)} copy(bf16[128,64,128]{2,1,0:T(8,128)(2,1)} %bitcast.53) | data formatting | bytes 4194304 | tf_op jit(solution)/shard_map/reshape | solution.py:244
  52.2 0.0 collective-permute-done.3.core_ref
  52.2 0.0 collective-permute-done.4.both_ref
  52.2 3.9 %right_parts.1 = bf16[2048,128]{1,0:T(8,128)(2,1)} custom-call(bf16[8,128,128]{2,1,0:T(8,128)(2,1)S(1)} %bitcast.51, bf16[8,128,128]{2,1,0:T(8,128)(2,1)S(1)} %collective-permute-done.2.x_ref, bf16[8,128,128]{2,1,0:T(8,128)(2,1)S(1)} %collective-permute-done.3.core_ref, bf16[8,128,128]{2,1,0:T(8,128)(2,1)S(1)} %collective-permute-done.4.both_ref, ...), custom_call_target="tpu_custom_call" | custom-call | tf_op jit(solution)/shard_map/right_parts/pallas_call | solution.py:211
  56.1 7.2 %all-to-all-start.3 = ((bf16[16,4,32,128]{3,2,1,0:T(8,128)(2,1)}), bf16[16,4,32,128]{3,2,1,0:T(8,128)(2,1)S(1)}, u32[]{:S(2)}, u32[]{:S(2)}) async-start(bf16[16,4,32,128]{3,2,1,0:T(8,128)(2,1)} %bitcast.10), calls=%async_computation.3 | async-start | bytes 1048576 | tf_op jit(solution)/shard_map/all_to_all | solution.py:24
  63.3 0.0 collective-permute-done
  63.3 0.0 copy-start.1
  63.3 3.1 %left_parts.1 = (bf16[16,128,128]{2,1,0:T(8,128)(2,1)S(1)}, bf16[16,128,128]{2,1,0:T(8,128)(2,1)S(1)}) custom-call(bf16[1024,128]{1,0:T(8,128)(2,1)S(1)} %bitcast.52, bf16[1024,128]{1,0:T(8,128)(2,1)} %bitcast.2.far_ref, bf16[128,64,128]{2,1,0:T(8,128)(2,1)S(1)} %bitcast.48), custom_call_target="tpu_custom_call" | custom-call | tf_op jit(solution)/shard_map/left_parts/pallas_call | solution.py:154
  66.5 0.0 copy-start.2
  66.5 0.0 copy-start.3
  66.5 2.5 %collective-permute-start.1 = (bf16[16,128,128]{2,1,0:T(8,128)(2,1)S(1)}, bf16[16,128,128]{2,1,0:T(8,128)(2,1)S(1)}, u32[]{:S(2)}, u32[]{:S(2)}) collective-permute-start(bf16[16,128,128]{2,1,0:T(8,128)(2,1)S(1)} %get-tuple-element.11), channel_id=1, source_target_pairs={{0,1},{1,0},{2,3},{3,2},{4,5},{5,4},{6,7},{7,6},{8,9},{9,8},{10,11... | collective-permute-start | bytes 1572872 | tf_op jit(solution)/shard_map/ppermute | solution.py:90
  69.0 0.0 copy-done
  69.0 0.1 convert_reduce_fusion.3
  69.1 1.4 collective-permute-done.1
  70.5 1.0 add_convert_fusion
  71.5 7.0 %all-to-all-done.3 = bf16[16,4,32,128]{3,2,1,0:T(8,128)(2,1)S(1)} async-done(((bf16[16,4,32,128]{3,2,1,0:T(8,128)(2,1)}), bf16[16,4,32,128]{3,2,1,0:T(8,128)(2,1)S(1)}, u32[]{:S(2)}, u32[]{:S(2)}) %all-to-all-start.3) | async-done | bytes 524320 | tf_op jit(solution)/shard_map/all_to_all | solution.py:24
  78.4 3.6 %all-to-all-start.1 = ((bf16[16,128,128]{2,1,0:T(8,128)(2,1)}), bf16[16,128,128]{2,1,0:T(8,128)(2,1)S(1)}, u32[]{:S(2)}, u32[]{:S(2)}) async-start(bf16[16,128,128]{2,1,0:T(8,128)(2,1)} %add_convert_fusion), calls=%async_computation.1 | async-start | bytes 1048576 | tf_op jit(solution)/shard_map/all_to_all | solution.py:256
  82.0 0.1 copy.18
  82.2 0.1 div.25
  82.3 0.2 multiply_reduce_fusion.2
  82.4 0.1 rsqrt.13
  82.5 0.1 pad.4.clone
  82.6 0.1 add_convert_fusion.1
  82.7 0.2 fusion.18
  82.9 0.1 convert_reduce_fusion
  83.0 12.6 %all-to-all-done.1 = bf16[16,128,128]{2,1,0:T(8,128)(2,1)S(1)} async-done(((bf16[16,128,128]{2,1,0:T(8,128)(2,1)}), bf16[16,128,128]{2,1,0:T(8,128)(2,1)S(1)}, u32[]{:S(2)}, u32[]{:S(2)}) %all-to-all-start.1) | async-done | bytes 524320 | tf_op jit(solution)/shard_map/all_to_all | solution.py:256
  95.7 0.1 convert_reduce_fusion.1
  95.7 0.1 fusion.11
  95.8 0.1 copy.23
  96.0 0.3 multiply_reduce_fusion
  96.2 0.2 convolution_bitcast_fusion
  96.5 0.8 multiply_convert_fusion
  97.2 0.1 maximum_maximum_fusion
  97.3 18.3 %all_to_all.36 = bf16[32,24,128]{2,1,0:T(8,128)(2,1)S(1)} all-to-all(bf16[32,24,128]{2,1,0:T(8,128)(2,1)S(1)} %pad_maximum_fusion), channel_id=1, replica_groups=mesh['row'=16,'col'=32] {'col'}, dimensions={0} | all-to-all | bytes 393216 | tf_op jit(solution)/shard_map/all_to_all | solution.py:79
  115.7 15.4 %all_to_all.37 = f32[16,24,128]{2,1,0:T(8,128)S(1)} all-to-all(f32[16,24,128]{2,1,0:T(8,128)S(1)} %broadcast_in_dim.22), channel_id=1, replica_groups=mesh['row'=16,'col'=32] {'row'}, dimensions={0} | all-to-all | bytes 393216 | tf_op jit(solution)/shard_map/all_to_all | solution.py:13
  131.1 0.6 slice_add_fusion
  131.7 14.5 %all_to_all.38 = bf16[32,16,128]{2,1,0:T(8,128)(2,1)S(1)} all-to-all(bf16[32,16,128]{2,1,0:T(8,128)(2,1)S(1)} %broadcast_in_dim.23), channel_id=1, replica_groups=mesh['row'=16,'col'=32] {'col'}, dimensions={0} | all-to-all | bytes 262144 | tf_op jit(solution)/shard_map/all_to_all | solution.py:13
  146.2 0.7 bitcast_convert_fusion
  (18 shorter events, 0.2 us)
Async XLA Ops:
  24.1 19.6 %all-to-all-start = ((bf16[8,4,32,128]{3,2,1,0:T(8,128)(2,1)}), bf16[8,4,32,128]{3,2,1,0:T(8,128)(2,1)S(1)}, u32[]{:S(2)}, u32[]{:S(2)}) async-start(bf16[8,4,32,128]{3,2,1,0:T(8,128)(2,1)} %broadcast_in_dim.17), calls=%async_computation | async-start | bytes 524288 | tf_op jit(solution)/shard_map/all_to_all | solution.py:238
  30.9 7.9 %collective-permute-start.2 = (bf16[8,128,128]{2,1,0:T(8,128)(2,1)S(1)}, bf16[8,128,128]{2,1,0:T(8,128)(2,1)S(1)}, u32[]{:S(2)}, u32[]{:S(2)}) collective-permute-start(bf16[8,128,128]{2,1,0:T(8,128)(2,1)S(1)} %bitcast.49), channel_id=1, source_target_pairs={{0,2},{1,3},{2,0},{3,1},{4,6},{5,7},{6,4},{7,5},{8,10},{9,11},{10,... | collective-permute-start | bytes 786440 | tf_op jit(solution)/shard_map/ppermute | solution.py:90
  34.0 18.2 %collective-permute-start.3 = (bf16[8,128,128]{2,1,0:T(8,128)(2,1)S(1)}, bf16[8,128,128]{2,1,0:T(8,128)(2,1)S(1)}, u32[]{:S(2)}, u32[]{:S(2)}) collective-permute-start(bf16[8,128,128]{2,1,0:T(8,128)(2,1)S(1)} %bitcast.50), channel_id=1, source_target_pairs={{0,1},{1,0},{2,3},{3,2},{4,5},{5,4},{6,7},{7,6},{8,9},{9,8},{10,11... | collective-permute-start | bytes 786440 | tf_op jit(solution)/shard_map/ppermute | solution.py:90
  38.8 13.4 %collective-permute-start.4 = (bf16[8,128,128]{2,1,0:T(8,128)(2,1)S(1)}, bf16[8,128,128]{2,1,0:T(8,128)(2,1)S(1)}, u32[]{:S(2)}, u32[]{:S(2)}) collective-permute-start(bf16[8,128,128]{2,1,0:T(8,128)(2,1)S(1)} %collective-permute-done.2.x_ref), channel_id=1, source_target_pairs={{0,1},{1,0},{2,3},{3,2},{4,5},{5,4},{6,7},{7,6},{8,9},{9,8},{10,11... | collective-permute-start | bytes 786440 | tf_op jit(solution)/shard_map/ppermute | solution.py:90
  43.7 19.6 %collective-permute-start = (bf16[8,4,32,128]{3,2,1,0:T(8,128)(2,1)S(1)}, bf16[8,4,32,128]{3,2,1,0:T(8,128)(2,1)}, u32[]{:S(2)}, u32[]{:S(2)}) collective-permute-start(bf16[8,4,32,128]{3,2,1,0:T(8,128)(2,1)S(1)} %all-to-all-done), channel_id=1, source_target_pairs={{0,256},{32,288},{64,320},{96,352},{128,384},{160,416},{192,448},{... | collective-permute-start | bytes 786440 | tf_op jit(solution)/shard_map/ppermute | solution.py:90
  56.1 12.9 %copy-start = (bf16[1,4,32,128]{3,2,1,0:T(8,128)(2,1)S(1)}, bf16[1,4,32,128]{3,2,1,0:T(8,128)(2,1)}, u32[]{:S(2)}) copy-start(bf16[1,4,32,128]{3,2,1,0:T(8,128)(2,1)} %param.7) | copy-start | bytes 98308
  56.1 22.3 %all-to-all-start.3 = ((bf16[16,4,32,128]{3,2,1,0:T(8,128)(2,1)}), bf16[16,4,32,128]{3,2,1,0:T(8,128)(2,1)S(1)}, u32[]{:S(2)}, u32[]{:S(2)}) async-start(bf16[16,4,32,128]{3,2,1,0:T(8,128)(2,1)} %bitcast.10), calls=%async_computation.3 | async-start | bytes 1048576 | tf_op jit(solution)/shard_map/all_to_all | solution.py:24
  63.3 18.7 %copy-start.1 = (bf16[4,128,128]{2,1,0:T(8,128)(2,1)S(1)}, bf16[4,128,128]{2,1,0:T(8,128)(2,1)}, u32[]{:S(2)}) copy-start(bf16[4,128,128]{2,1,0:T(8,128)(2,1)} %param.13) | copy-start | bytes 393220
  66.5 16.1 %copy-start.2 = (f32[128]{0:T(128)S(1)}, f32[128]{0:T(128)}, u32[]{:S(2)}) copy-start(f32[128]{0:T(128)} %param.11) | copy-start | bytes 1540
  66.5 16.1 %copy-start.3 = (f32[128]{0:T(128)S(1)}, f32[128]{0:T(128)}, u32[]{:S(2)}) copy-start(f32[128]{0:T(128)} %param.12) | copy-start | bytes 1540
  66.5 4.0 %collective-permute-start.1 = (bf16[16,128,128]{2,1,0:T(8,128)(2,1)S(1)}, bf16[16,128,128]{2,1,0:T(8,128)(2,1)S(1)}, u32[]{:S(2)}, u32[]{:S(2)}) collective-permute-start(bf16[16,128,128]{2,1,0:T(8,128)(2,1)S(1)} %get-tuple-element.11), channel_id=1, source_target_pairs={{0,1},{1,0},{2,3},{3,2},{4,5},{5,4},{6,7},{7,6},{8,9},{9,8},{10,11... | collective-permute-start | bytes 1572872 | tf_op jit(solution)/shard_map/ppermute | solution.py:90
  78.4 17.2 %all-to-all-start.1 = ((bf16[16,128,128]{2,1,0:T(8,128)(2,1)}), bf16[16,128,128]{2,1,0:T(8,128)(2,1)S(1)}, u32[]{:S(2)}, u32[]{:S(2)}) async-start(bf16[16,128,128]{2,1,0:T(8,128)(2,1)} %add_convert_fusion), calls=%async_computation.1 | async-start | bytes 1048576 | tf_op jit(solution)/shard_map/all_to_all | solution.py:256

commit v8 on v7

--- a/solution.py
+++ b/solution.py
@@ -64,21 +64,27 @@
     return (pair_grad.astype(jnp.bfloat16), weight_part, norm_part)
 
 
+def with_split_norm(part, rows):
+    norm = part[rows : rows + 2] + part[rows + 2 : rows + 4]
+    return jnp.concatenate([part[:rows], split_in_two(norm)], axis=0).astype(jnp.bfloat16)
+
+
+def split_in_two(norm):
+    high = lax.reduce_precision(norm, 8, 7)
+    return jnp.concatenate([high, norm - high, jnp.zeros((4, norm.shape[1]), norm.dtype)], axis=0)
+
+
 def summed_over_all(weight_part, norm_part):
     cols = lax.axis_size("col")
     shape = weight_part.shape
     width = shape[-1]
     chunks = weight_part.reshape(cols, -1, width).astype(jnp.bfloat16)
     rows = chunks.shape[1]
-    norm_high = lax.reduce_precision(norm_part, 8, 7)
-    norm_low = norm_part - norm_high
-    extra = jnp.concatenate(
-        [norm_high, norm_low, jnp.zeros((4, width), jnp.float32)], axis=0
-    ).astype(jnp.bfloat16)
+    extra = split_in_two(norm_part).astype(jnp.bfloat16)
     packed = jnp.concatenate([chunks, jnp.broadcast_to(extra[None], (cols, 8, width))], axis=1)
     arrived = lax.all_to_all(packed, "col", 0, 0, tiled=True)
     part = arrived.astype(jnp.float32).sum(axis=0)
-    whole = sent_to_all(part, "row").sum(axis=0)
+    whole = sent_to_all(with_split_norm(part, rows), "row").astype(jnp.float32).sum(axis=0)
     norm_grad = whole[rows : rows + 2] + whole[rows + 2 : rows + 4]
     chunk, norm_grad = lax.optimization_barrier((whole[:rows].astype(jnp.bfloat16), norm_grad))
     weight_grad = sent_to_all(chunk, "col").reshape(shape)

time: 148 us -> 148 us (level)
  no operation moved by 1% of the time
where the time goes in v8:
time: 148 us; the launch traced here: 147 us
  blocking collectives  68.9 us (47%)
  starting transfers between devices  37.4 us (25%)
  waiting for transfers between devices  21.1 us (14%)
  Pallas kernels  7.05 us (5%)
  local copies, waits for them, and re-layouts  6.63 us (4%)
  other arithmetic  3.74 us (3%)
    all_to_all x2, blocking collectives, sent_to_all(): lax.all_to_all(jnp.broadcast_to(x[None], (devices, *x.shape)), axis, 0, 0...  29.5 us
    all_to_all x1, blocking collectives, all_steps(): lax.all_to_all(own, 'col', 0, 0, tiled=True, axis_index_groups=lines_z)  21.1 us
    ppermute x5, starting transfers between devices, exchanged(): return lax.ppermute(x, axis, [(d, d ^ step) for d in range(devices)])  19.9 us
    all_to_all x1, blocking collectives, summed_over_all(): arrived = lax.all_to_all(packed, 'col', 0, 0, tiled=True)  18.3 us
    all_to_all x1, waiting for transfers between devices, all_steps(): lax.all_to_all(chip_part, 'col', 0, 0, tiled=True, axis_index_groups=one_...  12.7 us
    all_to_all x1, starting transfers between devices, sent_and_summed(): lax.all_to_all(parts, axis, split_axis=0, concat_axis=0, tiled=True)  7.16 us
    all_to_all x1, waiting for transfers between devices, sent_and_summed(): lax.all_to_all(parts, axis, split_axis=0, concat_axis=0, tiled=True)  6.99 us
    all_to_all x1, starting transfers between devices, all_steps(): lax.all_to_all(right_near, 'row', 0, 0, tiled=True, axis_index_groups=lin...  6.82 us
  transfers between devices with their start and end apart: 8, of which 3 were waited for; matrix products, arithmetic and copies ran while one was open for 4% of the time, Pallas kernels for 5%

profile of v8, /device:TPU:1, one launch (start us, length us, event | category | flops | bytes accessed | tf_op | source)
XLA Modules:
  0.0 146.5 jit_solution(15469406451682283751)
XLA Ops:
  0.6 0.8 broadcast_in_dim.17
  1.4 21.1 %all_to_all.35 = bf16[8,4,32,128]{3,2,1,0:T(8,128)(2,1)S(1)} all-to-all(bf16[8,4,32,128]{3,2,1,0:T(8,128)(2,1)S(1)} %broadcast_in_dim.17), channel_id=1, replica_groups={{0,4,8,12,16,20,24,28},{1,5,9,13,17,21,25,29},{2,6,10,14,18,22,26,30},{..., dimensions={0} | all-to-all | bytes 524288 | tf_op jit(solution)/shard_map/all_to_all | solution.py:254
  22.6 1.5 %broadcast_in_dim.15 = bf16[8,4,32,128]{3,2,1,0:T(8,128)(2,1)} broadcast(bf16[4,32,128]{2,1,0:T(8,128)(2,1)} %bitcast.62), dimensions={1,2,3} | broadcast | bytes 294912 | tf_op jit(solution)/shard_map/broadcast_in_dim | solution.py:243
  24.1 6.8 %all-to-all-start = ((bf16[8,4,32,128]{3,2,1,0:T(8,128)(2,1)}), bf16[8,4,32,128]{3,2,1,0:T(8,128)(2,1)S(1)}, u32[]{:S(2)}, u32[]{:S(2)}) async-start(bf16[8,4,32,128]{3,2,1,0:T(8,128)(2,1)} %broadcast_in_dim.15), calls=%async_computation | async-start | bytes 524288 | tf_op jit(solution)/shard_map/all_to_all | solution.py:244
  30.9 3.1 %collective-permute-start.2 = (bf16[8,128,128]{2,1,0:T(8,128)(2,1)S(1)}, bf16[8,128,128]{2,1,0:T(8,128)(2,1)S(1)}, u32[]{:S(2)}, u32[]{:S(2)}) collective-permute-start(bf16[8,128,128]{2,1,0:T(8,128)(2,1)S(1)} %bitcast.49), channel_id=1, source_target_pairs={{0,2},{1,3},{2,0},{3,1},{4,6},{5,7},{6,4},{7,5},{8,10},{9,11},{10,... | collective-permute-start | bytes 786440 | tf_op jit(solution)/shard_map/ppermute | solution.py:96
  34.0 4.8 %collective-permute-start.3 = (bf16[8,128,128]{2,1,0:T(8,128)(2,1)S(1)}, bf16[8,128,128]{2,1,0:T(8,128)(2,1)S(1)}, u32[]{:S(2)}, u32[]{:S(2)}) collective-permute-start(bf16[8,128,128]{2,1,0:T(8,128)(2,1)S(1)} %bitcast.50), channel_id=1, source_target_pairs={{0,1},{1,0},{2,3},{3,2},{4,5},{5,4},{6,7},{7,6},{8,9},{9,8},{10,11... | collective-permute-start | bytes 786440 | tf_op jit(solution)/shard_map/ppermute | solution.py:96
  38.8 0.0 collective-permute-done.2.x_ref
  38.8 4.8 %collective-permute-start.4 = (bf16[8,128,128]{2,1,0:T(8,128)(2,1)S(1)}, bf16[8,128,128]{2,1,0:T(8,128)(2,1)S(1)}, u32[]{:S(2)}, u32[]{:S(2)}) collective-permute-start(bf16[8,128,128]{2,1,0:T(8,128)(2,1)S(1)} %collective-permute-done.2.x_ref), channel_id=1, source_target_pairs={{0,1},{1,0},{2,3},{3,2},{4,5},{5,4},{6,7},{7,6},{8,9},{9,8},{10,11... | collective-permute-start | bytes 786440 | tf_op jit(solution)/shard_map/ppermute | solution.py:96
  43.7 0.0 all-to-all-done
  43.7 4.7 %collective-permute-start = (bf16[8,4,32,128]{3,2,1,0:T(8,128)(2,1)S(1)}, bf16[8,4,32,128]{3,2,1,0:T(8,128)(2,1)}, u32[]{:S(2)}, u32[]{:S(2)}) collective-permute-start(bf16[8,4,32,128]{3,2,1,0:T(8,128)(2,1)S(1)} %all-to-all-done), channel_id=1, source_target_pairs={{0,256},{32,288},{64,320},{96,352},{128,384},{160,416},{192,448},{... | collective-permute-start | bytes 786440 | tf_op jit(solution)/shard_map/ppermute | solution.py:96
  48.4 3.8 %copy.17 = bf16[128,64,128]{0,1,2:T(8,128)(2,1)S(1)} copy(bf16[128,64,128]{2,1,0:T(8,128)(2,1)} %bitcast.53) | data formatting | bytes 4194304 | tf_op jit(solution)/shard_map/reshape | solution.py:250
  52.2 0.0 collective-permute-done.3.core_ref
  52.2 0.0 collective-permute-done.4.both_ref
  52.2 3.9 %right_parts.1 = bf16[2048,128]{1,0:T(8,128)(2,1)} custom-call(bf16[8,128,128]{2,1,0:T(8,128)(2,1)S(1)} %bitcast.51, bf16[8,128,128]{2,1,0:T(8,128)(2,1)S(1)} %collective-permute-done.2.x_ref, bf16[8,128,128]{2,1,0:T(8,128)(2,1)S(1)} %collective-permute-done.3.core_ref, bf16[8,128,128]{2,1,0:T(8,128)(2,1)S(1)} %collective-permute-done.4.both_ref, ...), custom_call_target="tpu_custom_call" | custom-call | tf_op jit(solution)/shard_map/right_parts/pallas_call | solution.py:217
  56.1 7.2 %all-to-all-start.3 = ((bf16[16,4,32,128]{3,2,1,0:T(8,128)(2,1)}), bf16[16,4,32,128]{3,2,1,0:T(8,128)(2,1)S(1)}, u32[]{:S(2)}, u32[]{:S(2)}) async-start(bf16[16,4,32,128]{3,2,1,0:T(8,128)(2,1)} %bitcast.10), calls=%async_computation.3 | async-start | bytes 1048576 | tf_op jit(solution)/shard_map/all_to_all | solution.py:24
  63.3 0.0 collective-permute-done
  63.3 0.0 copy-start.1
  63.3 3.1 %left_parts.1 = (bf16[16,128,128]{2,1,0:T(8,128)(2,1)S(1)}, bf16[16,128,128]{2,1,0:T(8,128)(2,1)S(1)}) custom-call(bf16[1024,128]{1,0:T(8,128)(2,1)S(1)} %bitcast.52, bf16[1024,128]{1,0:T(8,128)(2,1)} %bitcast.2.far_ref, bf16[128,64,128]{2,1,0:T(8,128)(2,1)S(1)} %bitcast.48), custom_call_target="tpu_custom_call" | custom-call | tf_op jit(solution)/shard_map/left_parts/pallas_call | solution.py:160
  66.5 0.0 copy-start.2
  66.5 0.0 copy-start.3
  66.5 2.5 %collective-permute-start.1 = (bf16[16,128,128]{2,1,0:T(8,128)(2,1)S(1)}, bf16[16,128,128]{2,1,0:T(8,128)(2,1)S(1)}, u32[]{:S(2)}, u32[]{:S(2)}) collective-permute-start(bf16[16,128,128]{2,1,0:T(8,128)(2,1)S(1)} %get-tuple-element.11), channel_id=1, source_target_pairs={{0,1},{1,0},{2,3},{3,2},{4,5},{5,4},{6,7},{7,6},{8,9},{9,8},{10,11... | collective-permute-start | bytes 1572872 | tf_op jit(solution)/shard_map/ppermute | solution.py:96
  69.0 0.0 copy-done
  69.0 0.1 convert_reduce_fusion.4
  69.1 1.4 collective-permute-done.1
  70.5 1.0 add_convert_fusion
  71.5 7.0 %all-to-all-done.3 = bf16[16,4,32,128]{3,2,1,0:T(8,128)(2,1)S(1)} async-done(((bf16[16,4,32,128]{3,2,1,0:T(8,128)(2,1)}), bf16[16,4,32,128]{3,2,1,0:T(8,128)(2,1)S(1)}, u32[]{:S(2)}, u32[]{:S(2)}) %all-to-all-start.3) | async-done | bytes 524320 | tf_op jit(solution)/shard_map/all_to_all | solution.py:24
  78.4 3.6 %all-to-all-start.1 = ((bf16[16,128,128]{2,1,0:T(8,128)(2,1)}), bf16[16,128,128]{2,1,0:T(8,128)(2,1)S(1)}, u32[]{:S(2)}, u32[]{:S(2)}) async-start(bf16[16,128,128]{2,1,0:T(8,128)(2,1)} %add_convert_fusion), calls=%async_computation.1 | async-start | bytes 1048576 | tf_op jit(solution)/shard_map/all_to_all | solution.py:262
  82.0 0.0 copy-done.1
  82.0 0.1 copy.18
  82.2 0.1 div.25
  82.3 0.2 multiply_reduce_fusion.2
  82.4 0.1 rsqrt.13
  82.5 0.0 copy-done.2
  82.5 0.1 add_convert_fusion.1
  82.7 0.2 fusion.19
  82.8 0.1 convert_reduce_fusion
  82.9 12.7 %all-to-all-done.1 = bf16[16,128,128]{2,1,0:T(8,128)(2,1)S(1)} async-done(((bf16[16,128,128]{2,1,0:T(8,128)(2,1)}), bf16[16,128,128]{2,1,0:T(8,128)(2,1)S(1)}, u32[]{:S(2)}, u32[]{:S(2)}) %all-to-all-start.1) | async-done | bytes 524320 | tf_op jit(solution)/shard_map/all_to_all | solution.py:262
  95.7 0.1 convert_reduce_fusion.1
  95.7 0.1 fusion.11
  95.8 0.1 copy.23
  96.0 0.3 multiply_reduce_fusion
  96.2 0.2 convolution_bitcast_fusion
  96.5 0.8 multiply_convert_fusion
  97.3 18.3 %all_to_all.36 = bf16[32,24,128]{2,1,0:T(8,128)(2,1)S(1)} all-to-all(bf16[32,24,128]{2,1,0:T(8,128)(2,1)S(1)} %pad_maximum_fusion), channel_id=1, replica_groups=mesh['row'=16,'col'=32] {'col'}, dimensions={0} | all-to-all | bytes 393216 | tf_op jit(solution)/shard_map/all_to_all | solution.py:85
  115.7 15.3 %all_to_all.37 = bf16[16,24,128]{2,1,0:T(8,128)(2,1)S(1)} all-to-all(bf16[16,24,128]{2,1,0:T(8,128)(2,1)S(1)} %broadcast_in_dim.19), channel_id=1, replica_groups=mesh['row'=16,'col'=32] {'row'}, dimensions={0} | all-to-all | bytes 196608 | tf_op jit(solution)/shard_map/all_to_all | solution.py:13
  131.0 0.6 slice_add_fusion
  131.6 14.2 %all_to_all.38 = bf16[32,16,128]{2,1,0:T(8,128)(2,1)S(1)} all-to-all(bf16[32,16,128]{2,1,0:T(8,128)(2,1)S(1)} %broadcast_in_dim.20), channel_id=1, replica_groups=mesh['row'=16,'col'=32] {'col'}, dimensions={0} | all-to-all | bytes 262144 | tf_op jit(solution)/shard_map/all_to_all | solution.py:13
  145.8 0.7 bitcast_convert_fusion
  (20 shorter events, 0.2 us)
Async XLA Ops:
  24.1 19.6 %all-to-all-start = ((bf16[8,4,32,128]{3,2,1,0:T(8,128)(2,1)}), bf16[8,4,32,128]{3,2,1,0:T(8,128)(2,1)S(1)}, u32[]{:S(2)}, u32[]{:S(2)}) async-start(bf16[8,4,32,128]{3,2,1,0:T(8,128)(2,1)} %broadcast_in_dim.15), calls=%async_computation | async-start | bytes 524288 | tf_op jit(solution)/shard_map/all_to_all | solution.py:244
  30.9 7.9 %collective-permute-start.2 = (bf16[8,128,128]{2,1,0:T(8,128)(2,1)S(1)}, bf16[8,128,128]{2,1,0:T(8,128)(2,1)S(1)}, u32[]{:S(2)}, u32[]{:S(2)}) collective-permute-start(bf16[8,128,128]{2,1,0:T(8,128)(2,1)S(1)} %bitcast.49), channel_id=1, source_target_pairs={{0,2},{1,3},{2,0},{3,1},{4,6},{5,7},{6,4},{7,5},{8,10},{9,11},{10,... | collective-permute-start | bytes 786440 | tf_op jit(solution)/shard_map/ppermute | solution.py:96
  34.0 18.2 %collective-permute-start.3 = (bf16[8,128,128]{2,1,0:T(8,128)(2,1)S(1)}, bf16[8,128,128]{2,1,0:T(8,128)(2,1)S(1)}, u32[]{:S(2)}, u32[]{:S(2)}) collective-permute-start(bf16[8,128,128]{2,1,0:T(8,128)(2,1)S(1)} %bitcast.50), channel_id=1, source_target_pairs={{0,1},{1,0},{2,3},{3,2},{4,5},{5,4},{6,7},{7,6},{8,9},{9,8},{10,11... | collective-permute-start | bytes 786440 | tf_op jit(solution)/shard_map/ppermute | solution.py:96
  38.8 13.4 %collective-permute-start.4 = (bf16[8,128,128]{2,1,0:T(8,128)(2,1)S(1)}, bf16[8,128,128]{2,1,0:T(8,128)(2,1)S(1)}, u32[]{:S(2)}, u32[]{:S(2)}) collective-permute-start(bf16[8,128,128]{2,1,0:T(8,128)(2,1)S(1)} %collective-permute-done.2.x_ref), channel_id=1, source_target_pairs={{0,1},{1,0},{2,3},{3,2},{4,5},{5,4},{6,7},{7,6},{8,9},{9,8},{10,11... | collective-permute-start | bytes 786440 | tf_op jit(solution)/shard_map/ppermute | solution.py:96
  43.7 19.6 %collective-permute-start = (bf16[8,4,32,128]{3,2,1,0:T(8,128)(2,1)S(1)}, bf16[8,4,32,128]{3,2,1,0:T(8,128)(2,1)}, u32[]{:S(2)}, u32[]{:S(2)}) collective-permute-start(bf16[8,4,32,128]{3,2,1,0:T(8,128)(2,1)S(1)} %all-to-all-done), channel_id=1, source_target_pairs={{0,256},{32,288},{64,320},{96,352},{128,384},{160,416},{192,448},{... | collective-permute-start | bytes 786440 | tf_op jit(solution)/shard_map/ppermute | solution.py:96
  56.1 12.9 %copy-start = (bf16[1,4,32,128]{3,2,1,0:T(8,128)(2,1)S(1)}, bf16[1,4,32,128]{3,2,1,0:T(8,128)(2,1)}, u32[]{:S(2)}) copy-start(bf16[1,4,32,128]{3,2,1,0:T(8,128)(2,1)} %param.7) | copy-start | bytes 98308
  56.1 22.3 %all-to-all-start.3 = ((bf16[16,4,32,128]{3,2,1,0:T(8,128)(2,1)}), bf16[16,4,32,128]{3,2,1,0:T(8,128)(2,1)S(1)}, u32[]{:S(2)}, u32[]{:S(2)}) async-start(bf16[16,4,32,128]{3,2,1,0:T(8,128)(2,1)} %bitcast.10), calls=%async_computation.3 | async-start | bytes 1048576 | tf_op jit(solution)/shard_map/all_to_all | solution.py:24
  63.3 18.7 %copy-start.1 = (bf16[4,128,128]{2,1,0:T(8,128)(2,1)S(1)}, bf16[4,128,128]{2,1,0:T(8,128)(2,1)}, u32[]{:S(2)}) copy-start(bf16[4,128,128]{2,1,0:T(8,128)(2,1)} %param.13) | copy-start | bytes 393220
  66.5 16.1 %copy-start.2 = (f32[128]{0:T(128)S(1)}, f32[128]{0:T(128)}, u32[]{:S(2)}) copy-start(f32[128]{0:T(128)} %param.11) | copy-start | bytes 1540
  66.5 16.0 %copy-start.3 = (f32[128]{0:T(128)S(1)}, f32[128]{0:T(128)}, u32[]{:S(2)}) copy-start(f32[128]{0:T(128)} %param.12) | copy-start | bytes 1540
  66.5 4.0 %collective-permute-start.1 = (bf16[16,128,128]{2,1,0:T(8,128)(2,1)S(1)}, bf16[16,128,128]{2,1,0:T(8,128)(2,1)S(1)}, u32[]{:S(2)}, u32[]{:S(2)}) collective-permute-start(bf16[16,128,128]{2,1,0:T(8,128)(2,1)S(1)} %get-tuple-element.11), channel_id=1, source_target_pairs={{0,1},{1,0},{2,3},{3,2},{4,5},{5,4},{6,7},{7,6},{8,9},{9,8},{10,11... | collective-permute-start | bytes 1572872 | tf_op jit(solution)/shard_map/ppermute | solution.py:96
  78.4 17.2 %all-to-all-start.1 = ((bf16[16,128,128]{2,1,0:T(8,128)(2,1)}), bf16[16,128,128]{2,1,0:T(8,128)(2,1)S(1)}, u32[]{:S(2)}, u32[]{:S(2)}) async-start(bf16[16,128,128]{2,1,0:T(8,128)(2,1)} %add_convert_fusion), calls=%async_computation.1 | async-start | bytes 1048576 | tf_op jit(solution)/shard_map/all_to_all | solution.py:262

commit v9 on v8

--- a/solution.py
+++ b/solution.py
@@ -113,22 +113,19 @@
 
 
 def place_of():
-    row, col = lax.axis_index("row"), lax.axis_index("col")
-    half = lax.axis_size("row") // 2
-    return lax.div(row, half), lax.rem(lax.div(col, 2), 2), lax.rem(col, 2)
-
-
-def left_kernel(window_len, near_ref, far_ref, cot_ref, kept_ref, away_ref, *scratch):
+    col = lax.axis_index("col")
+    return lax.rem(lax.div(col, 2), 2), lax.rem(col, 2)
+
+
+def left_kernel(window_len, rows_ref, cot_ref, kept_ref, away_ref, *scratch):
     wide, by_key, product, rows_out = scratch
     hidden, cols, rows = cot_ref.shape
-    x_high, _, core = place_of()
-    group, step = window_len + PAD, hidden + PAD
-    for source, half in ((near_ref, x_high), (far_ref, 1 - x_high)):
-        for j in range(cols // 2):
-            at = pl.multiple_of((half * (cols // 2) + j) * group, 8)
-            wide[pl.ds(at, window_len), :] = source[pl.ds(j * window_len, window_len), :].astype(
-                jnp.float32
-            )
+    _, core = place_of()
+    group, step = window_len + PAD, hidden + PAD
+    for j in range(cols):
+        wide[pl.ds(j * group, window_len), :] = rows_ref[
+            pl.ds(j * window_len, window_len), :
+        ].astype(jnp.float32)
     for k in range(window_len):
         by_key[pl.ds(k * step, hidden), :] = turned(
             wide[pl.ds(k, cols, stride=group), :].astype(jnp.bfloat16)
@@ -152,7 +149,7 @@
                 ].astype(jnp.bfloat16)
 
 
-def left_parts(near, far, cot_turned, blocks, window_len):
+def left_parts(right_rows, cot_turned, blocks, window_len):
     hidden, cols, rows = cot_turned.shape
     group, step = window_len + PAD, hidden + PAD
     out = jax.ShapeDtypeStruct((blocks // 2, rows * window_len // blocks, hidden), jnp.bfloat16)
@@ -160,7 +157,7 @@
     return pl.pallas_call(
         functools.partial(left_kernel, window_len),
         out_shape=(out, out),
-        in_specs=[here, here, here],
+        in_specs=[here, here],
         out_specs=(here, here),
         scratch_shapes=[
             pltpu.VMEM((cols * group, hidden), jnp.float32),
@@ -170,13 +167,13 @@
         ],
         compiler_params=pltpu.CompilerParams(vmem_limit_bytes=VMEM_LIMIT),
         name="left_parts",
-    )(near, far, cot_turned)
+    )(right_rows, cot_turned)
 
 
 def right_kernel(window_len, own_ref, x_ref, core_ref, both_ref, cot_ref, out_ref, *scratch):
     wide, by_key, product, rows_out = scratch
     hidden, cols, rows = cot_ref.shape
-    _, x_low, core = place_of()
+    x_low, core = place_of()
     group, step = window_len + PAD, hidden + PAD
     tokens = own_ref.shape[1] // window_len
     for source, x, side in (
@@ -236,15 +233,9 @@
     block_count, own_rows, col_tokens, channels = tri_cotangent.shape
     window_len = saved_left.shape[2]
     cols = lax.axis_size("col")
-    rows = lax.axis_size("row")
-    lines_y = [[x * (rows // 2) + y for y in range(rows // 2)] for x in range(2)]
     lines_z = [[z * 4 + k for z in range(cols // 4)] for k in range(4)]
     one_core = [[c for c in range(cols) if c % 2 == k] for k in range(2)]
-    right_near = jnp.broadcast_to(saved_right, (rows // 2, *saved_right.shape[1:]))
-    right_near = lax.all_to_all(
-        right_near, "row", 0, 0, tiled=True, axis_index_groups=lines_y
-    )
-    right_far = exchanged(right_near, "row", rows // 2)
+    right_rows = sent_to_all(saved_right[0], "row").reshape(col_tokens * window_len, channels)
     cot_turned = lax.optimization_barrier(
         jnp.transpose(
             tri_cotangent.reshape(block_count * own_rows, col_tokens, channels), (2, 1, 0)
@@ -253,10 +244,7 @@
     own = jnp.broadcast_to(saved_left, (cols // 4, *saved_left.shape[1:]))
     own = lax.all_to_all(own, "col", 0, 0, tiled=True, axis_index_groups=lines_z)
     own = own.reshape(cols // 4, own_rows * window_len, channels)
-    flat = (-1, channels)
-    kept, away = left_parts(
-        right_near.reshape(flat), right_far.reshape(flat), cot_turned, cols, window_len
-    )
+    kept, away = left_parts(right_rows, cot_turned, cols, window_len)
     came = exchanged(away, "col", 1)
     chip_part = (kept.astype(jnp.float32) + came.astype(jnp.float32)).astype(jnp.bfloat16)
     left_arrived = lax.all_to_all(chip_part, "col", 0, 0, tiled=True, axis_index_groups=one_core)

time: 148 us -> 153 us (1.034)
  waiting for transfers between devices: 21.1 us -> 30.4 us
  starting transfers between devices: 37.4 us -> 35.1 us
  blocking collectives: 68.9 us -> 67.3 us
    ppermute x5 -> x4, starting transfers between devices: 19.9 us -> 13.5 us  [exchanged(): return lax.ppermute(x, axis, [(d, d ^ step) for d in range(devices)])]
    ppermute x5 -> x4, waiting for transfers between devices: 1.42 us -> 7.43 us  [exchanged(): return lax.ppermute(x, axis, [(d, d ^ step) for d in range(devices)])]
    all_to_all x1, starting transfers between devices: 6.82 us -> 9.39 us  [sent_to_all(): lax.all_to_all(jnp.broadcast_to(x[None], (devices, *x.shape)), axis, 0, 0...]
    all_to_all x1, waiting for transfers between devices: 6.99 us -> 9.03 us  [sent_and_summed(): lax.all_to_all(parts, axis, split_axis=0, concat_axis=0, tiled=True)]
    broadcast_in_dim x2 -> x3, local copies, waits for them, and re-layouts: 0.03 us -> 1.68 us  [sent_to_all(): jnp.broadcast_to(x[None], (devices, *x.shape))]
  transfers between devices with their start and end apart: 8 -> 7, of which waited for: 3 -> 4; matrix products, arithmetic and copies ran while one was open for 4% -> 4% of each run, Pallas kernels for 5% -> 5%
where the time goes in v9:
time: 153 us; the launch traced here: 152 us
  blocking collectives  67.3 us (44%)
  starting transfers between devices  35.1 us (23%)
  waiting for transfers between devices  30.4 us (20%)
  Pallas kernels  6.99 us (5%)
  local copies, waits for them, and re-layouts  6.79 us (4%)
  other arithmetic  3.7 us (2%)
    all_to_all x2, blocking collectives, sent_to_all(): lax.all_to_all(jnp.broadcast_to(x[None], (devices, *x.shape)), axis, 0, 0...  29 us
    all_to_all x1, blocking collectives, all_steps(): lax.all_to_all(own, 'col', 0, 0, tiled=True, axis_index_groups=lines_z)  21.1 us
    all_to_all x1, blocking collectives, summed_over_all(): arrived = lax.all_to_all(packed, 'col', 0, 0, tiled=True)  17.1 us
    all_to_all x1, waiting for transfers between devices, all_steps(): lax.all_to_all(chip_part, 'col', 0, 0, tiled=True, axis_index_groups=one_...  13.9 us
    ppermute x4, starting transfers between devices, exchanged(): return lax.ppermute(x, axis, [(d, d ^ step) for d in range(devices)])  13.5 us
    all_to_all x1, starting transfers between devices, sent_to_all(): lax.all_to_all(jnp.broadcast_to(x[None], (devices, *x.shape)), axis, 0, 0...  9.39 us
    all_to_all x1, waiting for transfers between devices, sent_and_summed(): lax.all_to_all(parts, axis, split_axis=0, concat_axis=0, tiled=True)  9.03 us
    all_to_all x1, starting transfers between devices, sent_and_summed(): lax.all_to_all(parts, axis, split_axis=0, concat_axis=0, tiled=True)  8.68 us
  transfers between devices with their start and end apart: 7, of which 4 were waited for; matrix products, arithmetic and copies ran while one was open for 4% of the time, Pallas kernels for 5%

profile of v9, /device:TPU:1, one launch (start us, length us, event | category | flops | bytes accessed | tf_op | source)
XLA Modules:
  0.0 151.8 jit_solution(3501197347451967421)
XLA Ops:
  0.6 0.8 broadcast_in_dim.17
  1.4 21.1 %all_to_all.35 = bf16[8,4,32,128]{3,2,1,0:T(8,128)(2,1)S(1)} all-to-all(bf16[8,4,32,128]{3,2,1,0:T(8,128)(2,1)S(1)} %broadcast_in_dim.17), channel_id=1, replica_groups={{0,4,8,12,16,20,24,28},{1,5,9,13,17,21,25,29},{2,6,10,14,18,22,26,30},{..., dimensions={0} | all-to-all | bytes 524288 | tf_op jit(solution)/shard_map/all_to_all | solution.py:245
  22.6 1.6 %broadcast_in_dim.15 = bf16[16,4,32,128]{3,2,1,0:T(8,128)(2,1)} broadcast(bf16[4,32,128]{2,1,0:T(8,128)(2,1)} %bitcast.61), dimensions={1,2,3} | broadcast | bytes 557056 | tf_op jit(solution)/shard_map/broadcast_in_dim | solution.py:13
  24.2 9.4 %all-to-all-start = ((bf16[16,4,32,128]{3,2,1,0:T(8,128)(2,1)}), bf16[16,4,32,128]{3,2,1,0:T(8,128)(2,1)S(1)}, u32[]{:S(2)}, u32[]{:S(2)}) async-start(bf16[16,4,32,128]{3,2,1,0:T(8,128)(2,1)} %broadcast_in_dim.15), calls=%async_computation | async-start | bytes 1048576 | tf_op jit(solution)/shard_map/all_to_all | solution.py:13
  33.6 2.2 %collective-permute-start.1 = (bf16[8,128,128]{2,1,0:T(8,128)(2,1)S(1)}, bf16[8,128,128]{2,1,0:T(8,128)(2,1)S(1)}, u32[]{:S(2)}, u32[]{:S(2)}) collective-permute-start(bf16[8,128,128]{2,1,0:T(8,128)(2,1)S(1)} %bitcast.49), channel_id=1, source_target_pairs={{0,2},{1,3},{2,0},{3,1},{4,6},{5,7},{6,4},{7,5},{8,10},{9,11},{10,... | collective-permute-start | bytes 786440 | tf_op jit(solution)/shard_map/ppermute | solution.py:96
  35.9 4.8 %collective-permute-start.2 = (bf16[8,128,128]{2,1,0:T(8,128)(2,1)S(1)}, bf16[8,128,128]{2,1,0:T(8,128)(2,1)S(1)}, u32[]{:S(2)}, u32[]{:S(2)}) collective-permute-start(bf16[8,128,128]{2,1,0:T(8,128)(2,1)S(1)} %bitcast.50), channel_id=1, source_target_pairs={{0,1},{1,0},{2,3},{3,2},{4,5},{5,4},{6,7},{7,6},{8,9},{9,8},{10,11... | collective-permute-start | bytes 786440 | tf_op jit(solution)/shard_map/ppermute | solution.py:96
  40.7 5.9 %collective-permute-done.1.x_ref = bf16[8,128,128]{2,1,0:T(8,128)(2,1)S(1)} collective-permute-done((bf16[8,128,128]{2,1,0:T(8,128)(2,1)S(1)}, bf16[8,128,128]{2,1,0:T(8,128)(2,1)S(1)}, u32[]{:S(2)}, u32[]{:S(2)}) %collective-permute-start.1) | collective-permute-done | bytes 262176 | tf_op jit(solution)/shard_map/ppermute | solution.py:96
  46.6 4.3 %collective-permute-start.3 = (bf16[8,128,128]{2,1,0:T(8,128)(2,1)S(1)}, bf16[8,128,128]{2,1,0:T(8,128)(2,1)}, u32[]{:S(2)}, u32[]{:S(2)}) collective-permute-start(bf16[8,128,128]{2,1,0:T(8,128)(2,1)S(1)} %collective-permute-done.1.x_ref), channel_id=1, source_target_pairs={{0,1},{1,0},{2,3},{3,2},{4,5},{5,4},{6,7},{7,6},{8,9},{9,8},{10,11... | collective-permute-start | bytes 786440 | tf_op jit(solution)/shard_map/ppermute | solution.py:96
  50.9 3.8 %copy.17 = bf16[128,64,128]{0,1,2:T(8,128)(2,1)S(1)} copy(bf16[128,64,128]{2,1,0:T(8,128)(2,1)} %bitcast.52) | data formatting | bytes 4194304 | tf_op jit(solution)/shard_map/reshape | solution.py:241
  54.7 0.0 collective-permute-done.2.core_ref
  54.7 0.0 collective-permute-done.3.both_ref
  54.7 4.9 %right_parts.1 = bf16[2048,128]{1,0:T(8,128)(2,1)} custom-call(bf16[8,128,128]{2,1,0:T(8,128)(2,1)S(1)} %bitcast.51, bf16[8,128,128]{2,1,0:T(8,128)(2,1)S(1)} %collective-permute-done.1.x_ref, bf16[8,128,128]{2,1,0:T(8,128)(2,1)S(1)} %collective-permute-done.2.core_ref, bf16[8,128,128]{2,1,0:T(8,128)(2,1)} %collective-permute-done.3.both_ref, ...), custom_call_target="tpu_custom_call" | custom-call | tf_op jit(solution)/shard_map/right_parts/pallas_call | solution.py:214
  59.6 0.0 copy-start
  59.6 0.0 all-to-all-done
  59.6 8.7 %all-to-all-start.3 = ((bf16[16,4,32,128]{3,2,1,0:T(8,128)(2,1)}), bf16[16,4,32,128]{3,2,1,0:T(8,128)(2,1)S(1)}, u32[]{:S(2)}, u32[]{:S(2)}) async-start(bf16[16,4,32,128]{3,2,1,0:T(8,128)(2,1)} %bitcast.9), calls=%async_computation.3 | async-start | bytes 1048576 | tf_op jit(solution)/shard_map/all_to_all | solution.py:24
  68.3 0.0 copy-start.1
  68.3 2.1 %left_parts.1 = (bf16[16,128,128]{2,1,0:T(8,128)(2,1)S(1)}, bf16[16,128,128]{2,1,0:T(8,128)(2,1)S(1)}) custom-call(bf16[2048,128]{1,0:T(8,128)(2,1)S(1)} %bitcast.48, bf16[128,64,128]{2,1,0:T(8,128)(2,1)S(1)} %bitcast.47), custom_call_target="tpu_custom_call" | custom-call | tf_op jit(solution)/shard_map/left_parts/pallas_call | solution.py:157
  70.4 0.0 copy-start.2
  70.4 0.0 copy-start.3
  70.5 2.2 %collective-permute-start = (bf16[16,128,128]{2,1,0:T(8,128)(2,1)S(1)}, bf16[16,128,128]{2,1,0:T(8,128)(2,1)S(1)}, u32[]{:S(2)}, u32[]{:S(2)}) collective-permute-start(bf16[16,128,128]{2,1,0:T(8,128)(2,1)S(1)} %get-tuple-element.11), channel_id=1, source_target_pairs={{0,1},{1,0},{2,3},{3,2},{4,5},{5,4},{6,7},{7,6},{8,9},{9,8},{10,11... | collective-permute-start | bytes 1572872 | tf_op jit(solution)/shard_map/ppermute | solution.py:96
  72.7 0.0 copy-done
  72.7 0.1 convert_reduce_fusion.4
  72.8 1.5 collective-permute-done
  74.3 0.9 add_convert_fusion
  75.2 9.0 %all-to-all-done.3 = bf16[16,4,32,128]{3,2,1,0:T(8,128)(2,1)S(1)} async-done(((bf16[16,4,32,128]{3,2,1,0:T(8,128)(2,1)}), bf16[16,4,32,128]{3,2,1,0:T(8,128)(2,1)S(1)}, u32[]{:S(2)}, u32[]{:S(2)}) %all-to-all-start.3) | async-done | bytes 524320 | tf_op jit(solution)/shard_map/all_to_all | solution.py:24
  84.2 3.6 %all-to-all-start.1 = ((bf16[16,128,128]{2,1,0:T(8,128)(2,1)}), bf16[16,128,128]{2,1,0:T(8,128)(2,1)S(1)}, u32[]{:S(2)}, u32[]{:S(2)}) async-start(bf16[16,128,128]{2,1,0:T(8,128)(2,1)} %add_convert_fusion), calls=%async_computation.1 | async-start | bytes 1048576 | tf_op jit(solution)/shard_map/all_to_all | solution.py:250
  87.8 0.1 div.25
  87.9 0.2 multiply_reduce_fusion.2
  88.1 0.1 rsqrt.13
  88.2 0.0 copy-done.1
  88.2 0.1 copy.18
  88.3 0.0 copy-done.2
  88.3 0.0 copy-done.3
  88.3 0.1 add_convert_fusion.1
  88.4 0.2 fusion.19
  88.6 0.1 convert_reduce_fusion
  88.7 13.9 %all-to-all-done.1 = bf16[16,128,128]{2,1,0:T(8,128)(2,1)S(1)} async-done(((bf16[16,128,128]{2,1,0:T(8,128)(2,1)}), bf16[16,128,128]{2,1,0:T(8,128)(2,1)S(1)}, u32[]{:S(2)}, u32[]{:S(2)}) %all-to-all-start.1) | async-done | bytes 524320 | tf_op jit(solution)/shard_map/all_to_all | solution.py:250
  102.6 0.1 convert_reduce_fusion.1
  102.7 0.1 fusion.11
  102.8 0.1 copy.23
  102.9 0.3 multiply_reduce_fusion
  103.2 0.2 convolution_bitcast_fusion
  103.4 0.8 multiply_convert_fusion
  104.3 17.1 %all_to_all.36 = bf16[32,24,128]{2,1,0:T(8,128)(2,1)S(1)} all-to-all(bf16[32,24,128]{2,1,0:T(8,128)(2,1)S(1)} %pad_maximum_fusion), channel_id=1, replica_groups=mesh['row'=16,'col'=32] {'col'}, dimensions={0} | all-to-all | bytes 393216 | tf_op jit(solution)/shard_map/all_to_all | solution.py:85
  121.5 14.8 %all_to_all.37 = bf16[16,24,128]{2,1,0:T(8,128)(2,1)S(1)} all-to-all(bf16[16,24,128]{2,1,0:T(8,128)(2,1)S(1)} %broadcast_in_dim.19), channel_id=1, replica_groups=mesh['row'=16,'col'=32] {'row'}, dimensions={0} | all-to-all | bytes 196608 | tf_op jit(solution)/shard_map/all_to_all | solution.py:13
  136.3 0.6 slice_add_fusion
  136.9 14.2 %all_to_all.38 = bf16[32,16,128]{2,1,0:T(8,128)(2,1)S(1)} all-to-all(bf16[32,16,128]{2,1,0:T(8,128)(2,1)S(1)} %broadcast_in_dim.20), channel_id=1, replica_groups=mesh['row'=16,'col'=32] {'col'}, dimensions={0} | all-to-all | bytes 262144 | tf_op jit(solution)/shard_map/all_to_all | solution.py:13
  151.1 0.7 bitcast_convert_fusion
  (18 shorter events, 0.2 us)
Async XLA Ops:
  24.2 35.4 %all-to-all-start = ((bf16[16,4,32,128]{3,2,1,0:T(8,128)(2,1)}), bf16[16,4,32,128]{3,2,1,0:T(8,128)(2,1)S(1)}, u32[]{:S(2)}, u32[]{:S(2)}) async-start(bf16[16,4,32,128]{3,2,1,0:T(8,128)(2,1)} %broadcast_in_dim.15), calls=%async_computation | async-start | bytes 1048576 | tf_op jit(solution)/shard_map/all_to_all | solution.py:13
  33.6 13.0 %collective-permute-start.1 = (bf16[8,128,128]{2,1,0:T(8,128)(2,1)S(1)}, bf16[8,128,128]{2,1,0:T(8,128)(2,1)S(1)}, u32[]{:S(2)}, u32[]{:S(2)}) collective-permute-start(bf16[8,128,128]{2,1,0:T(8,128)(2,1)S(1)} %bitcast.49), channel_id=1, source_target_pairs={{0,2},{1,3},{2,0},{3,1},{4,6},{5,7},{6,4},{7,5},{8,10},{9,11},{10,... | collective-permute-start | bytes 786440 | tf_op jit(solution)/shard_map/ppermute | solution.py:96
  35.9 18.9 %collective-permute-start.2 = (bf16[8,128,128]{2,1,0:T(8,128)(2,1)S(1)}, bf16[8,128,128]{2,1,0:T(8,128)(2,1)S(1)}, u32[]{:S(2)}, u32[]{:S(2)}) collective-permute-start(bf16[8,128,128]{2,1,0:T(8,128)(2,1)S(1)} %bitcast.50), channel_id=1, source_target_pairs={{0,1},{1,0},{2,3},{3,2},{4,5},{5,4},{6,7},{7,6},{8,9},{9,8},{10,11... | collective-permute-start | bytes 786440 | tf_op jit(solution)/shard_map/ppermute | solution.py:96
  46.6 8.1 %collective-permute-start.3 = (bf16[8,128,128]{2,1,0:T(8,128)(2,1)S(1)}, bf16[8,128,128]{2,1,0:T(8,128)(2,1)}, u32[]{:S(2)}, u32[]{:S(2)}) collective-permute-start(bf16[8,128,128]{2,1,0:T(8,128)(2,1)S(1)} %collective-permute-done.1.x_ref), channel_id=1, source_target_pairs={{0,1},{1,0},{2,3},{3,2},{4,5},{5,4},{6,7},{7,6},{8,9},{9,8},{10,11... | collective-permute-start | bytes 786440 | tf_op jit(solution)/shard_map/ppermute | solution.py:96
  59.6 13.0 %copy-start = (bf16[1,4,32,128]{3,2,1,0:T(8,128)(2,1)S(1)}, bf16[1,4,32,128]{3,2,1,0:T(8,128)(2,1)}, u32[]{:S(2)}) copy-start(bf16[1,4,32,128]{3,2,1,0:T(8,128)(2,1)} %param.7) | copy-start | bytes 98308
  59.6 24.6 %all-to-all-start.3 = ((bf16[16,4,32,128]{3,2,1,0:T(8,128)(2,1)}), bf16[16,4,32,128]{3,2,1,0:T(8,128)(2,1)S(1)}, u32[]{:S(2)}, u32[]{:S(2)}) async-start(bf16[16,4,32,128]{3,2,1,0:T(8,128)(2,1)} %bitcast.9), calls=%async_computation.3 | async-start | bytes 1048576 | tf_op jit(solution)/shard_map/all_to_all | solution.py:24
  68.3 19.9 %copy-start.1 = (bf16[4,128,128]{2,1,0:T(8,128)(2,1)S(1)}, bf16[4,128,128]{2,1,0:T(8,128)(2,1)}, u32[]{:S(2)}) copy-start(bf16[4,128,128]{2,1,0:T(8,128)(2,1)} %param.13) | copy-start | bytes 393220
  70.4 17.9 %copy-start.2 = (f32[128]{0:T(128)S(1)}, f32[128]{0:T(128)}, u32[]{:S(2)}) copy-start(f32[128]{0:T(128)} %param.11) | copy-start | bytes 1540
  70.4 17.9 %copy-start.3 = (f32[128]{0:T(128)S(1)}, f32[128]{0:T(128)}, u32[]{:S(2)}) copy-start(f32[128]{0:T(128)} %param.12) | copy-start | bytes 1540
  70.5 3.8 %collective-permute-start = (bf16[16,128,128]{2,1,0:T(8,128)(2,1)S(1)}, bf16[16,128,128]{2,1,0:T(8,128)(2,1)S(1)}, u32[]{:S(2)}, u32[]{:S(2)}) collective-permute-start(bf16[16,128,128]{2,1,0:T(8,128)(2,1)S(1)} %get-tuple-element.11), channel_id=1, source_target_pairs={{0,1},{1,0},{2,3},{3,2},{4,5},{5,4},{6,7},{7,6},{8,9},{9,8},{10,11... | collective-permute-start | bytes 1572872 | tf_op jit(solution)/shard_map/ppermute | solution.py:96
  84.2 18.4 %all-to-all-start.1 = ((bf16[16,128,128]{2,1,0:T(8,128)(2,1)}), bf16[16,128,128]{2,1,0:T(8,128)(2,1)S(1)}, u32[]{:S(2)}, u32[]{:S(2)}) async-start(bf16[16,128,128]{2,1,0:T(8,128)(2,1)} %add_convert_fusion), calls=%async_computation.1 | async-start | bytes 1048576 | tf_op jit(solution)/shard_map/all_to_all | solution.py:250

commit v10 on v8

--- a/solution.py
+++ b/solution.py
@@ -85,10 +85,10 @@
     arrived = lax.all_to_all(packed, "col", 0, 0, tiled=True)
     part = arrived.astype(jnp.float32).sum(axis=0)
     whole = sent_to_all(with_split_norm(part, rows), "row").astype(jnp.float32).sum(axis=0)
-    norm_grad = whole[rows : rows + 2] + whole[rows + 2 : rows + 4]
-    chunk, norm_grad = lax.optimization_barrier((whole[:rows].astype(jnp.bfloat16), norm_grad))
-    weight_grad = sent_to_all(chunk, "col").reshape(shape)
-    return weight_grad.astype(jnp.float32), norm_grad
+    chunk, sums = lax.optimization_barrier((whole[:rows].astype(jnp.bfloat16), whole[rows:]))
+    weight_grad = sent_to_all(chunk, "col").reshape(-1, width)
+    weight_grad, norm_grad = final_sums(weight_grad, sums)
+    return weight_grad.reshape(shape), norm_grad
 
 
 def exchanged(x, axis, step):
@@ -230,6 +230,43 @@
     )(*pieces, cot_turned)
 
 
+def pair_kernel(kept_ref, came_ref, out_ref):
+    total = kept_ref[...].astype(jnp.float32) + came_ref[...].astype(jnp.float32)
+    out_ref[...] = total.astype(jnp.bfloat16)
+
+
+def pair_sum(kept, came):
+    here = pl.BlockSpec(memory_space=pltpu.VMEM)
+    return pl.pallas_call(
+        pair_kernel,
+        out_shape=jax.ShapeDtypeStruct(kept.shape, kept.dtype),
+        in_specs=[here, here],
+        out_specs=here,
+        compiler_params=pltpu.CompilerParams(vmem_limit_bytes=VMEM_LIMIT // 4),
+        name="pair_sum",
+    )(kept, came)
+
+
+def final_kernel(weight_ref, sums_ref, weight_out, norm_out):
+    weight_out[...] = weight_ref[...].astype(jnp.float32)
+    norm_out[...] = sums_ref[0:2, :] + sums_ref[2:4, :]
+
+
+def final_sums(weight, sums):
+    here = pl.BlockSpec(memory_space=pltpu.VMEM)
+    return pl.pallas_call(
+        final_kernel,
+        out_shape=(
+            jax.ShapeDtypeStruct(weight.shape, jnp.float32),
+            jax.ShapeDtypeStruct((2, sums.shape[1]), jnp.float32),
+        ),
+        in_specs=[here, here],
+        out_specs=(here, here),
+        compiler_params=pltpu.CompilerParams(vmem_limit_bytes=VMEM_LIMIT // 4),
+        name="final_sums",
+    )(weight, sums)
+
+
 def all_steps(
     pair_window, tri_cotangent, saved_left, saved_right, norm_gain, norm_bias, proj_weight
 ):
@@ -258,7 +295,7 @@
         right_near.reshape(flat), right_far.reshape(flat), cot_turned, cols, window_len
     )
     came = exchanged(away, "col", 1)
-    chip_part = (kept.astype(jnp.float32) + came.astype(jnp.float32)).astype(jnp.bfloat16)
+    chip_part = pair_sum(kept, came)
     left_arrived = lax.all_to_all(chip_part, "col", 0, 0, tiled=True, axis_index_groups=one_core)
     across = exchanged(own, "col", 2)
     own_pair = exchanged(own, "col", 1)

time: 148 us -> 151 us (1.020)
  waiting for transfers between devices: 21.1 us -> 27.5 us
  other arithmetic: 3.74 us -> 1.5 us
    ppermute x5, waiting for transfers between devices: 1.42 us -> 12.3 us  [exchanged(): return lax.ppermute(x, axis, [(d, d ^ step) for d in range(devices)])]
    all_to_all x1, waiting for transfers between devices: 6.99 us -> 0.01 us  [sent_and_summed(): lax.all_to_all(parts, axis, split_axis=0, concat_axis=0, tiled=True)]
    all_to_all x1, waiting for transfers between devices: 12.7 us -> 15.2 us  [all_steps(): lax.all_to_all(chip_part, 'col', 0, 0, tiled=True, axis_index_groups=one_...]
    all_to_all x1, blocking collectives: 18.3 us -> 15.8 us  [summed_over_all(): arrived = lax.all_to_all(packed, 'col', 0, 0, tiled=True)]
    ppermute x5, starting transfers between devices: 19.9 us -> 17.5 us  [exchanged(): return lax.ppermute(x, axis, [(d, d ^ step) for d in range(devices)])]
    all_to_all x1, starting transfers between devices: 7.16 us -> 9.33 us  [sent_and_summed(): lax.all_to_all(parts, axis, split_axis=0, concat_axis=0, tiled=True)]
    convert_element_type x2 -> x0, other arithmetic: 1.67 us -> none  [the longest x1 0.95 us: all_steps(): (kept.astype(jnp.float32) + came.astype(jnp.float32)).astype(jnp.bfloat16)]
    pallas_call x0 -> x2, Pallas kernels: none -> 1.65 us  [the longest x1 0.93 us: pair_sum(): pl.pallas_call(pair_kernel, out_shape=jax.ShapeDtypeStruct(kept.shape, ke...]
where the time goes in v10:
time: 151 us; the launch traced here: 150 us
  blocking collectives  67.5 us (45%)
  starting transfers between devices  37.3 us (25%)
  waiting for transfers between devices  27.5 us (18%)
  Pallas kernels  7.74 us (5%)
  local copies, waits for them, and re-layouts  6.63 us (4%)
    all_to_all x2, blocking collectives, sent_to_all(): lax.all_to_all(jnp.broadcast_to(x[None], (devices, *x.shape)), axis, 0, 0...  30.5 us
    all_to_all x1, blocking collectives, all_steps(): lax.all_to_all(own, 'col', 0, 0, tiled=True, axis_index_groups=lines_z)  21.1 us
    ppermute x5, starting transfers between devices, exchanged(): return lax.ppermute(x, axis, [(d, d ^ step) for d in range(devices)])  17.5 us
    all_to_all x1, blocking collectives, summed_over_all(): arrived = lax.all_to_all(packed, 'col', 0, 0, tiled=True)  15.8 us
    all_to_all x1, waiting for transfers between devices, all_steps(): lax.all_to_all(chip_part, 'col', 0, 0, tiled=True, axis_index_groups=one_...  15.2 us
    ppermute x5, waiting for transfers between devices, exchanged(): return lax.ppermute(x, axis, [(d, d ^ step) for d in range(devices)])  12.3 us
    all_to_all x1, starting transfers between devices, sent_and_summed(): lax.all_to_all(parts, axis, split_axis=0, concat_axis=0, tiled=True)  9.33 us
    all_to_all x1, starting transfers between devices, all_steps(): lax.all_to_all(right_near, 'row', 0, 0, tiled=True, axis_index_groups=lin...  6.82 us
  transfers between devices with their start and end apart: 8, of which 3 were waited for; matrix products, arithmetic and copies ran while one was open for 4% of the time, Pallas kernels for 5%

profile of v10, /device:TPU:1, one launch (start us, length us, event | category | flops | bytes accessed | tf_op | source)
XLA Modules:
  0.0 149.7 jit_solution(12007772436312742976)
XLA Ops:
  0.6 0.8 broadcast_in_dim.17
  1.4 21.1 %all_to_all.35 = bf16[8,4,32,128]{3,2,1,0:T(8,128)(2,1)S(1)} all-to-all(bf16[8,4,32,128]{3,2,1,0:T(8,128)(2,1)S(1)} %broadcast_in_dim.17), channel_id=1, replica_groups={{0,4,8,12,16,20,24,28},{1,5,9,13,17,21,25,29},{2,6,10,14,18,22,26,30},{..., dimensions={0} | all-to-all | bytes 524288 | tf_op jit(solution)/shard_map/all_to_all | solution.py:291
  22.6 3.1 %collective-permute-start.2 = (bf16[8,128,128]{2,1,0:T(8,128)(2,1)S(1)}, bf16[8,128,128]{2,1,0:T(8,128)(2,1)S(1)}, u32[]{:S(2)}, u32[]{:S(2)}) collective-permute-start(bf16[8,128,128]{2,1,0:T(8,128)(2,1)S(1)} %bitcast.47), channel_id=1, source_target_pairs={{0,2},{1,3},{2,0},{3,1},{4,6},{5,7},{6,4},{7,5},{8,10},{9,11},{10,... | collective-permute-start | bytes 786440 | tf_op jit(solution)/shard_map/ppermute | solution.py:96
  25.7 1.5 %broadcast_in_dim.15 = bf16[8,4,32,128]{3,2,1,0:T(8,128)(2,1)} broadcast(bf16[4,32,128]{2,1,0:T(8,128)(2,1)} %bitcast.61), dimensions={1,2,3} | broadcast | bytes 294912 | tf_op jit(solution)/shard_map/broadcast_in_dim | solution.py:280
  27.2 6.8 %all-to-all-start = ((bf16[8,4,32,128]{3,2,1,0:T(8,128)(2,1)}), bf16[8,4,32,128]{3,2,1,0:T(8,128)(2,1)S(1)}, u32[]{:S(2)}, u32[]{:S(2)}) async-start(bf16[8,4,32,128]{3,2,1,0:T(8,128)(2,1)} %broadcast_in_dim.15), calls=%async_computation | async-start | bytes 524288 | tf_op jit(solution)/shard_map/all_to_all | solution.py:281
  34.0 4.8 %collective-permute-start.3 = (bf16[8,128,128]{2,1,0:T(8,128)(2,1)S(1)}, bf16[8,128,128]{2,1,0:T(8,128)(2,1)S(1)}, u32[]{:S(2)}, u32[]{:S(2)}) collective-permute-start(bf16[8,128,128]{2,1,0:T(8,128)(2,1)S(1)} %bitcast.48), channel_id=1, source_target_pairs={{0,1},{1,0},{2,3},{3,2},{4,5},{5,4},{6,7},{7,6},{8,9},{9,8},{10,11... | collective-permute-start | bytes 786440 | tf_op jit(solution)/shard_map/ppermute | solution.py:96
  38.8 0.0 collective-permute-done.2.x_ref
  38.8 1.9 %collective-permute-start.4 = (bf16[8,128,128]{2,1,0:T(8,128)(2,1)S(1)}, bf16[8,128,128]{2,1,0:T(8,128)(2,1)S(1)}, u32[]{:S(2)}, u32[]{:S(2)}) collective-permute-start(bf16[8,128,128]{2,1,0:T(8,128)(2,1)S(1)} %collective-permute-done.2.x_ref), channel_id=1, source_target_pairs={{0,1},{1,0},{2,3},{3,2},{4,5},{5,4},{6,7},{7,6},{8,9},{9,8},{10,11... | collective-permute-start | bytes 786440 | tf_op jit(solution)/shard_map/ppermute | solution.py:96
  40.8 3.8 %copy.17 = bf16[128,64,128]{0,1,2:T(8,128)(2,1)S(1)} copy(bf16[128,64,128]{2,1,0:T(8,128)(2,1)} %bitcast.53) | data formatting | bytes 4194304 | tf_op jit(solution)/shard_map/reshape | solution.py:287
  44.6 0.0 collective-permute-done.3.core_ref
  44.6 0.0 collective-permute-done.4.both_ref
  44.6 3.9 %right_parts.1 = bf16[2048,128]{1,0:T(8,128)(2,1)} custom-call(bf16[8,128,128]{2,1,0:T(8,128)(2,1)S(1)} %bitcast.49, bf16[8,128,128]{2,1,0:T(8,128)(2,1)S(1)} %collective-permute-done.2.x_ref, bf16[8,128,128]{2,1,0:T(8,128)(2,1)S(1)} %collective-permute-done.3.core_ref, bf16[8,128,128]{2,1,0:T(8,128)(2,1)S(1)} %collective-permute-done.4.both_ref, ...), custom_call_target="tpu_custom_call" | custom-call | tf_op jit(solution)/shard_map/right_parts/pallas_call | solution.py:217
  48.6 0.0 copy-start
  48.6 0.0 all-to-all-done
  48.6 9.3 %all-to-all-start.3 = ((bf16[16,4,32,128]{3,2,1,0:T(8,128)(2,1)}), bf16[16,4,32,128]{3,2,1,0:T(8,128)(2,1)S(1)}, u32[]{:S(2)}, u32[]{:S(2)}) async-start(bf16[16,4,32,128]{3,2,1,0:T(8,128)(2,1)} %bitcast.10), calls=%async_computation.3 | async-start | bytes 1048576 | tf_op jit(solution)/shard_map/all_to_all | solution.py:24
  57.9 4.8 %collective-permute-start = (bf16[8,4,32,128]{3,2,1,0:T(8,128)(2,1)S(1)}, bf16[8,4,32,128]{3,2,1,0:T(8,128)(2,1)S(1)}, u32[]{:S(2)}, u32[]{:S(2)}) collective-permute-start(bf16[8,4,32,128]{3,2,1,0:T(8,128)(2,1)S(1)} %all-to-all-done), channel_id=1, source_target_pairs={{0,256},{32,288},{64,320},{96,352},{128,384},{160,416},{192,448},{... | collective-permute-start | bytes 786440 | tf_op jit(solution)/shard_map/ppermute | solution.py:96
  62.7 10.9 %collective-permute-done = bf16[8,4,32,128]{3,2,1,0:T(8,128)(2,1)S(1)} collective-permute-done((bf16[8,4,32,128]{3,2,1,0:T(8,128)(2,1)S(1)}, bf16[8,4,32,128]{3,2,1,0:T(8,128)(2,1)S(1)}, u32[]{:S(2)}, u32[]{:S(2)}) %collective-permute-start) | collective-permute-done | bytes 262176 | tf_op jit(solution)/shard_map/ppermute | solution.py:96
  73.5 2.2 %left_parts.1 = (bf16[16,128,128]{2,1,0:T(8,128)(2,1)S(1)}, bf16[16,128,128]{2,1,0:T(8,128)(2,1)S(1)}) custom-call(bf16[1024,128]{1,0:T(8,128)(2,1)S(1)} %bitcast.50, bf16[1024,128]{1,0:T(8,128)(2,1)S(1)} %bitcast.52, bf16[128,64,128]{2,1,0:T(8,128)(2,1)S(1)} %bitcast.46), custom_call_target="tpu_custom_call" | custom-call | tf_op jit(solution)/shard_map/left_parts/pallas_call | solution.py:160
  75.7 0.0 copy-start.2
  75.7 0.0 copy-start.3
  75.7 2.9 %collective-permute-start.1 = (bf16[16,128,128]{2,1,0:T(8,128)(2,1)S(1)}, bf16[16,128,128]{2,1,0:T(8,128)(2,1)S(1)}, u32[]{:S(2)}, u32[]{:S(2)}) collective-permute-start(bf16[16,128,128]{2,1,0:T(8,128)(2,1)S(1)} %get-tuple-element.13), channel_id=1, source_target_pairs={{0,1},{1,0},{2,3},{3,2},{4,5},{5,4},{6,7},{7,6},{8,9},{9,8},{10,11... | collective-permute-start | bytes 1572872 | tf_op jit(solution)/shard_map/ppermute | solution.py:96
  78.7 0.0 copy-done
  78.7 0.1 convert_reduce_fusion.4
  78.8 1.4 collective-permute-done.1.came_ref
  80.2 0.9 pair_sum.1
  81.1 0.0 all-to-all-done.3
  81.1 3.6 %all-to-all-start.1 = ((bf16[16,128,128]{2,1,0:T(8,128)(2,1)}), bf16[16,128,128]{2,1,0:T(8,128)(2,1)S(1)}, u32[]{:S(2)}, u32[]{:S(2)}) async-start(bf16[16,128,128]{2,1,0:T(8,128)(2,1)} %pair_sum.1), calls=%async_computation.1 | async-start | bytes 1048576 | tf_op jit(solution)/shard_map/all_to_all | solution.py:299
  84.7 0.0 copy-done.1
  84.7 0.1 copy.18
  84.9 0.1 div.25
  84.9 0.2 multiply_reduce_fusion.2
  85.1 0.1 rsqrt.13
  85.2 0.0 copy-done.2
  85.2 0.0 copy-done.3
  85.2 0.1 add_convert_fusion
  85.3 0.2 fusion.19
  85.5 0.1 convert_reduce_fusion
  85.6 15.2 %all-to-all-done.1 = bf16[16,128,128]{2,1,0:T(8,128)(2,1)S(1)} async-done(((bf16[16,128,128]{2,1,0:T(8,128)(2,1)}), bf16[16,128,128]{2,1,0:T(8,128)(2,1)S(1)}, u32[]{:S(2)}, u32[]{:S(2)}) %all-to-all-start.1) | async-done | bytes 524320 | tf_op jit(solution)/shard_map/all_to_all | solution.py:299
  100.8 0.1 convert_reduce_fusion.1
  100.9 0.1 fusion.11
  101.0 0.1 copy.23
  101.1 0.3 multiply_reduce_fusion
  101.4 0.2 convolution_bitcast_fusion
  101.6 0.8 multiply_convert_fusion
  102.4 15.8 %all_to_all.36 = bf16[32,24,128]{2,1,0:T(8,128)(2,1)S(1)} all-to-all(bf16[32,24,128]{2,1,0:T(8,128)(2,1)S(1)} %pad_maximum_fusion), channel_id=1, replica_groups=mesh['row'=16,'col'=32] {'col'}, dimensions={0} | all-to-all | bytes 393216 | tf_op jit(solution)/shard_map/all_to_all | solution.py:85
  118.4 16.3 %all_to_all.37 = bf16[16,24,128]{2,1,0:T(8,128)(2,1)S(1)} all-to-all(bf16[16,24,128]{2,1,0:T(8,128)(2,1)S(1)} %broadcast_in_dim.19), channel_id=1, replica_groups=mesh['row'=16,'col'=32] {'row'}, dimensions={0} | all-to-all | bytes 196608 | tf_op jit(solution)/shard_map/all_to_all | solution.py:13
  134.7 14.2 %all_to_all.38 = bf16[32,16,128]{2,1,0:T(8,128)(2,1)S(1)} all-to-all(bf16[32,16,128]{2,1,0:T(8,128)(2,1)S(1)} %broadcast_in_dim.20), channel_id=1, replica_groups=mesh['row'=16,'col'=32] {'col'}, dimensions={0} | all-to-all | bytes 262144 | tf_op jit(solution)/shard_map/all_to_all | solution.py:13
  149.0 0.7 final_sums.1
  (20 shorter events, 0.2 us)
Async XLA Ops:
  22.6 16.2 %collective-permute-start.2 = (bf16[8,128,128]{2,1,0:T(8,128)(2,1)S(1)}, bf16[8,128,128]{2,1,0:T(8,128)(2,1)S(1)}, u32[]{:S(2)}, u32[]{:S(2)}) collective-permute-start(bf16[8,128,128]{2,1,0:T(8,128)(2,1)S(1)} %bitcast.47), channel_id=1, source_target_pairs={{0,2},{1,3},{2,0},{3,1},{4,6},{5,7},{6,4},{7,5},{8,10},{9,11},{10,... | collective-permute-start | bytes 786440 | tf_op jit(solution)/shard_map/ppermute | solution.py:96
  27.2 21.4 %all-to-all-start = ((bf16[8,4,32,128]{3,2,1,0:T(8,128)(2,1)}), bf16[8,4,32,128]{3,2,1,0:T(8,128)(2,1)S(1)}, u32[]{:S(2)}, u32[]{:S(2)}) async-start(bf16[8,4,32,128]{3,2,1,0:T(8,128)(2,1)} %broadcast_in_dim.15), calls=%async_computation | async-start | bytes 524288 | tf_op jit(solution)/shard_map/all_to_all | solution.py:281
  34.0 10.6 %collective-permute-start.3 = (bf16[8,128,128]{2,1,0:T(8,128)(2,1)S(1)}, bf16[8,128,128]{2,1,0:T(8,128)(2,1)S(1)}, u32[]{:S(2)}, u32[]{:S(2)}) collective-permute-start(bf16[8,128,128]{2,1,0:T(8,128)(2,1)S(1)} %bitcast.48), channel_id=1, source_target_pairs={{0,1},{1,0},{2,3},{3,2},{4,5},{5,4},{6,7},{7,6},{8,9},{9,8},{10,11... | collective-permute-start | bytes 786440 | tf_op jit(solution)/shard_map/ppermute | solution.py:96
  38.8 5.8 %collective-permute-start.4 = (bf16[8,128,128]{2,1,0:T(8,128)(2,1)S(1)}, bf16[8,128,128]{2,1,0:T(8,128)(2,1)S(1)}, u32[]{:S(2)}, u32[]{:S(2)}) collective-permute-start(bf16[8,128,128]{2,1,0:T(8,128)(2,1)S(1)} %collective-permute-done.2.x_ref), channel_id=1, source_target_pairs={{0,1},{1,0},{2,3},{3,2},{4,5},{5,4},{6,7},{7,6},{8,9},{9,8},{10,11... | collective-permute-start | bytes 786440 | tf_op jit(solution)/shard_map/ppermute | solution.py:96
  48.6 30.1 %copy-start = (bf16[1,4,32,128]{3,2,1,0:T(8,128)(2,1)S(1)}, bf16[1,4,32,128]{3,2,1,0:T(8,128)(2,1)}, u32[]{:S(2)}) copy-start(bf16[1,4,32,128]{3,2,1,0:T(8,128)(2,1)} %param.7) | copy-start | bytes 98308
  48.6 32.6 %all-to-all-start.3 = ((bf16[16,4,32,128]{3,2,1,0:T(8,128)(2,1)}), bf16[16,4,32,128]{3,2,1,0:T(8,128)(2,1)S(1)}, u32[]{:S(2)}, u32[]{:S(2)}) async-start(bf16[16,4,32,128]{3,2,1,0:T(8,128)(2,1)} %bitcast.10), calls=%async_computation.3 | async-start | bytes 1048576 | tf_op jit(solution)/shard_map/all_to_all | solution.py:24
  57.9 15.6 %collective-permute-start = (bf16[8,4,32,128]{3,2,1,0:T(8,128)(2,1)S(1)}, bf16[8,4,32,128]{3,2,1,0:T(8,128)(2,1)S(1)}, u32[]{:S(2)}, u32[]{:S(2)}) collective-permute-start(bf16[8,4,32,128]{3,2,1,0:T(8,128)(2,1)S(1)} %all-to-all-done), channel_id=1, source_target_pairs={{0,256},{32,288},{64,320},{96,352},{128,384},{160,416},{192,448},{... | collective-permute-start | bytes 786440 | tf_op jit(solution)/shard_map/ppermute | solution.py:96
  73.5 11.2 %copy-start.1 = (bf16[4,128,128]{2,1,0:T(8,128)(2,1)S(1)}, bf16[4,128,128]{2,1,0:T(8,128)(2,1)}, u32[]{:S(2)}) copy-start(bf16[4,128,128]{2,1,0:T(8,128)(2,1)} %param.13) | copy-start | bytes 393220
  75.7 9.5 %copy-start.2 = (f32[128]{0:T(128)S(1)}, f32[128]{0:T(128)}, u32[]{:S(2)}) copy-start(f32[128]{0:T(128)} %param.11) | copy-start | bytes 1540
  75.7 9.5 %copy-start.3 = (f32[128]{0:T(128)S(1)}, f32[128]{0:T(128)}, u32[]{:S(2)}) copy-start(f32[128]{0:T(128)} %param.12) | copy-start | bytes 1540
  75.7 4.5 %collective-permute-start.1 = (bf16[16,128,128]{2,1,0:T(8,128)(2,1)S(1)}, bf16[16,128,128]{2,1,0:T(8,128)(2,1)S(1)}, u32[]{:S(2)}, u32[]{:S(2)}) collective-permute-start(bf16[16,128,128]{2,1,0:T(8,128)(2,1)S(1)} %get-tuple-element.13), channel_id=1, source_target_pairs={{0,1},{1,0},{2,3},{3,2},{4,5},{5,4},{6,7},{7,6},{8,9},{9,8},{10,11... | collective-permute-start | bytes 1572872 | tf_op jit(solution)/shard_map/ppermute | solution.py:96
  81.1 19.7 %all-to-all-start.1 = ((bf16[16,128,128]{2,1,0:T(8,128)(2,1)}), bf16[16,128,128]{2,1,0:T(8,128)(2,1)S(1)}, u32[]{:S(2)}, u32[]{:S(2)}) async-start(bf16[16,128,128]{2,1,0:T(8,128)(2,1)} %pair_sum.1), calls=%async_computation.1 | async-start | bytes 1048576 | tf_op jit(solution)/shard_map/all_to_all | solution.py:299

commit v11 on v10

--- a/solution.py
+++ b/solution.py
@@ -61,7 +61,7 @@
         - jnp.mean(scaled_grad, axis=-1, keepdims=True)
         - unit_pair * jnp.mean(scaled_grad * unit_pair, axis=-1, keepdims=True)
     )
-    return (pair_grad.astype(jnp.bfloat16), weight_part, norm_part)
+    return (pair_grad, weight_part, norm_part)
 
 
 def with_split_norm(part, rows):
@@ -74,7 +74,7 @@
     return jnp.concatenate([high, norm - high, jnp.zeros((4, norm.shape[1]), norm.dtype)], axis=0)
 
 
-def summed_over_all(weight_part, norm_part):
+def summed_over_all(weight_part, norm_part, pair_grad):
     cols = lax.axis_size("col")
     shape = weight_part.shape
     width = shape[-1]
@@ -87,8 +87,8 @@
     whole = sent_to_all(with_split_norm(part, rows), "row").astype(jnp.float32).sum(axis=0)
     chunk, sums = lax.optimization_barrier((whole[:rows].astype(jnp.bfloat16), whole[rows:]))
     weight_grad = sent_to_all(chunk, "col").reshape(-1, width)
-    weight_grad, norm_grad = final_sums(weight_grad, sums)
-    return weight_grad.reshape(shape), norm_grad
+    weight_grad, norm_grad, pair_grad = final_sums(weight_grad, sums, pair_grad)
+    return weight_grad.reshape(shape), norm_grad, pair_grad
 
 
 def exchanged(x, axis, step):
@@ -230,41 +230,67 @@
     )(*pieces, cot_turned)
 
 
+def spread_kernel(x_ref, out_ref, done):
+    copies = [
+        pltpu.make_async_copy(x_ref, out_ref.at[n], done.at[n]) for n in range(out_ref.shape[0])
+    ]
+    for copy in copies:
+        copy.start()
+    for copy in copies:
+        copy.wait()
+
+
+def spread(x, count):
+    anywhere = pl.BlockSpec(memory_space=pl.ANY)
+    return pl.pallas_call(
+        spread_kernel,
+        out_shape=jax.ShapeDtypeStruct((count, *x.shape), x.dtype),
+        in_specs=[anywhere],
+        out_specs=anywhere,
+        scratch_shapes=[pltpu.SemaphoreType.DMA((count,))],
+        compiler_params=pltpu.CompilerParams(vmem_limit_bytes=VMEM_LIMIT // 4),
+        name="spread",
+    )(x)
+
+
 def pair_kernel(kept_ref, came_ref, out_ref):
     total = kept_ref[...].astype(jnp.float32) + came_ref[...].astype(jnp.float32)
     out_ref[...] = total.astype(jnp.bfloat16)
 
 
 def pair_sum(kept, came):
-    here = pl.BlockSpec(memory_space=pltpu.VMEM)
+    block = pl.BlockSpec((kept.shape[0] // 4, *kept.shape[1:]), lambda i: (i, 0, 0))
     return pl.pallas_call(
         pair_kernel,
+        grid=(4,),
         out_shape=jax.ShapeDtypeStruct(kept.shape, kept.dtype),
-        in_specs=[here, here],
-        out_specs=here,
+        in_specs=[block, block],
+        out_specs=block,
         compiler_params=pltpu.CompilerParams(vmem_limit_bytes=VMEM_LIMIT // 4),
         name="pair_sum",
     )(kept, came)
 
 
-def final_kernel(weight_ref, sums_ref, weight_out, norm_out):
+def final_kernel(weight_ref, sums_ref, pair_ref, weight_out, norm_out, pair_out):
+    pair_out[...] = pair_ref[...].astype(jnp.bfloat16)
     weight_out[...] = weight_ref[...].astype(jnp.float32)
     norm_out[...] = sums_ref[0:2, :] + sums_ref[2:4, :]
 
 
-def final_sums(weight, sums):
+def final_sums(weight, sums, pair):
     here = pl.BlockSpec(memory_space=pltpu.VMEM)
     return pl.pallas_call(
         final_kernel,
         out_shape=(
             jax.ShapeDtypeStruct(weight.shape, jnp.float32),
             jax.ShapeDtypeStruct((2, sums.shape[1]), jnp.float32),
+            jax.ShapeDtypeStruct(pair.shape, jnp.bfloat16),
         ),
-        in_specs=[here, here],
-        out_specs=(here, here),
+        in_specs=[here, here, here],
+        out_specs=(here, here, here),
         compiler_params=pltpu.CompilerParams(vmem_limit_bytes=VMEM_LIMIT // 4),
         name="final_sums",
-    )(weight, sums)
+    )(weight, sums, pair)
 
 
 def all_steps(
@@ -277,7 +303,7 @@
     lines_y = [[x * (rows // 2) + y for y in range(rows // 2)] for x in range(2)]
     lines_z = [[z * 4 + k for z in range(cols // 4)] for k in range(4)]
     one_core = [[c for c in range(cols) if c % 2 == k] for k in range(2)]
-    right_near = jnp.broadcast_to(saved_right, (rows // 2, *saved_right.shape[1:]))
+    right_near = spread(saved_right[0], rows // 2)
     right_near = lax.all_to_all(
         right_near, "row", 0, 0, tiled=True, axis_index_groups=lines_y
     )
@@ -316,7 +342,7 @@
     pair_grad, weight_part, norm_part = lax.optimization_barrier(
         (pair_grad, weight_part, norm_part)
     )
-    weight_grad, norm_grad = summed_over_all(weight_part, norm_part)
+    weight_grad, norm_grad, pair_grad = summed_over_all(weight_part, norm_part, pair_grad)
     return (pair_grad.reshape(pair_window.shape), weight_grad, norm_grad)
 
 

time: 151 us -> 151 us (level)
  transfers between devices with their start and end apart: 8 -> 8, of which waited for: 3 -> 3; matrix products, arithmetic and copies ran while one was open for 4% -> 3% of each run, Pallas kernels for 5% -> 6%
where the time goes in v11:
time: 151 us; the launch traced here: 150 us
  blocking collectives  67.5 us (45%)
  starting transfers between devices  37.3 us (25%)
  waiting for transfers between devices  27.5 us (18%)
  Pallas kernels  9 us (6%)
  local copies, waits for them, and re-layouts  5.88 us (4%)
    all_to_all x2, blocking collectives, sent_to_all(): lax.all_to_all(jnp.broadcast_to(x[None], (devices, *x.shape)), axis, 0, 0...  30.5 us
    all_to_all x1, blocking collectives, all_steps(): lax.all_to_all(own, 'col', 0, 0, tiled=True, axis_index_groups=lines_z)  21.1 us
    ppermute x5, starting transfers between devices, exchanged(): return lax.ppermute(x, axis, [(d, d ^ step) for d in range(devices)])  17.5 us
    all_to_all x1, blocking collectives, summed_over_all(): arrived = lax.all_to_all(packed, 'col', 0, 0, tiled=True)  15.8 us
    all_to_all x1, waiting for transfers between devices, all_steps(): lax.all_to_all(chip_part, 'col', 0, 0, tiled=True, axis_index_groups=one_...  15.2 us
    ppermute x5, waiting for transfers between devices, exchanged(): return lax.ppermute(x, axis, [(d, d ^ step) for d in range(devices)])  12.3 us
    all_to_all x1, starting transfers between devices, sent_and_summed(): lax.all_to_all(parts, axis, split_axis=0, concat_axis=0, tiled=True)  9.33 us
    all_to_all x1, starting transfers between devices, all_steps(): lax.all_to_all(right_near, 'row', 0, 0, tiled=True, axis_index_groups=lin...  6.83 us
  transfers between devices with their start and end apart: 8, of which 3 were waited for; matrix products, arithmetic and copies ran while one was open for 3% of the time, Pallas kernels for 6%

profile of v11, /device:TPU:1, one launch (start us, length us, event | category | flops | bytes accessed | tf_op | source)
XLA Modules:
  0.0 149.6 jit_solution(16435359231876107303)
XLA Ops:
  0.6 0.8 broadcast_in_dim.11
  1.4 21.1 %all_to_all.35 = bf16[8,4,32,128]{3,2,1,0:T(8,128)(2,1)S(1)} all-to-all(bf16[8,4,32,128]{3,2,1,0:T(8,128)(2,1)S(1)} %broadcast_in_dim.11), channel_id=1, replica_groups={{0,4,8,12,16,20,24,28},{1,5,9,13,17,21,25,29},{2,6,10,14,18,22,26,30},{..., dimensions={0} | all-to-all | bytes 524288 | tf_op jit(solution)/shard_map/all_to_all | solution.py:317
  22.6 3.1 %collective-permute-start.2 = (bf16[8,128,128]{2,1,0:T(8,128)(2,1)S(1)}, bf16[8,128,128]{2,1,0:T(8,128)(2,1)S(1)}, u32[]{:S(2)}, u32[]{:S(2)}) collective-permute-start(bf16[8,128,128]{2,1,0:T(8,128)(2,1)S(1)} %bitcast.47), channel_id=1, source_target_pairs={{0,2},{1,3},{2,0},{3,1},{4,6},{5,7},{6,4},{7,5},{8,10},{9,11},{10,... | collective-permute-start | bytes 786440 | tf_op jit(solution)/shard_map/ppermute | solution.py:96
  25.7 0.0 copy-start
  25.7 0.7 copy-done
  26.5 0.8 spread.1
  27.2 6.8 %all-to-all-start = ((bf16[8,4,32,128]{3,2,1,0:T(8,128)(2,1)}), bf16[8,4,32,128]{3,2,1,0:T(8,128)(2,1)S(1)}, u32[]{:S(2)}, u32[]{:S(2)}) async-start(bf16[8,4,32,128]{3,2,1,0:T(8,128)(2,1)} %spread.1), calls=%async_computation | async-start | bytes 524288 | tf_op jit(solution)/shard_map/all_to_all | solution.py:307
  34.1 4.8 %collective-permute-start.3 = (bf16[8,128,128]{2,1,0:T(8,128)(2,1)S(1)}, bf16[8,128,128]{2,1,0:T(8,128)(2,1)S(1)}, u32[]{:S(2)}, u32[]{:S(2)}) collective-permute-start(bf16[8,128,128]{2,1,0:T(8,128)(2,1)S(1)} %bitcast.48), channel_id=1, source_target_pairs={{0,1},{1,0},{2,3},{3,2},{4,5},{5,4},{6,7},{7,6},{8,9},{9,8},{10,11... | collective-permute-start | bytes 786440 | tf_op jit(solution)/shard_map/ppermute | solution.py:96
  38.9 0.0 collective-permute-done.2.x_ref
  38.9 1.9 %collective-permute-start.4 = (bf16[8,128,128]{2,1,0:T(8,128)(2,1)S(1)}, bf16[8,128,128]{2,1,0:T(8,128)(2,1)S(1)}, u32[]{:S(2)}, u32[]{:S(2)}) collective-permute-start(bf16[8,128,128]{2,1,0:T(8,128)(2,1)S(1)} %collective-permute-done.2.x_ref), channel_id=1, source_target_pairs={{0,1},{1,0},{2,3},{3,2},{4,5},{5,4},{6,7},{7,6},{8,9},{9,8},{10,11... | collective-permute-start | bytes 786440 | tf_op jit(solution)/shard_map/ppermute | solution.py:96
  40.8 3.8 %copy.17 = bf16[128,64,128]{0,1,2:T(8,128)(2,1)S(1)} copy(bf16[128,64,128]{2,1,0:T(8,128)(2,1)} %bitcast.54) | data formatting | bytes 4194304 | tf_op jit(solution)/shard_map/reshape | solution.py:313
  44.6 0.0 collective-permute-done.3.core_ref
  44.7 0.0 collective-permute-done.4.both_ref
  44.7 3.9 %right_parts.1 = bf16[2048,128]{1,0:T(8,128)(2,1)} custom-call(bf16[8,128,128]{2,1,0:T(8,128)(2,1)S(1)} %bitcast.49, bf16[8,128,128]{2,1,0:T(8,128)(2,1)S(1)} %collective-permute-done.2.x_ref, bf16[8,128,128]{2,1,0:T(8,128)(2,1)S(1)} %collective-permute-done.3.core_ref, bf16[8,128,128]{2,1,0:T(8,128)(2,1)S(1)} %collective-permute-done.4.both_ref, ...), custom_call_target="tpu_custom_call" | custom-call | tf_op jit(solution)/shard_map/right_parts/pallas_call | solution.py:217
  48.6 0.0 all-to-all-done
  48.6 9.3 %all-to-all-start.3 = ((bf16[16,4,32,128]{3,2,1,0:T(8,128)(2,1)}), bf16[16,4,32,128]{3,2,1,0:T(8,128)(2,1)S(1)}, u32[]{:S(2)}, u32[]{:S(2)}) async-start(bf16[16,4,32,128]{3,2,1,0:T(8,128)(2,1)} %bitcast.10), calls=%async_computation.3 | async-start | bytes 1048576 | tf_op jit(solution)/shard_map/all_to_all | solution.py:24
  57.9 4.8 %collective-permute-start = (bf16[8,4,32,128]{3,2,1,0:T(8,128)(2,1)S(1)}, bf16[8,4,32,128]{3,2,1,0:T(8,128)(2,1)S(1)}, u32[]{:S(2)}, u32[]{:S(2)}) collective-permute-start(bf16[8,4,32,128]{3,2,1,0:T(8,128)(2,1)S(1)} %all-to-all-done), channel_id=1, source_target_pairs={{0,256},{32,288},{64,320},{96,352},{128,384},{160,416},{192,448},{... | collective-permute-start | bytes 786440 | tf_op jit(solution)/shard_map/ppermute | solution.py:96
  62.7 10.9 %collective-permute-done = bf16[8,4,32,128]{3,2,1,0:T(8,128)(2,1)S(1)} collective-permute-done((bf16[8,4,32,128]{3,2,1,0:T(8,128)(2,1)S(1)}, bf16[8,4,32,128]{3,2,1,0:T(8,128)(2,1)S(1)}, u32[]{:S(2)}, u32[]{:S(2)}) %collective-permute-start) | collective-permute-done | bytes 262176 | tf_op jit(solution)/shard_map/ppermute | solution.py:96
  73.6 2.2 %left_parts.1 = (bf16[16,128,128]{2,1,0:T(8,128)(2,1)S(1)}, bf16[16,128,128]{2,1,0:T(8,128)(2,1)S(1)}) custom-call(bf16[1024,128]{1,0:T(8,128)(2,1)S(1)} %bitcast.50, bf16[1024,128]{1,0:T(8,128)(2,1)S(1)} %bitcast.52, bf16[128,64,128]{2,1,0:T(8,128)(2,1)S(1)} %bitcast.46), custom_call_target="tpu_custom_call" | custom-call | tf_op jit(solution)/shard_map/left_parts/pallas_call | solution.py:160
  75.7 0.0 copy-start.3
  75.7 0.0 copy-start.4
  75.8 2.9 %collective-permute-start.1 = (bf16[16,128,128]{2,1,0:T(8,128)(2,1)S(1)}, bf16[16,128,128]{2,1,0:T(8,128)(2,1)S(1)}, u32[]{:S(2)}, u32[]{:S(2)}) collective-permute-start(bf16[16,128,128]{2,1,0:T(8,128)(2,1)S(1)} %get-tuple-element.14), channel_id=1, source_target_pairs={{0,1},{1,0},{2,3},{3,2},{4,5},{5,4},{6,7},{7,6},{8,9},{9,8},{10,11... | collective-permute-start | bytes 1572872 | tf_op jit(solution)/shard_map/ppermute | solution.py:96
  78.7 0.0 copy-done.1
  78.7 0.1 convert_reduce_fusion.4
  78.8 1.4 collective-permute-done.1.came_ref
  80.2 1.4 pair_sum.1
  81.7 0.0 all-to-all-done.3
  81.7 3.6 %all-to-all-start.1 = ((bf16[16,128,128]{2,1,0:T(8,128)(2,1)}), bf16[16,128,128]{2,1,0:T(8,128)(2,1)S(1)}, u32[]{:S(2)}, u32[]{:S(2)}) async-start(bf16[16,128,128]{2,1,0:T(8,128)(2,1)} %pair_sum.1), calls=%async_computation.1 | async-start | bytes 1048576 | tf_op jit(solution)/shard_map/all_to_all | solution.py:325
  85.2 0.0 copy-done.2
  85.3 0.1 copy.18
  85.4 0.1 div.25
  85.5 0.2 multiply_reduce_fusion.2
  85.7 0.1 rsqrt.13
  85.7 0.0 copy-done.3
  85.7 0.1 add_convert_fusion
  85.9 0.2 fusion.19
  86.1 0.1 convert_reduce_fusion
  86.1 15.2 %all-to-all-done.1 = bf16[16,128,128]{2,1,0:T(8,128)(2,1)S(1)} async-done(((bf16[16,128,128]{2,1,0:T(8,128)(2,1)}), bf16[16,128,128]{2,1,0:T(8,128)(2,1)S(1)}, u32[]{:S(2)}, u32[]{:S(2)}) %all-to-all-start.1) | async-done | bytes 524320 | tf_op jit(solution)/shard_map/all_to_all | solution.py:325
  101.3 0.1 convert_reduce_fusion.1
  101.4 0.1 fusion.11
  101.5 0.1 copy.23
  101.6 0.3 multiply_reduce_fusion
  101.9 0.2 convolution_bitcast_fusion
  102.2 0.1 subtract_multiply_fusion.pair_ref
  102.4 15.8 %all_to_all.36 = bf16[32,24,128]{2,1,0:T(8,128)(2,1)S(1)} all-to-all(bf16[32,24,128]{2,1,0:T(8,128)(2,1)S(1)} %pad_maximum_fusion), channel_id=1, replica_groups=mesh['row'=16,'col'=32] {'col'}, dimensions={0} | all-to-all | bytes 393216 | tf_op jit(solution)/shard_map/all_to_all | solution.py:85
  118.3 16.3 %all_to_all.37 = bf16[16,24,128]{2,1,0:T(8,128)(2,1)S(1)} all-to-all(bf16[16,24,128]{2,1,0:T(8,128)(2,1)S(1)} %broadcast_in_dim.13), channel_id=1, replica_groups=mesh['row'=16,'col'=32] {'row'}, dimensions={0} | all-to-all | bytes 196608 | tf_op jit(solution)/shard_map/all_to_all | solution.py:13
  134.7 14.2 %all_to_all.38 = bf16[32,16,128]{2,1,0:T(8,128)(2,1)S(1)} all-to-all(bf16[32,16,128]{2,1,0:T(8,128)(2,1)S(1)} %broadcast_in_dim.14), channel_id=1, replica_groups=mesh['row'=16,'col'=32] {'col'}, dimensions={0} | all-to-all | bytes 262144 | tf_op jit(solution)/shard_map/all_to_all | solution.py:13
  148.9 0.7 final_sums.1
  (22 shorter events, 0.2 us)
Async XLA Ops:
  22.6 16.3 %collective-permute-start.2 = (bf16[8,128,128]{2,1,0:T(8,128)(2,1)S(1)}, bf16[8,128,128]{2,1,0:T(8,128)(2,1)S(1)}, u32[]{:S(2)}, u32[]{:S(2)}) collective-permute-start(bf16[8,128,128]{2,1,0:T(8,128)(2,1)S(1)} %bitcast.47), channel_id=1, source_target_pairs={{0,2},{1,3},{2,0},{3,1},{4,6},{5,7},{6,4},{7,5},{8,10},{9,11},{10,... | collective-permute-start | bytes 786440 | tf_op jit(solution)/shard_map/ppermute | solution.py:96
  25.7 0.8 copy-start
  27.2 21.4 %all-to-all-start = ((bf16[8,4,32,128]{3,2,1,0:T(8,128)(2,1)}), bf16[8,4,32,128]{3,2,1,0:T(8,128)(2,1)S(1)}, u32[]{:S(2)}, u32[]{:S(2)}) async-start(bf16[8,4,32,128]{3,2,1,0:T(8,128)(2,1)} %spread.1), calls=%async_computation | async-start | bytes 524288 | tf_op jit(solution)/shard_map/all_to_all | solution.py:307
  34.1 10.6 %collective-permute-start.3 = (bf16[8,128,128]{2,1,0:T(8,128)(2,1)S(1)}, bf16[8,128,128]{2,1,0:T(8,128)(2,1)S(1)}, u32[]{:S(2)}, u32[]{:S(2)}) collective-permute-start(bf16[8,128,128]{2,1,0:T(8,128)(2,1)S(1)} %bitcast.48), channel_id=1, source_target_pairs={{0,1},{1,0},{2,3},{3,2},{4,5},{5,4},{6,7},{7,6},{8,9},{9,8},{10,11... | collective-permute-start | bytes 786440 | tf_op jit(solution)/shard_map/ppermute | solution.py:96
  38.9 5.8 %collective-permute-start.4 = (bf16[8,128,128]{2,1,0:T(8,128)(2,1)S(1)}, bf16[8,128,128]{2,1,0:T(8,128)(2,1)S(1)}, u32[]{:S(2)}, u32[]{:S(2)}) collective-permute-start(bf16[8,128,128]{2,1,0:T(8,128)(2,1)S(1)} %collective-permute-done.2.x_ref), channel_id=1, source_target_pairs={{0,1},{1,0},{2,3},{3,2},{4,5},{5,4},{6,7},{7,6},{8,9},{9,8},{10,11... | collective-permute-start | bytes 786440 | tf_op jit(solution)/shard_map/ppermute | solution.py:96
  48.6 30.1 %copy-start.1 = (bf16[1,4,32,128]{3,2,1,0:T(8,128)(2,1)S(1)}, bf16[1,4,32,128]{3,2,1,0:T(8,128)(2,1)}, u32[]{:S(2)}) copy-start(bf16[1,4,32,128]{3,2,1,0:T(8,128)(2,1)} %param.7) | copy-start | bytes 98308
  48.6 33.1 %all-to-all-start.3 = ((bf16[16,4,32,128]{3,2,1,0:T(8,128)(2,1)}), bf16[16,4,32,128]{3,2,1,0:T(8,128)(2,1)S(1)}, u32[]{:S(2)}, u32[]{:S(2)}) async-start(bf16[16,4,32,128]{3,2,1,0:T(8,128)(2,1)} %bitcast.10), calls=%async_computation.3 | async-start | bytes 1048576 | tf_op jit(solution)/shard_map/all_to_all | solution.py:24
  57.9 15.6 %collective-permute-start = (bf16[8,4,32,128]{3,2,1,0:T(8,128)(2,1)S(1)}, bf16[8,4,32,128]{3,2,1,0:T(8,128)(2,1)S(1)}, u32[]{:S(2)}, u32[]{:S(2)}) collective-permute-start(bf16[8,4,32,128]{3,2,1,0:T(8,128)(2,1)S(1)} %all-to-all-done), channel_id=1, source_target_pairs={{0,256},{32,288},{64,320},{96,352},{128,384},{160,416},{192,448},{... | collective-permute-start | bytes 786440 | tf_op jit(solution)/shard_map/ppermute | solution.py:96
  73.6 11.7 %copy-start.2 = (bf16[4,128,128]{2,1,0:T(8,128)(2,1)S(1)}, bf16[4,128,128]{2,1,0:T(8,128)(2,1)}, u32[]{:S(2)}) copy-start(bf16[4,128,128]{2,1,0:T(8,128)(2,1)} %param.13) | copy-start | bytes 393220
  75.7 10.0 %copy-start.3 = (f32[128]{0:T(128)S(1)}, f32[128]{0:T(128)}, u32[]{:S(2)}) copy-start(f32[128]{0:T(128)} %param.11) | copy-start | bytes 1540
  75.7 10.0 %copy-start.4 = (f32[128]{0:T(128)S(1)}, f32[128]{0:T(128)}, u32[]{:S(2)}) copy-start(f32[128]{0:T(128)} %param.12) | copy-start | bytes 1540
  75.8 4.5 %collective-permute-start.1 = (bf16[16,128,128]{2,1,0:T(8,128)(2,1)S(1)}, bf16[16,128,128]{2,1,0:T(8,128)(2,1)S(1)}, u32[]{:S(2)}, u32[]{:S(2)}) collective-permute-start(bf16[16,128,128]{2,1,0:T(8,128)(2,1)S(1)} %get-tuple-element.14), channel_id=1, source_target_pairs={{0,1},{1,0},{2,3},{3,2},{4,5},{5,4},{6,7},{7,6},{8,9},{9,8},{10,11... | collective-permute-start | bytes 1572872 | tf_op jit(solution)/shard_map/ppermute | solution.py:96
  81.7 19.7 %all-to-all-start.1 = ((bf16[16,128,128]{2,1,0:T(8,128)(2,1)}), bf16[16,128,128]{2,1,0:T(8,128)(2,1)S(1)}, u32[]{:S(2)}, u32[]{:S(2)}) async-start(bf16[16,128,128]{2,1,0:T(8,128)(2,1)} %pair_sum.1), calls=%async_computation.1 | async-start | bytes 1048576 | tf_op jit(solution)/shard_map/all_to_all | solution.py:325

commit v12 on v11

--- a/solution.py
+++ b/solution.py
@@ -230,42 +230,42 @@
     )(*pieces, cot_turned)
 
 
-def spread_kernel(x_ref, out_ref, done):
-    copies = [
-        pltpu.make_async_copy(x_ref, out_ref.at[n], done.at[n]) for n in range(out_ref.shape[0])
+def pair_kernel(kept_ref, came_hbm, out_hbm, came, out, arrived, left):
+    blocks = arrived.shape[0]
+    size = kept_ref.shape[0] // blocks
+    parts = [pl.ds(n * size, size) for n in range(blocks)]
+    incoming = [
+        pltpu.make_async_copy(came_hbm.at[part], came.at[part], arrived.at[n])
+        for n, part in enumerate(parts)
     ]
-    for copy in copies:
+    outgoing = [
+        pltpu.make_async_copy(out.at[part], out_hbm.at[part], left.at[n])
+        for n, part in enumerate(parts)
+    ]
+    for copy in incoming:
         copy.start()
-    for copy in copies:
+    for n, part in enumerate(parts):
+        incoming[n].wait()
+        total = kept_ref[part].astype(jnp.float32) + came[part].astype(jnp.float32)
+        out[part] = total.astype(jnp.bfloat16)
+        outgoing[n].start()
+    for copy in outgoing:
         copy.wait()
 
 
-def spread(x, count):
-    anywhere = pl.BlockSpec(memory_space=pl.ANY)
-    return pl.pallas_call(
-        spread_kernel,
-        out_shape=jax.ShapeDtypeStruct((count, *x.shape), x.dtype),
-        in_specs=[anywhere],
-        out_specs=anywhere,
-        scratch_shapes=[pltpu.SemaphoreType.DMA((count,))],
-        compiler_params=pltpu.CompilerParams(vmem_limit_bytes=VMEM_LIMIT // 4),
-        name="spread",
-    )(x)
-
-
-def pair_kernel(kept_ref, came_ref, out_ref):
-    total = kept_ref[...].astype(jnp.float32) + came_ref[...].astype(jnp.float32)
-    out_ref[...] = total.astype(jnp.bfloat16)
-
-
 def pair_sum(kept, came):
-    block = pl.BlockSpec((kept.shape[0] // 4, *kept.shape[1:]), lambda i: (i, 0, 0))
+    here, anywhere = pl.BlockSpec(memory_space=pltpu.VMEM), pl.BlockSpec(memory_space=pl.ANY)
     return pl.pallas_call(
         pair_kernel,
-        grid=(4,),
         out_shape=jax.ShapeDtypeStruct(kept.shape, kept.dtype),
-        in_specs=[block, block],
-        out_specs=block,
+        in_specs=[here, anywhere],
+        out_specs=anywhere,
+        scratch_shapes=[
+            pltpu.VMEM(kept.shape, kept.dtype),
+            pltpu.VMEM(kept.shape, kept.dtype),
+            pltpu.SemaphoreType.DMA((4,)),
+            pltpu.SemaphoreType.DMA((4,)),
+        ],
         compiler_params=pltpu.CompilerParams(vmem_limit_bytes=VMEM_LIMIT // 4),
         name="pair_sum",
     )(kept, came)
@@ -303,7 +303,7 @@
     lines_y = [[x * (rows // 2) + y for y in range(rows // 2)] for x in range(2)]
     lines_z = [[z * 4 + k for z in range(cols // 4)] for k in range(4)]
     one_core = [[c for c in range(cols) if c % 2 == k] for k in range(2)]
-    right_near = spread(saved_right[0], rows // 2)
+    right_near = jnp.broadcast_to(saved_right, (rows // 2, *saved_right.shape[1:]))
     right_near = lax.all_to_all(
         right_near, "row", 0, 0, tiled=True, axis_index_groups=lines_y
     )

time: 151 us -> 151 us (level)
  transfers between devices with their start and end apart: 8 -> 8, of which waited for: 3 -> 3; matrix products, arithmetic and copies ran while one was open for 3% -> 4% of each run, Pallas kernels for 6% -> 5%
where the time goes in v12:
time: 151 us; the launch traced here: 150 us
  blocking collectives  67.5 us (45%)
  starting transfers between devices  37.3 us (25%)
  waiting for transfers between devices  27.5 us (18%)
  Pallas kernels  8.35 us (6%)
  local copies, waits for them, and re-layouts  6.63 us (4%)
    all_to_all x2, blocking collectives, sent_to_all(): lax.all_to_all(jnp.broadcast_to(x[None], (devices, *x.shape)), axis, 0, 0...  30.5 us
    all_to_all x1, blocking collectives, all_steps(): lax.all_to_all(own, 'col', 0, 0, tiled=True, axis_index_groups=lines_z)  21.1 us
    ppermute x5, starting transfers between devices, exchanged(): return lax.ppermute(x, axis, [(d, d ^ step) for d in range(devices)])  17.5 us
    all_to_all x1, blocking collectives, summed_over_all(): arrived = lax.all_to_all(packed, 'col', 0, 0, tiled=True)  15.8 us
    all_to_all x1, waiting for transfers between devices, all_steps(): lax.all_to_all(chip_part, 'col', 0, 0, tiled=True, axis_index_groups=one_...  15.2 us
    ppermute x5, waiting for transfers between devices, exchanged(): return lax.ppermute(x, axis, [(d, d ^ step) for d in range(devices)])  12.3 us
    all_to_all x1, starting transfers between devices, sent_and_summed(): lax.all_to_all(parts, axis, split_axis=0, concat_axis=0, tiled=True)  9.33 us
    all_to_all x1, starting transfers between devices, all_steps(): lax.all_to_all(right_near, 'row', 0, 0, tiled=True, axis_index_groups=lin...  6.82 us
  transfers between devices with their start and end apart: 8, of which 3 were waited for; matrix products, arithmetic and copies ran while one was open for 4% of the time, Pallas kernels for 5%

profile of v12, /device:TPU:1, one launch (start us, length us, event | category | flops | bytes accessed | tf_op | source)
XLA Modules:
  0.0 149.7 jit_solution(14316888926744850798)
XLA Ops:
  0.6 0.8 broadcast_in_dim.17
  1.4 21.1 %all_to_all.35 = bf16[8,4,32,128]{3,2,1,0:T(8,128)(2,1)S(1)} all-to-all(bf16[8,4,32,128]{3,2,1,0:T(8,128)(2,1)S(1)} %broadcast_in_dim.17), channel_id=1, replica_groups={{0,4,8,12,16,20,24,28},{1,5,9,13,17,21,25,29},{2,6,10,14,18,22,26,30},{..., dimensions={0} | all-to-all | bytes 524288 | tf_op jit(solution)/shard_map/all_to_all | solution.py:317
  22.6 3.1 %collective-permute-start.2 = (bf16[8,128,128]{2,1,0:T(8,128)(2,1)S(1)}, bf16[8,128,128]{2,1,0:T(8,128)(2,1)S(1)}, u32[]{:S(2)}, u32[]{:S(2)}) collective-permute-start(bf16[8,128,128]{2,1,0:T(8,128)(2,1)S(1)} %bitcast.47), channel_id=1, source_target_pairs={{0,2},{1,3},{2,0},{3,1},{4,6},{5,7},{6,4},{7,5},{8,10},{9,11},{10,... | collective-permute-start | bytes 786440 | tf_op jit(solution)/shard_map/ppermute | solution.py:96
  25.7 1.5 %broadcast_in_dim.15 = bf16[8,4,32,128]{3,2,1,0:T(8,128)(2,1)} broadcast(bf16[4,32,128]{2,1,0:T(8,128)(2,1)} %bitcast.61), dimensions={1,2,3} | broadcast | bytes 294912 | tf_op jit(solution)/shard_map/broadcast_in_dim | solution.py:306
  27.2 6.8 %all-to-all-start = ((bf16[8,4,32,128]{3,2,1,0:T(8,128)(2,1)}), bf16[8,4,32,128]{3,2,1,0:T(8,128)(2,1)S(1)}, u32[]{:S(2)}, u32[]{:S(2)}) async-start(bf16[8,4,32,128]{3,2,1,0:T(8,128)(2,1)} %broadcast_in_dim.15), calls=%async_computation | async-start | bytes 524288 | tf_op jit(solution)/shard_map/all_to_all | solution.py:307
  34.0 4.8 %collective-permute-start.3 = (bf16[8,128,128]{2,1,0:T(8,128)(2,1)S(1)}, bf16[8,128,128]{2,1,0:T(8,128)(2,1)S(1)}, u32[]{:S(2)}, u32[]{:S(2)}) collective-permute-start(bf16[8,128,128]{2,1,0:T(8,128)(2,1)S(1)} %bitcast.48), channel_id=1, source_target_pairs={{0,1},{1,0},{2,3},{3,2},{4,5},{5,4},{6,7},{7,6},{8,9},{9,8},{10,11... | collective-permute-start | bytes 786440 | tf_op jit(solution)/shard_map/ppermute | solution.py:96
  38.8 0.0 collective-permute-done.2.x_ref
  38.8 1.9 %collective-permute-start.4 = (bf16[8,128,128]{2,1,0:T(8,128)(2,1)S(1)}, bf16[8,128,128]{2,1,0:T(8,128)(2,1)S(1)}, u32[]{:S(2)}, u32[]{:S(2)}) collective-permute-start(bf16[8,128,128]{2,1,0:T(8,128)(2,1)S(1)} %collective-permute-done.2.x_ref), channel_id=1, source_target_pairs={{0,1},{1,0},{2,3},{3,2},{4,5},{5,4},{6,7},{7,6},{8,9},{9,8},{10,11... | collective-permute-start | bytes 786440 | tf_op jit(solution)/shard_map/ppermute | solution.py:96
  40.8 3.8 %copy.17 = bf16[128,64,128]{0,1,2:T(8,128)(2,1)S(1)} copy(bf16[128,64,128]{2,1,0:T(8,128)(2,1)} %bitcast.53) | data formatting | bytes 4194304 | tf_op jit(solution)/shard_map/reshape | solution.py:313
  44.6 0.0 collective-permute-done.3.core_ref
  44.6 0.0 collective-permute-done.4.both_ref
  44.6 3.9 %right_parts.1 = bf16[2048,128]{1,0:T(8,128)(2,1)} custom-call(bf16[8,128,128]{2,1,0:T(8,128)(2,1)S(1)} %bitcast.49, bf16[8,128,128]{2,1,0:T(8,128)(2,1)S(1)} %collective-permute-done.2.x_ref, bf16[8,128,128]{2,1,0:T(8,128)(2,1)S(1)} %collective-permute-done.3.core_ref, bf16[8,128,128]{2,1,0:T(8,128)(2,1)S(1)} %collective-permute-done.4.both_ref, ...), custom_call_target="tpu_custom_call" | custom-call | tf_op jit(solution)/shard_map/right_parts/pallas_call | solution.py:217
  48.6 0.0 copy-start
  48.6 0.0 all-to-all-done
  48.6 9.3 %all-to-all-start.3 = ((bf16[16,4,32,128]{3,2,1,0:T(8,128)(2,1)}), bf16[16,4,32,128]{3,2,1,0:T(8,128)(2,1)S(1)}, u32[]{:S(2)}, u32[]{:S(2)}) async-start(bf16[16,4,32,128]{3,2,1,0:T(8,128)(2,1)} %bitcast.10), calls=%async_computation.3 | async-start | bytes 1048576 | tf_op jit(solution)/shard_map/all_to_all | solution.py:24
  57.9 4.8 %collective-permute-start = (bf16[8,4,32,128]{3,2,1,0:T(8,128)(2,1)S(1)}, bf16[8,4,32,128]{3,2,1,0:T(8,128)(2,1)S(1)}, u32[]{:S(2)}, u32[]{:S(2)}) collective-permute-start(bf16[8,4,32,128]{3,2,1,0:T(8,128)(2,1)S(1)} %all-to-all-done), channel_id=1, source_target_pairs={{0,256},{32,288},{64,320},{96,352},{128,384},{160,416},{192,448},{... | collective-permute-start | bytes 786440 | tf_op jit(solution)/shard_map/ppermute | solution.py:96
  62.7 10.9 %collective-permute-done = bf16[8,4,32,128]{3,2,1,0:T(8,128)(2,1)S(1)} collective-permute-done((bf16[8,4,32,128]{3,2,1,0:T(8,128)(2,1)S(1)}, bf16[8,4,32,128]{3,2,1,0:T(8,128)(2,1)S(1)}, u32[]{:S(2)}, u32[]{:S(2)}) %collective-permute-start) | collective-permute-done | bytes 262176 | tf_op jit(solution)/shard_map/ppermute | solution.py:96
  73.5 2.2 %left_parts.1 = (bf16[16,128,128]{2,1,0:T(8,128)(2,1)S(1)}, bf16[16,128,128]{2,1,0:T(8,128)(2,1)S(1)}) custom-call(bf16[1024,128]{1,0:T(8,128)(2,1)S(1)} %bitcast.50, bf16[1024,128]{1,0:T(8,128)(2,1)S(1)} %bitcast.52, bf16[128,64,128]{2,1,0:T(8,128)(2,1)S(1)} %bitcast.46), custom_call_target="tpu_custom_call" | custom-call | tf_op jit(solution)/shard_map/left_parts/pallas_call | solution.py:160
  75.7 0.0 copy-start.2
  75.7 0.0 copy-start.3
  75.7 2.9 %collective-permute-start.1 = (bf16[16,128,128]{2,1,0:T(8,128)(2,1)S(1)}, bf16[16,128,128]{2,1,0:T(8,128)(2,1)S(1)}, u32[]{:S(2)}, u32[]{:S(2)}) collective-permute-start(bf16[16,128,128]{2,1,0:T(8,128)(2,1)S(1)} %get-tuple-element.14), channel_id=1, source_target_pairs={{0,1},{1,0},{2,3},{3,2},{4,5},{5,4},{6,7},{7,6},{8,9},{9,8},{10,11... | collective-permute-start | bytes 1572872 | tf_op jit(solution)/shard_map/ppermute | solution.py:96
  78.7 0.0 copy-done
  78.7 0.1 convert_reduce_fusion.4
  78.8 1.4 collective-permute-done.1.came_hbm
  80.2 1.5 %pair_sum.1 = bf16[16,128,128]{2,1,0:T(8,128)(2,1)} custom-call(bf16[16,128,128]{2,1,0:T(8,128)(2,1)S(1)} %get-tuple-element.13.kept_ref, bf16[16,128,128]{2,1,0:T(8,128)(2,1)S(1)} %collective-permute-done.1.came_hbm), custom_call_target="tpu_custom_call" | custom-call | tf_op jit(solution)/shard_map/pair_sum/pallas_call | solution.py:258
  81.7 0.0 all-to-all-done.3
  81.7 3.6 %all-to-all-start.1 = ((bf16[16,128,128]{2,1,0:T(8,128)(2,1)}), bf16[16,128,128]{2,1,0:T(8,128)(2,1)S(1)}, u32[]{:S(2)}, u32[]{:S(2)}) async-start(bf16[16,128,128]{2,1,0:T(8,128)(2,1)} %pair_sum.1), calls=%async_computation.1 | async-start | bytes 1048576 | tf_op jit(solution)/shard_map/all_to_all | solution.py:325
  85.4 0.0 copy-done.1
  85.4 0.1 copy.18
  85.5 0.1 div.25
  85.6 0.2 multiply_reduce_fusion.2
  85.8 0.1 rsqrt.13
  85.8 0.0 copy-done.2
  85.8 0.0 copy-done.3
  85.8 0.1 add_convert_fusion
  86.0 0.2 fusion.19
  86.2 0.1 convert_reduce_fusion
  86.2 15.2 %all-to-all-done.1 = bf16[16,128,128]{2,1,0:T(8,128)(2,1)S(1)} async-done(((bf16[16,128,128]{2,1,0:T(8,128)(2,1)}), bf16[16,128,128]{2,1,0:T(8,128)(2,1)S(1)}, u32[]{:S(2)}, u32[]{:S(2)}) %all-to-all-start.1) | async-done | bytes 524320 | tf_op jit(solution)/shard_map/all_to_all | solution.py:325
  101.4 0.1 convert_reduce_fusion.1
  101.5 0.1 fusion.11
  101.6 0.1 copy.23
  101.8 0.3 multiply_reduce_fusion
  102.0 0.2 convolution_bitcast_fusion
  102.3 0.1 subtract_multiply_fusion.pair_ref
  102.5 15.8 %all_to_all.36 = bf16[32,24,128]{2,1,0:T(8,128)(2,1)S(1)} all-to-all(bf16[32,24,128]{2,1,0:T(8,128)(2,1)S(1)} %pad_maximum_fusion), channel_id=1, replica_groups=mesh['row'=16,'col'=32] {'col'}, dimensions={0} | all-to-all | bytes 393216 | tf_op jit(solution)/shard_map/all_to_all | solution.py:85
  118.4 16.3 %all_to_all.37 = bf16[16,24,128]{2,1,0:T(8,128)(2,1)S(1)} all-to-all(bf16[16,24,128]{2,1,0:T(8,128)(2,1)S(1)} %broadcast_in_dim.19), channel_id=1, replica_groups=mesh['row'=16,'col'=32] {'row'}, dimensions={0} | all-to-all | bytes 196608 | tf_op jit(solution)/shard_map/all_to_all | solution.py:13
  134.8 14.2 %all_to_all.38 = bf16[32,16,128]{2,1,0:T(8,128)(2,1)S(1)} all-to-all(bf16[32,16,128]{2,1,0:T(8,128)(2,1)S(1)} %broadcast_in_dim.20), channel_id=1, replica_groups=mesh['row'=16,'col'=32] {'col'}, dimensions={0} | all-to-all | bytes 262144 | tf_op jit(solution)/shard_map/all_to_all | solution.py:13
  149.0 0.7 final_sums.1
  (20 shorter events, 0.2 us)
Async XLA Ops:
  22.6 16.2 %collective-permute-start.2 = (bf16[8,128,128]{2,1,0:T(8,128)(2,1)S(1)}, bf16[8,128,128]{2,1,0:T(8,128)(2,1)S(1)}, u32[]{:S(2)}, u32[]{:S(2)}) collective-permute-start(bf16[8,128,128]{2,1,0:T(8,128)(2,1)S(1)} %bitcast.47), channel_id=1, source_target_pairs={{0,2},{1,3},{2,0},{3,1},{4,6},{5,7},{6,4},{7,5},{8,10},{9,11},{10,... | collective-permute-start | bytes 786440 | tf_op jit(solution)/shard_map/ppermute | solution.py:96
  27.2 21.4 %all-to-all-start = ((bf16[8,4,32,128]{3,2,1,0:T(8,128)(2,1)}), bf16[8,4,32,128]{3,2,1,0:T(8,128)(2,1)S(1)}, u32[]{:S(2)}, u32[]{:S(2)}) async-start(bf16[8,4,32,128]{3,2,1,0:T(8,128)(2,1)} %broadcast_in_dim.15), calls=%async_computation | async-start | bytes 524288 | tf_op jit(solution)/shard_map/all_to_all | solution.py:307
  34.0 10.6 %collective-permute-start.3 = (bf16[8,128,128]{2,1,0:T(8,128)(2,1)S(1)}, bf16[8,128,128]{2,1,0:T(8,128)(2,1)S(1)}, u32[]{:S(2)}, u32[]{:S(2)}) collective-permute-start(bf16[8,128,128]{2,1,0:T(8,128)(2,1)S(1)} %bitcast.48), channel_id=1, source_target_pairs={{0,1},{1,0},{2,3},{3,2},{4,5},{5,4},{6,7},{7,6},{8,9},{9,8},{10,11... | collective-permute-start | bytes 786440 | tf_op jit(solution)/shard_map/ppermute | solution.py:96
  38.8 5.8 %collective-permute-start.4 = (bf16[8,128,128]{2,1,0:T(8,128)(2,1)S(1)}, bf16[8,128,128]{2,1,0:T(8,128)(2,1)S(1)}, u32[]{:S(2)}, u32[]{:S(2)}) collective-permute-start(bf16[8,128,128]{2,1,0:T(8,128)(2,1)S(1)} %collective-permute-done.2.x_ref), channel_id=1, source_target_pairs={{0,1},{1,0},{2,3},{3,2},{4,5},{5,4},{6,7},{7,6},{8,9},{9,8},{10,11... | collective-permute-start | bytes 786440 | tf_op jit(solution)/shard_map/ppermute | solution.py:96
  48.6 30.1 %copy-start = (bf16[1,4,32,128]{3,2,1,0:T(8,128)(2,1)S(1)}, bf16[1,4,32,128]{3,2,1,0:T(8,128)(2,1)}, u32[]{:S(2)}) copy-start(bf16[1,4,32,128]{3,2,1,0:T(8,128)(2,1)} %param.7) | copy-start | bytes 98308
  48.6 33.2 %all-to-all-start.3 = ((bf16[16,4,32,128]{3,2,1,0:T(8,128)(2,1)}), bf16[16,4,32,128]{3,2,1,0:T(8,128)(2,1)S(1)}, u32[]{:S(2)}, u32[]{:S(2)}) async-start(bf16[16,4,32,128]{3,2,1,0:T(8,128)(2,1)} %bitcast.10), calls=%async_computation.3 | async-start | bytes 1048576 | tf_op jit(solution)/shard_map/all_to_all | solution.py:24
  57.9 15.6 %collective-permute-start = (bf16[8,4,32,128]{3,2,1,0:T(8,128)(2,1)S(1)}, bf16[8,4,32,128]{3,2,1,0:T(8,128)(2,1)S(1)}, u32[]{:S(2)}, u32[]{:S(2)}) collective-permute-start(bf16[8,4,32,128]{3,2,1,0:T(8,128)(2,1)S(1)} %all-to-all-done), channel_id=1, source_target_pairs={{0,256},{32,288},{64,320},{96,352},{128,384},{160,416},{192,448},{... | collective-permute-start | bytes 786440 | tf_op jit(solution)/shard_map/ppermute | solution.py:96
  73.5 11.8 %copy-start.1 = (bf16[4,128,128]{2,1,0:T(8,128)(2,1)S(1)}, bf16[4,128,128]{2,1,0:T(8,128)(2,1)}, u32[]{:S(2)}) copy-start(bf16[4,128,128]{2,1,0:T(8,128)(2,1)} %param.13) | copy-start | bytes 393220
  75.7 10.1 %copy-start.2 = (f32[128]{0:T(128)S(1)}, f32[128]{0:T(128)}, u32[]{:S(2)}) copy-start(f32[128]{0:T(128)} %param.11) | copy-start | bytes 1540
  75.7 10.1 %copy-start.3 = (f32[128]{0:T(128)S(1)}, f32[128]{0:T(128)}, u32[]{:S(2)}) copy-start(f32[128]{0:T(128)} %param.12) | copy-start | bytes 1540
  75.7 4.5 %collective-permute-start.1 = (bf16[16,128,128]{2,1,0:T(8,128)(2,1)S(1)}, bf16[16,128,128]{2,1,0:T(8,128)(2,1)S(1)}, u32[]{:S(2)}, u32[]{:S(2)}) collective-permute-start(bf16[16,128,128]{2,1,0:T(8,128)(2,1)S(1)} %get-tuple-element.14), channel_id=1, source_target_pairs={{0,1},{1,0},{2,3},{3,2},{4,5},{5,4},{6,7},{7,6},{8,9},{9,8},{10,11... | collective-permute-start | bytes 1572872 | tf_op jit(solution)/shard_map/ppermute | solution.py:96
  81.7 19.7 %all-to-all-start.1 = ((bf16[16,128,128]{2,1,0:T(8,128)(2,1)}), bf16[16,128,128]{2,1,0:T(8,128)(2,1)S(1)}, u32[]{:S(2)}, u32[]{:S(2)}) async-start(bf16[16,128,128]{2,1,0:T(8,128)(2,1)} %pair_sum.1), calls=%async_computation.1 | async-start | bytes 1048576 | tf_op jit(solution)/shard_map/all_to_all | solution.py:325

commit v13 on v12

--- a/solution.py
+++ b/solution.py
@@ -6,11 +6,6 @@
 from jax.experimental import pallas as pl
 from jax.experimental.pallas import tpu as pltpu
 from jax.sharding import PartitionSpec as P
-
-
-def sent_to_all(x, axis):
-    devices = lax.axis_size(axis)
-    return lax.all_to_all(jnp.broadcast_to(x[None], (devices, *x.shape)), axis, 0, 0, tiled=True)
 
 
 def split_up(x, dim, devices):
@@ -75,18 +70,33 @@
 
 
 def summed_over_all(weight_part, norm_part, pair_grad):
-    cols = lax.axis_size("col")
+    half, cols = lax.axis_size("row") // 2, lax.axis_size("col")
+    members = 2 * cols
+    lines_y = [[x * half + y for y in range(half)] for x in range(2)]
+    planes = [
+        [(x * half + y) * cols + c for x in range(2) for c in range(cols)] for y in range(half)
+    ]
     shape = weight_part.shape
     width = shape[-1]
-    chunks = weight_part.reshape(cols, -1, width).astype(jnp.bfloat16)
+    chunks = weight_part.reshape(members, -1, width).astype(jnp.bfloat16)
     rows = chunks.shape[1]
     extra = split_in_two(norm_part).astype(jnp.bfloat16)
-    packed = jnp.concatenate([chunks, jnp.broadcast_to(extra[None], (cols, 8, width))], axis=1)
-    arrived = lax.all_to_all(packed, "col", 0, 0, tiled=True)
+    packed = jnp.concatenate([chunks, jnp.broadcast_to(extra[None], (members, 8, width))], axis=1)
+    arrived = lax.all_to_all(
+        packed, ("row", "col"), 0, 0, tiled=True, axis_index_groups=planes
+    )
     part = arrived.astype(jnp.float32).sum(axis=0)
-    whole = sent_to_all(with_split_norm(part, rows), "row").astype(jnp.float32).sum(axis=0)
+    packed = with_split_norm(part, rows)
+    arrived = lax.all_to_all(
+        jnp.broadcast_to(packed[None], (half, *packed.shape)),
+        "row", 0, 0, tiled=True, axis_index_groups=lines_y,
+    )
+    whole = arrived.astype(jnp.float32).sum(axis=0)
     chunk, sums = lax.optimization_barrier((whole[:rows].astype(jnp.bfloat16), whole[rows:]))
-    weight_grad = sent_to_all(chunk, "col").reshape(-1, width)
+    weight_grad = lax.all_to_all(
+        jnp.broadcast_to(chunk[None], (members, *chunk.shape)),
+        ("row", "col"), 0, 0, tiled=True, axis_index_groups=planes,
+    ).reshape(-1, width)
     weight_grad, norm_grad, pair_grad = final_sums(weight_grad, sums, pair_grad)
     return weight_grad.reshape(shape), norm_grad, pair_grad
 

time: 151 us -> 154 us (1.020)
  blocking collectives: 67.5 us -> 70.7 us
    all_to_all x3, blocking collectives: 46.3 us -> 49.6 us  [the longest x1 21 us: summed_over_all(): lax.all_to_all(packed, ('row', 'col'), 0, 0, tiled=True, axis_index_group...]
where the time goes in v13:
time: 154 us; the launch traced here: 153 us
  blocking collectives  70.7 us (46%)
  starting transfers between devices  37.3 us (24%)
  waiting for transfers between devices  27.5 us (18%)
  Pallas kernels  8.35 us (5%)
  local copies, waits for them, and re-layouts  6.63 us (4%)
    all_to_all x1, blocking collectives, all_steps(): lax.all_to_all(own, 'col', 0, 0, tiled=True, axis_index_groups=lines_z)  21.1 us
    all_to_all x1, blocking collectives, summed_over_all(): lax.all_to_all(packed, ('row', 'col'), 0, 0, tiled=True, axis_index_group...  21 us
    ppermute x5, starting transfers between devices, exchanged(): return lax.ppermute(x, axis, [(d, d ^ step) for d in range(devices)])  17.5 us
    all_to_all x1, blocking collectives, summed_over_all(): lax.all_to_all(jnp.broadcast_to(chunk[None], (members, *chunk.shape)), ('...  16.8 us
    all_to_all x1, waiting for transfers between devices, all_steps(): lax.all_to_all(chip_part, 'col', 0, 0, tiled=True, axis_index_groups=one_...  15.2 us
    ppermute x5, waiting for transfers between devices, exchanged(): return lax.ppermute(x, axis, [(d, d ^ step) for d in range(devices)])  12.3 us
    all_to_all x1, blocking collectives, summed_over_all(): lax.all_to_all(jnp.broadcast_to(packed[None], (half, *packed.shape)), 'ro...  11.9 us
    all_to_all x1, starting transfers between devices, sent_and_summed(): lax.all_to_all(parts, axis, split_axis=0, concat_axis=0, tiled=True)  9.33 us
  transfers between devices with their start and end apart: 8, of which 3 were waited for; matrix products, arithmetic and copies ran while one was open for 4% of the time, Pallas kernels for 5%

profile of v13, /device:TPU:1, one launch (start us, length us, event | category | flops | bytes accessed | tf_op | source)
XLA Modules:
  0.0 153.1 jit_solution(5769270123560977207)
XLA Ops:
  0.6 0.8 broadcast_in_dim.17
  1.4 21.1 %all_to_all.35 = bf16[8,4,32,128]{3,2,1,0:T(8,128)(2,1)S(1)} all-to-all(bf16[8,4,32,128]{3,2,1,0:T(8,128)(2,1)S(1)} %broadcast_in_dim.17), channel_id=1, replica_groups={{0,4,8,12,16,20,24,28},{1,5,9,13,17,21,25,29},{2,6,10,14,18,22,26,30},{..., dimensions={0} | all-to-all | bytes 524288 | tf_op jit(solution)/shard_map/all_to_all | solution.py:327
  22.6 3.1 %collective-permute-start.2 = (bf16[8,128,128]{2,1,0:T(8,128)(2,1)S(1)}, bf16[8,128,128]{2,1,0:T(8,128)(2,1)S(1)}, u32[]{:S(2)}, u32[]{:S(2)}) collective-permute-start(bf16[8,128,128]{2,1,0:T(8,128)(2,1)S(1)} %bitcast.47), channel_id=1, source_target_pairs={{0,2},{1,3},{2,0},{3,1},{4,6},{5,7},{6,4},{7,5},{8,10},{9,11},{10,... | collective-permute-start | bytes 786440 | tf_op jit(solution)/shard_map/ppermute | solution.py:106
  25.7 1.5 broadcast_in_dim.15
  27.2 6.8 %all-to-all-start = ((bf16[8,4,32,128]{3,2,1,0:T(8,128)(2,1)}), bf16[8,4,32,128]{3,2,1,0:T(8,128)(2,1)S(1)}, u32[]{:S(2)}, u32[]{:S(2)}) async-start(bf16[8,4,32,128]{3,2,1,0:T(8,128)(2,1)} %broadcast_in_dim.15), calls=%async_computation | async-start | bytes 524288 | tf_op jit(solution)/shard_map/all_to_all | solution.py:317
  34.0 4.8 %collective-permute-start.3 = (bf16[8,128,128]{2,1,0:T(8,128)(2,1)S(1)}, bf16[8,128,128]{2,1,0:T(8,128)(2,1)S(1)}, u32[]{:S(2)}, u32[]{:S(2)}) collective-permute-start(bf16[8,128,128]{2,1,0:T(8,128)(2,1)S(1)} %bitcast.48), channel_id=1, source_target_pairs={{0,1},{1,0},{2,3},{3,2},{4,5},{5,4},{6,7},{7,6},{8,9},{9,8},{10,11... | collective-permute-start | bytes 786440 | tf_op jit(solution)/shard_map/ppermute | solution.py:106
  38.8 0.0 collective-permute-done.2.x_ref
  38.8 1.9 %collective-permute-start.4 = (bf16[8,128,128]{2,1,0:T(8,128)(2,1)S(1)}, bf16[8,128,128]{2,1,0:T(8,128)(2,1)S(1)}, u32[]{:S(2)}, u32[]{:S(2)}) collective-permute-start(bf16[8,128,128]{2,1,0:T(8,128)(2,1)S(1)} %collective-permute-done.2.x_ref), channel_id=1, source_target_pairs={{0,1},{1,0},{2,3},{3,2},{4,5},{5,4},{6,7},{7,6},{8,9},{9,8},{10,11... | collective-permute-start | bytes 786440 | tf_op jit(solution)/shard_map/ppermute | solution.py:106
  40.8 3.8 %copy.17 = bf16[128,64,128]{0,1,2:T(8,128)(2,1)S(1)} copy(bf16[128,64,128]{2,1,0:T(8,128)(2,1)} %bitcast.53) | data formatting | bytes 4194304 | tf_op jit(solution)/shard_map/reshape | solution.py:323
  44.6 0.0 collective-permute-done.3.core_ref
  44.6 0.0 collective-permute-done.4.both_ref
  44.6 3.9 %right_parts.1 = bf16[2048,128]{1,0:T(8,128)(2,1)} custom-call(bf16[8,128,128]{2,1,0:T(8,128)(2,1)S(1)} %bitcast.49, bf16[8,128,128]{2,1,0:T(8,128)(2,1)S(1)} %collective-permute-done.2.x_ref, bf16[8,128,128]{2,1,0:T(8,128)(2,1)S(1)} %collective-permute-done.3.core_ref, bf16[8,128,128]{2,1,0:T(8,128)(2,1)S(1)} %collective-permute-done.4.both_ref, ...), custom_call_target="tpu_custom_call" | custom-call | tf_op jit(solution)/shard_map/right_parts/pallas_call | solution.py:227
  48.6 0.0 all-to-all-done
  48.6 9.3 %all-to-all-start.3 = ((bf16[16,4,32,128]{3,2,1,0:T(8,128)(2,1)}), bf16[16,4,32,128]{3,2,1,0:T(8,128)(2,1)S(1)}, u32[]{:S(2)}, u32[]{:S(2)}) async-start(bf16[16,4,32,128]{3,2,1,0:T(8,128)(2,1)} %bitcast.10), calls=%async_computation.3 | async-start | bytes 1048576 | tf_op jit(solution)/shard_map/all_to_all | solution.py:19
  57.9 4.8 %collective-permute-start = (bf16[8,4,32,128]{3,2,1,0:T(8,128)(2,1)S(1)}, bf16[8,4,32,128]{3,2,1,0:T(8,128)(2,1)S(1)}, u32[]{:S(2)}, u32[]{:S(2)}) collective-permute-start(bf16[8,4,32,128]{3,2,1,0:T(8,128)(2,1)S(1)} %all-to-all-done), channel_id=1, source_target_pairs={{0,256},{32,288},{64,320},{96,352},{128,384},{160,416},{192,448},{... | collective-permute-start | bytes 786440 | tf_op jit(solution)/shard_map/ppermute | solution.py:106
  62.7 10.9 %collective-permute-done = bf16[8,4,32,128]{3,2,1,0:T(8,128)(2,1)S(1)} collective-permute-done((bf16[8,4,32,128]{3,2,1,0:T(8,128)(2,1)S(1)}, bf16[8,4,32,128]{3,2,1,0:T(8,128)(2,1)S(1)}, u32[]{:S(2)}, u32[]{:S(2)}) %collective-permute-start) | collective-permute-done | bytes 262176 | tf_op jit(solution)/shard_map/ppermute | solution.py:106
  73.5 2.2 %left_parts.1 = (bf16[16,128,128]{2,1,0:T(8,128)(2,1)S(1)}, bf16[16,128,128]{2,1,0:T(8,128)(2,1)S(1)}) custom-call(bf16[1024,128]{1,0:T(8,128)(2,1)S(1)} %bitcast.50, bf16[1024,128]{1,0:T(8,128)(2,1)S(1)} %bitcast.52, bf16[128,64,128]{2,1,0:T(8,128)(2,1)S(1)} %bitcast.46), custom_call_target="tpu_custom_call" | custom-call | tf_op jit(solution)/shard_map/left_parts/pallas_call | solution.py:170
  75.7 0.0 copy-start.2
  75.7 0.0 copy-start.3
  75.7 2.9 %collective-permute-start.1 = (bf16[16,128,128]{2,1,0:T(8,128)(2,1)S(1)}, bf16[16,128,128]{2,1,0:T(8,128)(2,1)S(1)}, u32[]{:S(2)}, u32[]{:S(2)}) collective-permute-start(bf16[16,128,128]{2,1,0:T(8,128)(2,1)S(1)} %get-tuple-element.14), channel_id=1, source_target_pairs={{0,1},{1,0},{2,3},{3,2},{4,5},{5,4},{6,7},{7,6},{8,9},{9,8},{10,11... | collective-permute-start | bytes 1572872 | tf_op jit(solution)/shard_map/ppermute | solution.py:106
  78.7 0.0 copy-done
  78.7 0.1 convert_reduce_fusion.4
  78.8 1.4 collective-permute-done.1.came_hbm
  80.2 1.5 %pair_sum.1 = bf16[16,128,128]{2,1,0:T(8,128)(2,1)} custom-call(bf16[16,128,128]{2,1,0:T(8,128)(2,1)S(1)} %get-tuple-element.13.kept_ref, bf16[16,128,128]{2,1,0:T(8,128)(2,1)S(1)} %collective-permute-done.1.came_hbm), custom_call_target="tpu_custom_call" | custom-call | tf_op jit(solution)/shard_map/pair_sum/pallas_call | solution.py:268
  81.7 0.0 all-to-all-done.3
  81.7 3.6 %all-to-all-start.1 = ((bf16[16,128,128]{2,1,0:T(8,128)(2,1)}), bf16[16,128,128]{2,1,0:T(8,128)(2,1)S(1)}, u32[]{:S(2)}, u32[]{:S(2)}) async-start(bf16[16,128,128]{2,1,0:T(8,128)(2,1)} %pair_sum.1), calls=%async_computation.1 | async-start | bytes 1048576 | tf_op jit(solution)/shard_map/all_to_all | solution.py:335
  85.4 0.0 copy-done.1
  85.4 0.1 copy.18
  85.5 0.1 div.25
  85.6 0.2 multiply_reduce_fusion.2
  85.8 0.1 rsqrt.13
  85.8 0.0 copy-done.2
  85.8 0.0 copy-done.3
  85.8 0.1 add_convert_fusion
  86.0 0.2 fusion.19
  86.2 0.1 convert_reduce_fusion
  86.2 15.2 %all-to-all-done.1 = bf16[16,128,128]{2,1,0:T(8,128)(2,1)S(1)} async-done(((bf16[16,128,128]{2,1,0:T(8,128)(2,1)}), bf16[16,128,128]{2,1,0:T(8,128)(2,1)S(1)}, u32[]{:S(2)}, u32[]{:S(2)}) %all-to-all-start.1) | async-done | bytes 524320 | tf_op jit(solution)/shard_map/all_to_all | solution.py:335
  101.4 0.1 convert_reduce_fusion.1
  101.5 0.1 fusion.11
  101.6 0.1 copy.23
  101.8 0.3 multiply_reduce_fusion
  102.0 0.2 convolution_bitcast_fusion
  102.3 0.1 subtract_multiply_fusion.pair_ref
  102.5 21.0 %all_to_all.36 = bf16[64,16,128]{2,1,0:T(8,128)(2,1)S(1)} all-to-all(bf16[64,16,128]{2,1,0:T(8,128)(2,1)S(1)} %pad_maximum_fusion), channel_id=1, replica_groups={{0,1,2,3,4,5,6,7,8,9,10,11,12,13,14,15,16,17,18,19,20,21,22,23,24,25,26..., dimensions={0} | all-to-all | bytes 524288 | tf_op jit(solution)/shard_map/all_to_all | solution.py:85
  123.5 0.1 convert_reduce_fusion.2
  123.6 11.9 %all_to_all.37 = bf16[8,16,128]{2,1,0:T(8,128)(2,1)S(1)} all-to-all(bf16[8,16,128]{2,1,0:T(8,128)(2,1)S(1)} %broadcast_in_dim.19), channel_id=1, replica_groups={{0,32,64,96,128,160,192,224},{256,288,320,352,384,416,448,480},{1,33,65..., dimensions={0} | all-to-all | bytes 65536 | tf_op jit(solution)/shard_map/all_to_all | solution.py:90
  135.6 16.8 %all_to_all.38 = bf16[64,8,128]{2,1,0:T(8,128)(2,1)S(1)} all-to-all(bf16[64,8,128]{2,1,0:T(8,128)(2,1)S(1)} %broadcast_in_dim.20), channel_id=1, replica_groups={{0,1,2,3,4,5,6,7,8,9,10,11,12,13,14,15,16,17,18,19,20,21,22,23,24,25,26..., dimensions={0} | all-to-all | bytes 262144 | tf_op jit(solution)/shard_map/all_to_all | solution.py:96
  152.3 0.7 final_sums.1
  (20 shorter events, 0.2 us)
Async XLA Ops:
  22.6 16.2 %collective-permute-start.2 = (bf16[8,128,128]{2,1,0:T(8,128)(2,1)S(1)}, bf16[8,128,128]{2,1,0:T(8,128)(2,1)S(1)}, u32[]{:S(2)}, u32[]{:S(2)}) collective-permute-start(bf16[8,128,128]{2,1,0:T(8,128)(2,1)S(1)} %bitcast.47), channel_id=1, source_target_pairs={{0,2},{1,3},{2,0},{3,1},{4,6},{5,7},{6,4},{7,5},{8,10},{9,11},{10,... | collective-permute-start | bytes 786440 | tf_op jit(solution)/shard_map/ppermute | solution.py:106
  27.2 21.4 %all-to-all-start = ((bf16[8,4,32,128]{3,2,1,0:T(8,128)(2,1)}), bf16[8,4,32,128]{3,2,1,0:T(8,128)(2,1)S(1)}, u32[]{:S(2)}, u32[]{:S(2)}) async-start(bf16[8,4,32,128]{3,2,1,0:T(8,128)(2,1)} %broadcast_in_dim.15), calls=%async_computation | async-start | bytes 524288 | tf_op jit(solution)/shard_map/all_to_all | solution.py:317
  34.0 10.6 %collective-permute-start.3 = (bf16[8,128,128]{2,1,0:T(8,128)(2,1)S(1)}, bf16[8,128,128]{2,1,0:T(8,128)(2,1)S(1)}, u32[]{:S(2)}, u32[]{:S(2)}) collective-permute-start(bf16[8,128,128]{2,1,0:T(8,128)(2,1)S(1)} %bitcast.48), channel_id=1, source_target_pairs={{0,1},{1,0},{2,3},{3,2},{4,5},{5,4},{6,7},{7,6},{8,9},{9,8},{10,11... | collective-permute-start | bytes 786440 | tf_op jit(solution)/shard_map/ppermute | solution.py:106
  38.8 5.8 %collective-permute-start.4 = (bf16[8,128,128]{2,1,0:T(8,128)(2,1)S(1)}, bf16[8,128,128]{2,1,0:T(8,128)(2,1)S(1)}, u32[]{:S(2)}, u32[]{:S(2)}) collective-permute-start(bf16[8,128,128]{2,1,0:T(8,128)(2,1)S(1)} %collective-permute-done.2.x_ref), channel_id=1, source_target_pairs={{0,1},{1,0},{2,3},{3,2},{4,5},{5,4},{6,7},{7,6},{8,9},{9,8},{10,11... | collective-permute-start | bytes 786440 | tf_op jit(solution)/shard_map/ppermute | solution.py:106
  48.6 30.1 %copy-start = (bf16[1,4,32,128]{3,2,1,0:T(8,128)(2,1)S(1)}, bf16[1,4,32,128]{3,2,1,0:T(8,128)(2,1)}, u32[]{:S(2)}) copy-start(bf16[1,4,32,128]{3,2,1,0:T(8,128)(2,1)} %param.7) | copy-start | bytes 98308
  48.6 33.2 %all-to-all-start.3 = ((bf16[16,4,32,128]{3,2,1,0:T(8,128)(2,1)}), bf16[16,4,32,128]{3,2,1,0:T(8,128)(2,1)S(1)}, u32[]{:S(2)}, u32[]{:S(2)}) async-start(bf16[16,4,32,128]{3,2,1,0:T(8,128)(2,1)} %bitcast.10), calls=%async_computation.3 | async-start | bytes 1048576 | tf_op jit(solution)/shard_map/all_to_all | solution.py:19
  57.9 15.6 %collective-permute-start = (bf16[8,4,32,128]{3,2,1,0:T(8,128)(2,1)S(1)}, bf16[8,4,32,128]{3,2,1,0:T(8,128)(2,1)S(1)}, u32[]{:S(2)}, u32[]{:S(2)}) collective-permute-start(bf16[8,4,32,128]{3,2,1,0:T(8,128)(2,1)S(1)} %all-to-all-done), channel_id=1, source_target_pairs={{0,256},{32,288},{64,320},{96,352},{128,384},{160,416},{192,448},{... | collective-permute-start | bytes 786440 | tf_op jit(solution)/shard_map/ppermute | solution.py:106
  73.5 11.8 %copy-start.1 = (bf16[4,128,128]{2,1,0:T(8,128)(2,1)S(1)}, bf16[4,128,128]{2,1,0:T(8,128)(2,1)}, u32[]{:S(2)}) copy-start(bf16[4,128,128]{2,1,0:T(8,128)(2,1)} %param.13) | copy-start | bytes 393220
  75.7 10.1 %copy-start.2 = (f32[128]{0:T(128)S(1)}, f32[128]{0:T(128)}, u32[]{:S(2)}) copy-start(f32[128]{0:T(128)} %param.11) | copy-start | bytes 1540
  75.7 10.1 %copy-start.3 = (f32[128]{0:T(128)S(1)}, f32[128]{0:T(128)}, u32[]{:S(2)}) copy-start(f32[128]{0:T(128)} %param.12) | copy-start | bytes 1540
  75.7 4.5 %collective-permute-start.1 = (bf16[16,128,128]{2,1,0:T(8,128)(2,1)S(1)}, bf16[16,128,128]{2,1,0:T(8,128)(2,1)S(1)}, u32[]{:S(2)}, u32[]{:S(2)}) collective-permute-start(bf16[16,128,128]{2,1,0:T(8,128)(2,1)S(1)} %get-tuple-element.14), channel_id=1, source_target_pairs={{0,1},{1,0},{2,3},{3,2},{4,5},{5,4},{6,7},{7,6},{8,9},{9,8},{10,11... | collective-permute-start | bytes 1572872 | tf_op jit(solution)/shard_map/ppermute | solution.py:106
  81.7 19.7 %all-to-all-start.1 = ((bf16[16,128,128]{2,1,0:T(8,128)(2,1)}), bf16[16,128,128]{2,1,0:T(8,128)(2,1)S(1)}, u32[]{:S(2)}, u32[]{:S(2)}) async-start(bf16[16,128,128]{2,1,0:T(8,128)(2,1)} %pair_sum.1), calls=%async_computation.1 | async-start | bytes 1048576 | tf_op jit(solution)/shard_map/all_to_all | solution.py:335
